TPU v7x, 32 devices: a whole 2x2x4 slice. The times are simulated.
32 devices in a mesh: slab: 2 (over x), row: 8 (over z, y), col: 2 (over core).
Axes of the slice: x: 2, y: 2, z: 4, core: 2. Of those that a mesh axis runs over, the one named last changes fastest.
Arguments:
- image: float32 [1024, 4096], P(('slab', 'row'), 'col'), parts along dimension 0, may hold values from -6 to 6
Outputs:
- dog_fine: bfloat16 [4, 1024, 4096], P(None, ('slab', 'row'), 'col'), parts along dimension 1
- hessian_fine: bfloat16 [2, 1024, 4096], P(None, ('slab', 'row'), 'col'), parts along dimension 1
- dog_coarse: bfloat16 [4, 512, 2048], P(None, ('slab', 'row', 'col')), parts along dimension 1
- hessian_coarse: bfloat16 [2, 512, 2048], P(None, ('slab', 'row', 'col')), parts along dimension 1
There are 2 independent parts, one for each index of `slab`. A program takes and returns all parts, laid end to end along the dimension named above; each array names one. Nothing has to cross between parts.
All inputs are finite; a program needn't handle non-finite values.
Results may differ from a plain program's by a relative error of at most 0.0013.
Values may be sent and summed in bfloat16 or wider, within the bound.
No kernel may reach another device: no remote copies, remote signals or barrier semaphores. Data moves between devices by JAX's collectives and lax.ppermute only.
A program may use at most 64 MiB of HBM per device.

v0:
```python
import jax
import jax.numpy as jnp
from jax import lax
from jax.sharding import PartitionSpec as P

SIGMAS = [1.6 * 2.0 ** (k / 4.0) for k in range(5)]


def with_halo(x, sides, width):
    for axis, dim in sides:
        devices, length = (lax.axis_size(axis), x.shape[dim])
        up = [(i, (i + 1) % devices) for i in range(devices - 1)]
        down = [(j, i) for i, j in up]
        last = lax.slice_in_dim(x, length - width, length, axis=dim)
        first = lax.slice_in_dim(x, 0, width, axis=dim)
        before = lax.ppermute(last, axis, up)
        after = lax.ppermute(first, axis, down)
        x = jnp.concatenate([before, x, after], axis=dim)
    return x


def band(sigma, count_out, count_in, offset):
    outer = jnp.arange(count_out)[:, None]
    inner = jnp.arange(count_in)[None, :]
    diff = inner - outer + offset
    spread = jnp.arange(25).astype(jnp.float32) - 12.0
    total = jnp.sum(jnp.exp(-spread * spread / (2.0 * sigma * sigma)))
    centred = diff.astype(jnp.float32) - 12.0
    weights = jnp.exp(-centred * centred / (2.0 * sigma * sigma)) / total
    return jnp.where((diff >= 0) & (diff <= 24), weights, 0.0)


def vertical(field, sigma):
    count = field.shape[0]
    matrix = band(sigma, count - 24, count, 0)
    return jnp.dot(matrix, field, precision=lax.Precision.HIGHEST)


def horizontal(field, sigma):
    length = field.shape[1]
    out_len = length - 24
    blocks = -(-out_len // 128)
    padded = jnp.pad(field, ((0, 0), (0, (blocks + 1) * 128 - length)))
    tiles = padded.reshape(field.shape[0], blocks + 1, 128)
    main = band(sigma, 128, 128, 0)
    carry = band(sigma, 128, 128, 128)
    result = jnp.einsum("rbi,oi->rbo", tiles[:, :blocks], main, precision=lax.Precision.HIGHEST)
    result = result + jnp.einsum(
        "rbi,oi->rbo", tiles[:, 1:], carry, precision=lax.Precision.HIGHEST
    )
    return result.reshape(field.shape[0], blocks * 128)[:, :out_len]


def hessian_valid(padded):
    centre = padded[:, 1:-1, 1:-1]
    dxx = padded[:, 1:-1, 2:] + padded[:, 1:-1, :-2] - 2.0 * centre
    dyy = padded[:, 2:, 1:-1] + padded[:, :-2, 1:-1] - 2.0 * centre
    dxy = (padded[:, 2:, 2:] - padded[:, 2:, :-2] - padded[:, :-2, 2:] + padded[:, :-2, :-2]) / 4.0
    return dxx * dyy - dxy * dxy


def scale_space(extended, spare, row_start, col_start, height, width, dog_gain, hess_gain):
    rows = extended.shape[0] - 24 - 2 * spare
    cols = extended.shape[1] - 24 - 2 * spare
    levels = [horizontal(vertical(extended, s), s) for s in SIGMAS]
    diffs = [levels[k + 1] - levels[k] for k in range(4)]
    dogs = jnp.stack(
        [
            (dog_gain * d[spare : spare + rows, spare : spare + cols]).astype(jnp.bfloat16)
            for d in diffs
        ]
    )
    middle = jnp.stack([diffs[1], diffs[2]])
    row_pos = row_start - 1 + jnp.arange(rows + 2)
    col_pos = col_start - 1 + jnp.arange(cols + 2)
    inside = ((row_pos >= 0) & (row_pos < height))[:, None] & ((col_pos >= 0) & (col_pos < width))[
        None, :
    ]
    padded = middle * inside.astype(jnp.float32)[None]
    hess = (hess_gain * hessian_valid(padded)).astype(jnp.bfloat16)
    return (dogs, hess, levels[4][spare : spare + rows, spare : spare + cols])


def local(image):
    tile_rows, tile_cols = image.shape
    spare = 1
    reach = 12 + spare
    height = tile_rows * lax.axis_size("row")
    width = tile_cols * lax.axis_size("col")
    extended = with_halo(image, (("row", 0), ("col", 1)), reach)
    dog_fine, hessian_fine, top_level = scale_space(
        extended,
        spare,
        lax.axis_index("row") * tile_rows,
        lax.axis_index("col") * tile_cols,
        height,
        width,
        20.0,
        5000.0,
    )
    coarse_base = top_level[0::2, 0::2]
    grown = with_halo(coarse_base, (("row", 0), ("col", 1)), reach)
    dog_tile, hess_tile, unused = scale_space(
        grown,
        spare,
        lax.axis_index("row") * coarse_base.shape[0],
        lax.axis_index("col") * coarse_base.shape[1],
        height // 2,
        width // 2,
        80.0,
        200000.0,
    )
    stacked = jnp.concatenate([dog_tile, hess_tile], axis=0)
    relaid = lax.all_to_all(stacked, "col", split_axis=1, concat_axis=2, tiled=True)
    dog_coarse = relaid[:4]
    hessian_coarse = relaid[4:]
    return (dog_fine, hessian_fine, dog_coarse, hessian_coarse)


def solution(mesh):
    return jax.shard_map(
        local,
        mesh=mesh,
        in_specs=(P(("slab", "row"), "col"),),
        out_specs=(
            P(None, ("slab", "row"), "col"),
            P(None, ("slab", "row"), "col"),
            P(None, ("slab", "row", "col"), None),
            P(None, ("slab", "row", "col"), None),
        ),
        check_vma=False,
    )
```

profile of v0, /device:TPU:11, one launch (start us, length us, event | category | flops | bytes accessed | tf_op | source)
XLA Modules:
  0.0 97.5 jit_solution(10586258024756835656)
XLA Ops:
  1.7 3.0 %collective-permute-start.1 = (f32[13,2048]{1,0:T(8,128)S(1)}, f32[13,2048]{1,0:T(8,128)S(1)}, u32[]{:S(2)}, u32[]{:S(2)}) collective-permute-start(f32[13,2048]{1,0:T(8,128)S(1)} %get-tuple-element.21), channel_id=1, source_target_pairs={{2,0},{4,2},{6,4},{8,6},{10,8},{12,10},{14,12},{3,1},{5,3},{7,5},{... | collective-permute-start | bytes 319496 | tf_op jit(solution)/shard_map/ppermute | solution.py:17
  4.7 2.2 %collective-permute-start = (f32[13,2048]{1,0:T(8,128)S(1)}, f32[13,2048]{1,0:T(8,128)S(1)}, u32[]{:S(2)}, u32[]{:S(2)}) collective-permute-start(f32[13,2048]{1,0:T(8,128)S(1)} %get-tuple-element.20), channel_id=1, source_target_pairs={{0,2},{2,4},{4,6},{6,8},{8,10},{10,12},{12,14},{1,3},{3,5},{5,7},{... | collective-permute-start | bytes 319496 | tf_op jit(solution)/shard_map/ppermute | solution.py:16
  8.0 3.8 %collective-permute-done = f32[13,2048]{1,0:T(8,128)S(1)} collective-permute-done((f32[13,2048]{1,0:T(8,128)S(1)}, f32[13,2048]{1,0:T(8,128)S(1)}, u32[]{:S(2)}, u32[]{:S(2)}) %collective-permute-start) | collective-permute-done | bytes 106528 | tf_op jit(solution)/shard_map/ppermute | solution.py:16
  11.9 1.3 %collective-permute-start.2 = (f32[90,13]{1,0:T(8,128)S(1)}, f32[90,13]{1,0:T(8,128)S(1)}, u32[]{:S(2)}, u32[]{:S(2)}) collective-permute-start(f32[90,13]{1,0:T(8,128)S(1)} %get-tuple-element.15), channel_id=1, source_target_pairs={{0,1},{2,3},{4,5},{6,7},{8,9},{10,11},{12,13},{14,15},{16,17},{18,... | collective-permute-start | bytes 14048 | tf_op jit(solution)/shard_map/ppermute | solution.py:16
  13.2 3.6 %collective-permute-start.3 = (f32[90,13]{1,0:T(8,128)S(1)}, f32[90,13]{1,0:T(8,128)S(1)}, u32[]{:S(2)}, u32[]{:S(2)}) collective-permute-start(f32[90,13]{1,0:T(8,128)S(1)} %get-tuple-element.14), channel_id=1, source_target_pairs={{1,0},{3,2},{5,4},{7,6},{9,8},{11,10},{13,12},{15,14},{17,16},{19,... | collective-permute-start | bytes 14048 | tf_op jit(solution)/shard_map/ppermute | solution.py:17
  20.4 1.4 %fusion.118 = f32[66,2074]{1,0:T(8,128)S(1)} fusion(f32[90,2074]{1,0:T(8,128)S(1)} %concatenate.16, f32[]{:T(128)} %exponential_reduce_fusion.4), kind=kOutput, calls=%fused_computation.175 | convolution fusion | flops 147900064 | bytes 1294180 | tf_op jit(solution)/shard_map/dot_general | solution.py:36
  22.1 1.8 %fusion.21 = f32[66,17,128]{2,0,1:T(8,128)S(1)} fusion(f32[66,17,128]{2,1,0:T(8,128)S(1)} %get-tuple-element.7, f32[]{:T(128)} %exponential_reduce_fusion.4), kind=kOutput, calls=%fused_computation.40 | convolution fusion | flops 220774400 | bytes 1148932 | tf_op jit(solution)/shard_map/rbi,oi->rbo/dot_general | solution.py:47
  23.9 1.8 %convolution_add_fusion.4 = f32[66,17,128]{2,0,1:T(8,128)S(1)} fusion(f32[66,17,128]{2,0,1:T(8,128)S(1)} %fusion.21, f32[66,17,128]{2,1,0:T(8,128)S(1)} %get-tuple-element.6, f32[]{:T(128)} %exponential_reduce_fusion.4), kind=kOutput, calls=%fused_computation.4 | convolution fusion | flops 220934400 | bytes 1723396 | tf_op jit(solution)/shard_map/rbi,oi->rbo/dot_general | solution.py:48
  26.9 1.4 %fusion.108 = f32[66,2074]{1,0:T(8,128)S(1)} fusion(f32[90,2074]{1,0:T(8,128)S(1)} %concatenate.16, f32[]{:T(128)} %exponential_reduce_fusion.2), kind=kOutput, calls=%fused_computation.165 | convolution fusion | flops 147900064 | bytes 1294180 | tf_op jit(solution)/shard_map/dot_general | solution.py:36
  28.5 1.8 %fusion.15 = f32[66,17,128]{2,0,1:T(8,128)S(1)} fusion(f32[66,17,128]{2,1,0:T(8,128)S(1)} %get-tuple-element.9, f32[]{:T(128)} %exponential_reduce_fusion.2), kind=kOutput, calls=%fused_computation.34 | convolution fusion | flops 220774400 | bytes 1148932 | tf_op jit(solution)/shard_map/rbi,oi->rbo/dot_general | solution.py:47
  30.4 1.8 %convolution_add_fusion.2 = f32[66,17,128]{2,0,1:T(8,128)S(1)} fusion(f32[66,17,128]{2,0,1:T(8,128)S(1)} %fusion.15, f32[66,17,128]{2,1,0:T(8,128)S(1)} %get-tuple-element.8, f32[]{:T(128)} %exponential_reduce_fusion.2), kind=kOutput, calls=%fused_computation.2 | convolution fusion | flops 220934400 | bytes 1723396 | tf_op jit(solution)/shard_map/rbi,oi->rbo/dot_general | solution.py:48
  33.3 1.4 %fusion.103 = f32[66,2074]{1,0:T(8,128)S(1)} fusion(f32[90,2074]{1,0:T(8,128)S(1)} %concatenate.16, f32[]{:T(128)} %exponential_reduce_fusion.1), kind=kOutput, calls=%fused_computation.160 | convolution fusion | flops 147900064 | bytes 1294180 | tf_op jit(solution)/shard_map/dot_general | solution.py:36
  35.0 1.8 %fusion.12 = f32[66,17,128]{2,0,1:T(8,128)S(1)} fusion(f32[66,17,128]{2,1,0:T(8,128)S(1)} %get-tuple-element.13, f32[]{:T(128)} %exponential_reduce_fusion.1), kind=kOutput, calls=%fused_computation.31 | convolution fusion | flops 220774400 | bytes 1148932 | tf_op jit(solution)/shard_map/rbi,oi->rbo/dot_general | solution.py:47
  36.8 1.8 %convolution_add_fusion.1 = f32[66,17,128]{2,0,1:T(8,128)S(1)} fusion(f32[66,17,128]{2,0,1:T(8,128)S(1)} %fusion.12, f32[66,17,128]{2,1,0:T(8,128)S(1)} %get-tuple-element.12, f32[]{:T(128)} %exponential_reduce_fusion.1), kind=kOutput, calls=%fused_computation.1 | convolution fusion | flops 220934400 | bytes 1723396 | tf_op jit(solution)/shard_map/rbi,oi->rbo/dot_general | solution.py:48
  39.7 1.3 %fusion.98 = f32[66,2074]{1,0:T(8,128)S(1)} fusion(f32[90,2074]{1,0:T(8,128)S(1)} %concatenate.16, f32[]{:T(128)} %exponential_reduce_fusion), kind=kOutput, calls=%fused_computation.155 | convolution fusion | flops 147900064 | bytes 1294180 | tf_op jit(solution)/shard_map/dot_general | solution.py:36
  41.3 1.9 %fusion.9 = f32[66,17,128]{2,0,1:T(8,128)S(1)} fusion(f32[66,17,128]{2,1,0:T(8,128)S(1)} %get-tuple-element.11, f32[]{:T(128)} %exponential_reduce_fusion), kind=kOutput, calls=%fused_computation.28 | convolution fusion | flops 220774400 | bytes 1148932 | tf_op jit(solution)/shard_map/rbi,oi->rbo/dot_general | solution.py:47
  43.2 1.7 %convolution_add_fusion = f32[66,17,128]{2,0,1:T(8,128)S(1)} fusion(f32[66,17,128]{2,0,1:T(8,128)S(1)} %fusion.9, f32[66,17,128]{2,1,0:T(8,128)S(1)} %get-tuple-element.10, f32[]{:T(128)} %exponential_reduce_fusion), kind=kOutput, calls=%fused_computation | convolution fusion | flops 220934400 | bytes 1723396 | tf_op jit(solution)/shard_map/rbi,oi->rbo/dot_general | solution.py:48
  45.3 1.4 %fusion.113 = f32[66,2074]{1,0:T(8,128)S(1)} fusion(f32[90,2074]{1,0:T(8,128)S(1)} %concatenate.16, f32[]{:T(128)} %exponential_reduce_fusion.3), kind=kOutput, calls=%fused_computation.170 | convolution fusion | flops 147900064 | bytes 1294180 | tf_op jit(solution)/shard_map/dot_general | solution.py:36
  47.0 1.8 %fusion.18 = f32[66,17,128]{2,0,1:T(8,128)S(1)} fusion(f32[66,17,128]{2,1,0:T(8,128)S(1)} %get-tuple-element.5, f32[]{:T(128)} %exponential_reduce_fusion.3), kind=kOutput, calls=%fused_computation.37 | convolution fusion | flops 220774400 | bytes 1148932 | tf_op jit(solution)/shard_map/rbi,oi->rbo/dot_general | solution.py:47
  48.8 1.8 %convolution_add_fusion.3 = f32[66,17,128]{2,0,1:T(8,128)S(1)} fusion(f32[66,17,128]{2,0,1:T(8,128)S(1)} %fusion.18, f32[66,17,128]{2,1,0:T(8,128)S(1)} %get-tuple-element.4, f32[]{:T(128)} %exponential_reduce_fusion.3), kind=kOutput, calls=%fused_computation.3 | convolution fusion | flops 220934400 | bytes 1723396 | tf_op jit(solution)/shard_map/rbi,oi->rbo/dot_general | solution.py:48
  52.1 4.4 %slice.244 = f32[32,1024]{1,0:T(8,128)S(1)} slice(f32[64,2048]{1,0:T(8,128)S(1)} %slice.313), slice={[0:64:2], [0:2048:2]} | slice | bytes 262144 | tf_op jit(solution)/shard_map/slice | solution.py:101
  56.5 3.4 %collective-permute-start.5 = (f32[13,1024]{1,0:T(8,128)S(1)}, f32[13,1024]{1,0:T(8,128)S(1)}, u32[]{:S(2)}, u32[]{:S(2)}) collective-permute-start(f32[13,1024]{1,0:T(8,128)S(1)} %get-tuple-element.39), channel_id=1, source_target_pairs={{2,0},{4,2},{6,4},{8,6},{10,8},{12,10},{14,12},{3,1},{5,3},{7,5},{... | collective-permute-start | bytes 159752 | tf_op jit(solution)/shard_map/ppermute | solution.py:17
  59.9 2.3 %collective-permute-start.4 = (f32[13,1024]{1,0:T(8,128)S(1)}, f32[13,1024]{1,0:T(8,128)S(1)}, u32[]{:S(2)}, u32[]{:S(2)}) collective-permute-start(f32[13,1024]{1,0:T(8,128)S(1)} %get-tuple-element.38), channel_id=1, source_target_pairs={{0,2},{2,4},{4,6},{6,8},{8,10},{10,12},{12,14},{1,3},{3,5},{5,7},{... | collective-permute-start | bytes 159752 | tf_op jit(solution)/shard_map/ppermute | solution.py:16
  62.2 1.3 %fusion.376 = (f32[66,2050]{1,0:T(8,128)S(1)}, f32[66,2050]{1,0:T(8,128)S(1)}, f32[66,2050]{1,0:T(8,128)S(1)}, f32[66,2050]{1,0:T(8,128)S(1)}) fusion(f32[66,2176]{1,0:T(8,128)S(1)} %bitcast.140, f32[66,2176]{1,0:T(8,128)S(1)} %bitcast.141, f32[66,2176]{1,0:T(8,128)} %bitcast.142), kind=kLoop, calls=%fused_computation.436 | loop fusion | flops 270600 | bytes 3788400 | tf_op jit(solution)/shard_map/slice | solution.py:51
  65.2 2.5 %fusion.4 = bf16[2,64,2048]{2,1,0:T(8,128)(2,1)} fusion(f32[2,66,2050]{2,1,0:T(8,128)S(1)} %maximum_multiply_fusion), kind=kLoop, calls=%fused_computation.16 | loop fusion | flops 3670016 | bytes 9961472 | tf_op jit(solution)/shard_map/convert_element_type | solution.py:80
  67.8 1.3 %collective-permute-start.6 = (f32[58,13]{1,0:T(8,128)S(1)}, f32[58,13]{1,0:T(8,128)S(1)}, u32[]{:S(2)}, u32[]{:S(2)}) collective-permute-start(f32[58,13]{1,0:T(8,128)S(1)} %get-tuple-element.33), channel_id=1, source_target_pairs={{0,1},{2,3},{4,5},{6,7},{8,9},{10,11},{12,13},{14,15},{16,17},{18,... | collective-permute-start | bytes 9056 | tf_op jit(solution)/shard_map/ppermute | solution.py:16
  69.1 3.0 %collective-permute-start.7 = (f32[58,13]{1,0:T(8,128)S(1)}, f32[58,13]{1,0:T(8,128)S(1)}, u32[]{:S(2)}, u32[]{:S(2)}) collective-permute-start(f32[58,13]{1,0:T(8,128)S(1)} %get-tuple-element.32), channel_id=1, source_target_pairs={{1,0},{3,2},{5,4},{7,6},{9,8},{11,10},{13,12},{15,14},{17,16},{19,... | collective-permute-start | bytes 9056 | tf_op jit(solution)/shard_map/ppermute | solution.py:17
  78.4 1.2 %fusion.51 = f32[34,9,128]{2,0,1:T(8,128)S(1)} fusion(f32[34,9,128]{2,1,0:T(8,128)S(1)} %get-tuple-element.31, f32[]{:T(128)} %exponential_reduce_fusion.3), kind=kOutput, calls=%fused_computation.86 | convolution fusion | flops 60342272 | bytes 313348 | tf_op jit(solution)/shard_map/rbi,oi->rbo/dot_general | solution.py:47
  79.5 1.1 %convolution_add_fusion.8 = f32[34,9,128]{2,0,1:T(8,128)S(1)} fusion(f32[34,9,128]{2,0,1:T(8,128)S(1)} %fusion.51, f32[34,9,128]{2,1,0:T(8,128)S(1)} %get-tuple-element.30, f32[]{:T(128)} %exponential_reduce_fusion.3), kind=kOutput, calls=%fused_computation.9 | convolution fusion | flops 60397824 | bytes 470020 | tf_op jit(solution)/shard_map/rbi,oi->rbo/dot_general | solution.py:48
  83.4 1.1 %fusion.48 = f32[34,9,128]{2,0,1:T(8,128)S(1)} fusion(f32[34,9,128]{2,1,0:T(8,128)S(1)} %get-tuple-element.27, f32[]{:T(128)} %exponential_reduce_fusion.2), kind=kOutput, calls=%fused_computation.83 | convolution fusion | flops 60342272 | bytes 313348 | tf_op jit(solution)/shard_map/rbi,oi->rbo/dot_general | solution.py:47
  85.9 1.1 %fusion.54 = f32[34,9,128]{2,0,1:T(8,128)S(1)} fusion(f32[34,9,128]{2,1,0:T(8,128)S(1)} %get-tuple-element.29, f32[]{:T(128)} %exponential_reduce_fusion.4), kind=kOutput, calls=%fused_computation.89 | convolution fusion | flops 60342272 | bytes 313348 | tf_op jit(solution)/shard_map/rbi,oi->rbo/dot_general | solution.py:47
  92.0 3.9 %all_to_all.15 = bf16[6,32,1024]{2,0,1:T(8,128)(2,1)S(1)} all-to-all(bf16[6,32,1024]{2,0,1:T(8,128)(2,1)S(1)} %copy.117), channel_id=1, replica_groups=mesh['slab'=2,'row'=8,'col'=2] {'col'}, dimensions={1} | all-to-all | bytes 786432 | tf_op jit(solution)/shard_map/all_to_all | solution.py:114
  (123 shorter events, 30.5 us)
Async XLA Ops:
  0.6 11.1 %copy-start.3 = (f32[64,2048]{1,0:T(8,128)S(1)}, f32[64,2048]{1,0:T(8,128)}, u32[]{:S(2)}) copy-start(f32[64,2048]{1,0:T(8,128)} %param.1) | copy-start | bytes 1572868
  1.7 6.3 %collective-permute-start.1 = (f32[13,2048]{1,0:T(8,128)S(1)}, f32[13,2048]{1,0:T(8,128)S(1)}, u32[]{:S(2)}, u32[]{:S(2)}) collective-permute-start(f32[13,2048]{1,0:T(8,128)S(1)} %get-tuple-element.21), channel_id=1, source_target_pairs={{2,0},{4,2},{6,4},{8,6},{10,8},{12,10},{14,12},{3,1},{5,3},{7,5},{... | collective-permute-start | bytes 319496 | tf_op jit(solution)/shard_map/ppermute | solution.py:17
  4.7 7.0 %collective-permute-start = (f32[13,2048]{1,0:T(8,128)S(1)}, f32[13,2048]{1,0:T(8,128)S(1)}, u32[]{:S(2)}, u32[]{:S(2)}) collective-permute-start(f32[13,2048]{1,0:T(8,128)S(1)} %get-tuple-element.20), channel_id=1, source_target_pairs={{0,2},{2,4},{4,6},{6,8},{8,10},{10,12},{12,14},{1,3},{3,5},{5,7},{... | collective-permute-start | bytes 319496 | tf_op jit(solution)/shard_map/ppermute | solution.py:16
  11.9 8.1 %collective-permute-start.2 = (f32[90,13]{1,0:T(8,128)S(1)}, f32[90,13]{1,0:T(8,128)S(1)}, u32[]{:S(2)}, u32[]{:S(2)}) collective-permute-start(f32[90,13]{1,0:T(8,128)S(1)} %get-tuple-element.15), channel_id=1, source_target_pairs={{0,1},{2,3},{4,5},{6,7},{8,9},{10,11},{12,13},{14,15},{16,17},{18,... | collective-permute-start | bytes 14048 | tf_op jit(solution)/shard_map/ppermute | solution.py:16
  13.2 6.9 %collective-permute-start.3 = (f32[90,13]{1,0:T(8,128)S(1)}, f32[90,13]{1,0:T(8,128)S(1)}, u32[]{:S(2)}, u32[]{:S(2)}) collective-permute-start(f32[90,13]{1,0:T(8,128)S(1)} %get-tuple-element.14), channel_id=1, source_target_pairs={{1,0},{3,2},{5,4},{7,6},{9,8},{11,10},{13,12},{15,14},{17,16},{19,... | collective-permute-start | bytes 14048 | tf_op jit(solution)/shard_map/ppermute | solution.py:17
  50.9 11.3 %copy-start = (f32[9,8,17,128]{3,1,2,0:T(8,128)S(1)}, f32[9,8,17,128]{3,1,2,0:T(8,128)}, u32[]{:S(2)}) copy-start(f32[9,8,17,128]{3,1,2,0:T(8,128)} %copy.143) | copy-start | bytes 1880068
  50.9 11.3 %copy-start.1 = (f32[9,8,17,128]{3,1,2,0:T(8,128)S(1)}, f32[9,8,17,128]{3,1,2,0:T(8,128)}, u32[]{:S(2)}) copy-start(f32[9,8,17,128]{3,1,2,0:T(8,128)} %copy.145) | copy-start | bytes 1880068
  56.5 11.2 %collective-permute-start.5 = (f32[13,1024]{1,0:T(8,128)S(1)}, f32[13,1024]{1,0:T(8,128)S(1)}, u32[]{:S(2)}, u32[]{:S(2)}) collective-permute-start(f32[13,1024]{1,0:T(8,128)S(1)} %get-tuple-element.39), channel_id=1, source_target_pairs={{2,0},{4,2},{6,4},{8,6},{10,8},{12,10},{14,12},{3,1},{5,3},{7,5},{... | collective-permute-start | bytes 159752 | tf_op jit(solution)/shard_map/ppermute | solution.py:17
  59.9 7.8 %collective-permute-start.4 = (f32[13,1024]{1,0:T(8,128)S(1)}, f32[13,1024]{1,0:T(8,128)S(1)}, u32[]{:S(2)}, u32[]{:S(2)}) collective-permute-start(f32[13,1024]{1,0:T(8,128)S(1)} %get-tuple-element.38), channel_id=1, source_target_pairs={{0,2},{2,4},{4,6},{6,8},{8,10},{10,12},{12,14},{1,3},{3,5},{5,7},{... | collective-permute-start | bytes 159752 | tf_op jit(solution)/shard_map/ppermute | solution.py:16
  63.5 1.1 %copy-start.2 = (f32[9,8,17,128]{3,1,2,0:T(8,128)S(1)}, f32[9,8,17,128]{3,1,2,0:T(8,128)}, u32[]{:S(2)}) copy-start(f32[9,8,17,128]{3,1,2,0:T(8,128)} %copy.144) | copy-start | bytes 1880068
  67.8 5.4 %collective-permute-start.6 = (f32[58,13]{1,0:T(8,128)S(1)}, f32[58,13]{1,0:T(8,128)S(1)}, u32[]{:S(2)}, u32[]{:S(2)}) collective-permute-start(f32[58,13]{1,0:T(8,128)S(1)} %get-tuple-element.33), channel_id=1, source_target_pairs={{0,1},{2,3},{4,5},{6,7},{8,9},{10,11},{12,13},{14,15},{16,17},{18,... | collective-permute-start | bytes 9056 | tf_op jit(solution)/shard_map/ppermute | solution.py:16
  69.1 4.1 %collective-permute-start.7 = (f32[58,13]{1,0:T(8,128)S(1)}, f32[58,13]{1,0:T(8,128)S(1)}, u32[]{:S(2)}, u32[]{:S(2)}) collective-permute-start(f32[58,13]{1,0:T(8,128)S(1)} %get-tuple-element.32), channel_id=1, source_target_pairs={{1,0},{3,2},{5,4},{7,6},{9,8},{11,10},{13,12},{15,14},{17,16},{19,... | collective-permute-start | bytes 9056 | tf_op jit(solution)/shard_map/ppermute | solution.py:17
where the time goes:
time: 99.3 us; the launch traced here: 97.5 us
  matrix products  40.7 us (41%)
  starting transfers between devices  20.2 us (20%)
  local copies, waits for them, and re-layouts  16.1 us (16%)
  other arithmetic  10.5 us (11%)
  waiting for transfers between devices  4.58 us (5%)
  blocking collectives  3.86 us (4%)
  between operations  1.55 us (2%)
    dot_general x10, matrix products, horizontal(): jnp.einsum('rbi,oi->rbo', tiles[:, :blocks], main, precision=lax.Precisio...  14.7 us
    dot_general x10, matrix products, horizontal(): jnp.einsum('rbi,oi->rbo', tiles[:, 1:], carry, precision=lax.Precision.HI...  14.4 us
    ppermute x4, starting transfers between devices, with_halo(): after = lax.ppermute(first, axis, down)  13.1 us
    dot_general x10, matrix products, vertical(): return jnp.dot(matrix, field, precision=lax.Precision.HIGHEST)  11.7 us
    ppermute x4, starting transfers between devices, with_halo(): before = lax.ppermute(last, axis, up)  7.08 us
    unnamed x30, local copies, waits for them, and re-layouts  5.25 us
    slice x1, local copies, waits for them, and re-layouts, local(): coarse_base = top_level[0::2, 0::2]  4.39 us
    all_to_all x1, blocking collectives, local(): lax.all_to_all(stacked, 'col', split_axis=1, concat_axis=2, tiled=True)  3.86 us
  transfers between devices with their start and end apart: 8, of which 2 were waited for; matrix products, arithmetic and copies ran while one was open for 10% of the time, Pallas kernels for 0%

commit v1 on v0

v1 whole, which is shorter than its diff:
```python
import jax
import jax.numpy as jnp
import numpy as np
from jax import lax
from jax.experimental import pallas as pl
from jax.experimental.pallas import tpu as pltpu
from jax.sharding import PartitionSpec as P

SIGMAS = [1.6 * 2.0 ** (k / 4.0) for k in range(5)]
LEVELS = len(SIGMAS)
REACH = 12
LANES = 128
BLOCK = 256
PAD = 8
FAR = 40
NEAR = 8
BF16 = jnp.bfloat16
F32 = jnp.float32


def taps(sigma):
    offset = np.arange(2 * REACH + 1, dtype=np.float64) - REACH
    weights = np.exp(-offset * offset / (2.0 * sigma * sigma))
    return (weights / weights.sum()).astype(np.float32)


def two_parts(matrix):
    high = np.asarray(matrix, np.float32).astype(BF16)
    low = (np.asarray(matrix, np.float32) - high.astype(np.float32)).astype(BF16)
    return high, low


def tap_at(sigma, index):
    weights = taps(sigma)
    inside = (index >= 0) & (index <= 2 * REACH)
    return np.where(inside, weights[np.clip(index, 0, 2 * REACH)], np.float32(0.0))


def row_matrix(sigma, centres, inputs):
    return tap_at(sigma, inputs[None, :] - centres[:, None] + REACH)


def column_weights(sigma, step):
    width = BLOCK * step
    out = np.arange(BLOCK)[None, :] * step
    high, low = two_parts(tap_at(sigma, np.arange(width)[:, None] - out + REACH))
    lane = np.arange(LANES)[:, None]
    right = np.where(lane < REACH, tap_at(sigma, width + lane - out + REACH), 0.0)
    left = np.where(lane >= LANES - REACH, tap_at(sigma, lane - LANES - out + REACH), 0.0)
    edge_high, edge_low = two_parts(right + left)
    edge = np.concatenate([edge_high.astype(np.float32), edge_high.astype(np.float32)])
    edge[:LANES] += np.roll(edge_low.astype(np.float32), 32, axis=0)
    return high, low, edge.astype(BF16)


def split(value):
    high = value.astype(BF16)
    low = (value - high.astype(F32)).astype(BF16)
    return high, low


def mm(a, b):
    return jnp.dot(a, b, preferred_element_type=F32)


def edge_columns(high, low, at, width):
    def both(ref):
        left = ref[:, at - LANES : at].astype(F32)
        right = ref[:, at + width : at + width + LANES].astype(F32)
        lane = lax.broadcasted_iota(jnp.int32, left.shape, 1)
        return jnp.where(lane < LANES // 2, right, left), lane

    eh, lane = both(high)
    el, _ = both(low)
    again = pltpu.roll(eh, 32, 1)
    eh = jnp.where((lane >= 16) & (lane < 64), again, eh)
    return jnp.concatenate([eh.astype(BF16), el.astype(BF16)], axis=1)


def hess_rows(d, first, count, at, width):
    up = d[first - 1 : first - 1 + count, at : at + width]
    mid = d[first : first + count, at : at + width]
    down = d[first + 1 : first + 1 + count, at : at + width]
    whole = slice(first - 1, first + count + 1)
    after = d[whole, at + 1 : at + width + 1]
    before = d[whole, at - 1 : at + width - 1]
    across = after - before
    twice = 2.0 * mid
    dxx = after[1:-1] + before[1:-1] - twice
    dyy = up + down - twice
    dxy = (across[2:] - across[:-2]) * 0.25
    return dxx * dyy - dxy * dxy


def pack_kernel(x_ref, side_ref, own_ref, up_ref, down_ref):
    rows, cols = x_ref.shape

    def put(value, lo, hi):
        high, low = split(value)
        own_ref[:rows, lo:hi] = high
        own_ref[rows:, lo:hi] = low
        up_ref[:FAR, lo:hi] = high[:FAR]
        up_ref[FAR:, lo:hi] = low[:NEAR]
        down_ref[:FAR, lo:hi] = high[rows - FAR :]
        down_ref[FAR:, lo:hi] = low[rows - NEAR :]

    for at in range(0, cols, BLOCK):
        put(x_ref[:, at : at + BLOCK], at, at + BLOCK)
    put(side_ref[...], cols, cols + LANES)


def fine_kernel(place_ref, own_ref, top_ref, bot_ref, lh_ref, ll_ref, bh_ref, bl_ref,
                wc_ref, wl_ref, we_ref, dc_ref, dl_ref, de_ref,
                dog_ref, hess_ref, keep_ref, send_ref,
                vh, vl, bvh, bvl, lev, d1, d2):
    _, out_rows, cols = dog_ref.shape
    row, col, last_row, coarse_height = place_ref[0], place_ref[1], place_ref[2], place_ref[3]
    tall = out_rows + 2 * PAD
    base_rows = bh_ref.shape[1]
    diffs = {1: d1, 2: d2}
    is_left = col == 0

    def rows_of(at, width):
        stack = jnp.concatenate(
            [own_ref[:, at : at + width], top_ref[:, at : at + width], bot_ref[:, at : at + width]], axis=0
        )
        base = mm(bh_ref[col], stack) + mm(bl_ref[col], stack)
        yield None, base
        for s in range(LEVELS):
            part = slice(s * tall, (s + 1) * tall)
            yield s, mm(lh_ref[part], stack) + mm(ll_ref[part], stack)

    for at in range(0, cols, BLOCK):
        for s, value in rows_of(at, BLOCK):
            high, low = split(value)
            to = slice(LANES + at, LANES + at + BLOCK)
            if s is None:
                bvh[:, to], bvl[:, to] = high, low
            else:
                vh[s, :, to], vl[s, :, to] = high, low
    for s, value in rows_of(cols, LANES):
        left = jnp.where(is_left, 0.0, value)
        right = jnp.where(is_left, value, 0.0)
        for part, to in ((left, slice(0, LANES)), (right, slice(LANES + cols, 2 * LANES + cols))):
            high, low = split(part)
            if s is None:
                bvh[:, to], bvl[:, to] = high, low
            else:
                vh[s, :, to], vl[s, :, to] = high, low

    first_keep = row * (out_rows // 2) - REACH - 1 + col * (out_rows // 4)
    first_send = row * (out_rows // 2) - REACH - 1 + (1 - col) * (out_rows // 4)
    half = base_rows // 2
    index = lax.broadcasted_iota(jnp.int32, (base_rows, BLOCK), 0)
    place = jnp.where(index < half, first_keep + index, first_send + index - half)
    inside = (place >= 0) & (place < coarse_height)
    for j in range(cols // (2 * BLOCK)):
        at = LANES + 2 * BLOCK * j
        high = bvh[:, at : at + 2 * BLOCK]
        low = bvl[:, at : at + 2 * BLOCK]
        edge = edge_columns(bvh, bvl, at, 2 * BLOCK)
        value = mm(high, dc_ref[...]) + mm(low, dc_ref[...]) + mm(high, dl_ref[...]) + mm(edge, de_ref[...])
        value = jnp.where(inside, value, 0.0)
        keep_ref[:, j * BLOCK : (j + 1) * BLOCK] = value[:half]
        send_ref[:, j * BLOCK : (j + 1) * BLOCK] = value[half:]

    group = 4
    seam = pl.multiple_of(jnp.where(is_left, cols, 0), LANES)
    for s in range(LEVELS):
        k = s - 1
        for g in range(0, cols // BLOCK, group):
            ats = [LANES + BLOCK * (g + i) for i in range(group)]
            high = jnp.concatenate([vh[s, :, at : at + BLOCK] for at in ats], axis=0)
            low = jnp.concatenate([vl[s, :, at : at + BLOCK] for at in ats], axis=0)
            edge = jnp.concatenate([edge_columns(vh.at[s], vl.at[s], at, BLOCK) for at in ats], axis=0)
            value = mm(high, wc_ref[s]) + mm(low, wc_ref[s]) + mm(high, wl_ref[s]) + mm(edge, we_ref[s])
            for i, at in enumerate(ats):
                new = value[i * tall : (i + 1) * tall]
                if s > 0:
                    d = new - lev[:, at : at + BLOCK]
                    dog_ref[k, :, at - LANES : at - LANES + BLOCK] = (20.0 * d[PAD : PAD + out_rows]).astype(BF16)
                    if k in diffs:
                        diffs[k][:, at : at + BLOCK] = d
                lev[:, at : at + BLOCK] = new
        if s in (1, 2, 3):
            high = vh[s, :, pl.ds(seam, BLOCK)]
            low = vl[s, :, pl.ds(seam, BLOCK)]
            new = mm(high, wc_ref[s]) + mm(low, wc_ref[s]) + mm(high, wl_ref[s])
            if s > 1:
                d = new - lev[:, cols + 2 * LANES :]
                diffs[k][:, :LANES] = jnp.where(is_left, 0.0, d[:, :LANES])
                diffs[k][:, cols + LANES :] = jnp.where(is_left, d[:, LANES:], 0.0)
            lev[:, cols + 2 * LANES :] = new

    for m, k in enumerate((1, 2)):
        d = diffs[k]

        @pl.when(row == 0)
        def _():
            d[PAD - 1 : PAD, :] = jnp.zeros((1, d.shape[1]), F32)

        @pl.when(row == last_row)
        def _():
            d[PAD + out_rows : PAD + out_rows + 1, :] = jnp.zeros((1, d.shape[1]), F32)

        for at in range(0, cols, BLOCK):
            h = hess_rows(d, PAD, out_rows, LANES + at, BLOCK)
            hess_ref[m, :, at : at + BLOCK] = (5000.0 * h).astype(BF16)


def coarse_kernel(place_ref, keep_ref, other_ref, lh_ref, wc_ref, wl_ref, we_ref,
                  dog_ref, hess_ref, vh, vl, lev, d1, d2):
    _, out_rows, cols = dog_ref.shape
    row, col, last_row = place_ref[0], place_ref[1], place_ref[2]
    tall = out_rows + 2 * PAD
    diffs = {1: d1, 2: d2}
    is_left = col == 0
    half = cols // 2
    zero = jnp.zeros((tall, LANES), BF16)
    for s in range(LEVELS):
        for ref in (vh, vl):
            ref[s, :, :LANES] = zero
            ref[s, :, LANES + cols :] = zero
    zero = jnp.zeros((tall, LANES), F32)
    for d in (d1, d2):
        d[:, :LANES] = zero
        d[:, LANES + cols :] = zero

    for at in range(0, cols, BLOCK):
        source = slice(at % half, at % half + BLOCK)
        first = is_left if at < half else jnp.logical_not(is_left)
        high, low = split(jnp.where(first, keep_ref[:, source], other_ref[:, source]))
        stack = jnp.concatenate([high, low, high], axis=0)
        value = mm(lh_ref[...], stack)
        to = slice(LANES + at, LANES + at + BLOCK)
        for s in range(LEVELS):
            vh[s, :, to], vl[s, :, to] = split(value[s * tall : (s + 1) * tall])

    group = 8
    for s in range(LEVELS):
        k = s - 1
        for g in range(0, cols // BLOCK, group):
            ats = [LANES + BLOCK * (g + i) for i in range(group)]
            high = jnp.concatenate([vh[s, :, at : at + BLOCK] for at in ats], axis=0)
            low = jnp.concatenate([vl[s, :, at : at + BLOCK] for at in ats], axis=0)
            edge = jnp.concatenate([edge_columns(vh.at[s], vl.at[s], at, BLOCK) for at in ats], axis=0)
            value = mm(high, wc_ref[s]) + mm(low, wc_ref[s]) + mm(high, wl_ref[s]) + mm(edge, we_ref[s])
            for i, at in enumerate(ats):
                new = value[i * tall : (i + 1) * tall]
                if s > 0:
                    d = new - lev[:, at : at + BLOCK]
                    dog_ref[k, :, at - LANES : at - LANES + BLOCK] = (80.0 * d[PAD : PAD + out_rows]).astype(BF16)
                    if k in diffs:
                        diffs[k][:, at : at + BLOCK] = d
                lev[:, at : at + BLOCK] = new

    for m, k in enumerate((1, 2)):
        d = diffs[k]

        @pl.when((row == 0) & (col == 0))
        def _():
            d[PAD - 1 : PAD, :] = jnp.zeros((1, d.shape[1]), F32)

        @pl.when((row == last_row) & (col == 1))
        def _():
            d[PAD + out_rows : PAD + out_rows + 1, :] = jnp.zeros((1, d.shape[1]), F32)

        for at in range(0, cols, BLOCK):
            h = hess_rows(d, PAD, out_rows, LANES + at, BLOCK)
            hess_ref[m, :, at : at + BLOCK] = (200000.0 * h).astype(BF16)


def fine_constants(rows):
    own = np.arange(rows)
    top = np.arange(-FAR, 0)
    bot = np.arange(rows, rows + FAR)
    inputs = np.concatenate([own, own, top, top[FAR - NEAR :], bot, bot[:NEAR]])
    is_high = np.concatenate(
        [np.ones(rows), np.zeros(rows), np.ones(FAR), np.zeros(NEAR), np.ones(FAR), np.zeros(NEAR)]
    )

    def matrices(sigma, centres, valid):
        high, low = two_parts(row_matrix(sigma, centres, inputs) * valid[:, None])
        return high, (low.astype(np.float32) * is_high[None, :]).astype(BF16)

    centres = np.arange(-PAD, rows + PAD)
    valid = ((centres >= -1) & (centres <= rows)).astype(np.float32)
    level = [matrices(s, centres, valid) for s in SIGMAS]
    strip = rows // 4
    count = strip + 2 * (REACH + 1)
    padded = -(-count // 16) * 16
    ok = (np.arange(padded) < count).astype(np.float32)
    base = []
    for core in range(2):
        both = [2 * (c * strip - REACH - 1 + np.arange(padded)) for c in (core, 1 - core)]
        base.append(matrices(SIGMAS[-1], np.concatenate(both), np.concatenate([ok, ok])))
    return (
        np.concatenate([a for a, _ in level]),
        np.concatenate([b for _, b in level]),
        np.stack([a for a, _ in base]),
        np.stack([b for _, b in base]),
        padded,
    )


def coarse_constants(strip, padded):
    inputs = np.arange(padded) - REACH - 1
    centres = np.arange(-PAD, strip + PAD)
    valid = ((centres >= -1) & (centres <= strip)).astype(np.float32)
    parts = []
    for s in SIGMAS:
        high, low = two_parts(row_matrix(s, centres, inputs) * valid[:, None])
        parts.append(np.concatenate([high, high, low], axis=1))
    return np.concatenate(parts)


def vmem_specs(count):
    return [pl.BlockSpec(memory_space=pltpu.VMEM) for _ in range(count)]


def local(image):
    rows, cols = image.shape
    row_count = lax.axis_size("row")
    row = lax.axis_index("row")
    col = lax.axis_index("col")
    strip = rows // 4
    lh, ll, bh, bl, padded = fine_constants(rows)
    cw = coarse_constants(strip, padded)
    bands = [column_weights(s, 1) for s in SIGMAS]
    wc, wl, we = (np.stack([b[i] for b in bands]) for i in range(3))
    dc, dl, de = column_weights(SIGMAS[-1], 2)
    place = jnp.stack([row, col, jnp.int32(row_count - 1), jnp.int32(row_count * rows // 2)]).astype(jnp.int32)

    side = jnp.where(col == 0, image[:, cols - LANES :], image[:, :LANES])
    side = lax.ppermute(side, "col", [(0, 1), (1, 0)])
    wide = cols + LANES
    own, up, down = pl.pallas_call(
        pack_kernel,
        out_shape=(
            jax.ShapeDtypeStruct((2 * rows, wide), BF16),
            jax.ShapeDtypeStruct((FAR + NEAR, wide), BF16),
            jax.ShapeDtypeStruct((FAR + NEAR, wide), BF16),
        ),
        in_specs=vmem_specs(2),
        out_specs=tuple(vmem_specs(3)),
        name="pack",
    )(image, side)
    bot = lax.ppermute(up, "row", [(i + 1, i) for i in range(row_count - 1)])
    top = lax.ppermute(down, "row", [(i, i + 1) for i in range(row_count - 1)])

    tall = rows + 2 * PAD
    smem = pl.BlockSpec(memory_space=pltpu.SMEM)
    dog_fine, hess_fine, keep, send = pl.pallas_call(
        fine_kernel,
        out_shape=(
            jax.ShapeDtypeStruct((4, rows, cols), BF16),
            jax.ShapeDtypeStruct((2, rows, cols), BF16),
            jax.ShapeDtypeStruct((padded, cols // 2), F32),
            jax.ShapeDtypeStruct((padded, cols // 2), F32),
        ),
        in_specs=[smem] + vmem_specs(13),
        out_specs=tuple(vmem_specs(4)),
        scratch_shapes=[
            pltpu.VMEM((LEVELS, tall, cols + 2 * LANES), BF16),
            pltpu.VMEM((LEVELS, tall, cols + 2 * LANES), BF16),
            pltpu.VMEM((2 * padded, cols + 2 * LANES), BF16),
            pltpu.VMEM((2 * padded, cols + 2 * LANES), BF16),
            pltpu.VMEM((tall, cols + 2 * LANES + BLOCK), F32),
            pltpu.VMEM((tall, cols + 2 * LANES), F32),
            pltpu.VMEM((tall, cols + 2 * LANES), F32),
        ],
        name="fine",
    )(place, own, top, bot, lh, ll, bh, bl, wc, wl, we, dc, dl, de)

    other = lax.ppermute(send, "col", [(0, 1), (1, 0)])
    small = strip + 2 * PAD
    dog_coarse, hess_coarse = pl.pallas_call(
        coarse_kernel,
        out_shape=(
            jax.ShapeDtypeStruct((4, strip, cols), BF16),
            jax.ShapeDtypeStruct((2, strip, cols), BF16),
        ),
        in_specs=[smem] + vmem_specs(6),
        out_specs=tuple(vmem_specs(2)),
        scratch_shapes=[
            pltpu.VMEM((LEVELS, small, cols + 2 * LANES), BF16),
            pltpu.VMEM((LEVELS, small, cols + 2 * LANES), BF16),
            pltpu.VMEM((small, cols + 2 * LANES), F32),
            pltpu.VMEM((small, cols + 2 * LANES), F32),
            pltpu.VMEM((small, cols + 2 * LANES), F32),
        ],
        name="coarse",
    )(place, keep, other, cw, wc, wl, we)
    return dog_fine, hess_fine, dog_coarse, hess_coarse


def solution(mesh):
    return jax.shard_map(
        local,
        mesh=mesh,
        in_specs=(P(("slab", "row"), "col"),),
        out_specs=(
            P(None, ("slab", "row"), "col"),
            P(None, ("slab", "row"), "col"),
            P(None, ("slab", "row", "col"), None),
            P(None, ("slab", "row", "col"), None),
        ),
        check_vma=False,
    )
```

time: 99.3 us -> 38.2 us (0.38); the launches traced: 97.5 us -> 37.9 us
  matrix products: 40.7 us -> 0 us
  Pallas kernels: 0 us -> 16.6 us
  local copies, waits for them, and re-layouts: 16.1 us -> 1.97 us
  starting transfers between devices: 20.2 us -> 7.34 us
  other arithmetic: 10.5 us -> 1.44 us
  waiting for transfers between devices: 4.58 us -> 9.85 us
  blocking collectives: 3.86 us -> 0 us
    dot_general x30 -> x0, matrix products: 40.7 us -> none  [the longest x10 14.7 us: horizontal(): jnp.einsum('rbi,oi->rbo', tiles[:, :blocks], main, precision=lax.Precisio...]
    pallas_call x0 -> x3, Pallas kernels: none -> 16.6 us  [the longest x1 10.2 us: local(): pl.pallas_call(fine_kernel, out_shape=(jax.ShapeDtypeStruct((4, rows, col...]
    ppermute x8 -> x4, starting transfers between devices: 20.2 us -> 7.34 us  [the longest x1 3.14 us: local(): top = lax.ppermute(down, 'row', [(i, i + 1) for i in range(row_count - 1)])]
    slice x18 -> x0, local copies, waits for them, and re-layouts: 7.96 us -> none  [the longest x1 4.39 us: local(): coarse_base = top_level[0::2, 0::2]]
    ppermute x8 -> x4, waiting for transfers between devices: 4.58 us -> 9.85 us  [the longest x1 5.19 us: local(): bot = lax.ppermute(up, 'row', [(i + 1, i) for i in range(row_count - 1)])]
    all_to_all x1 -> x0, blocking collectives: 3.86 us -> none  [local(): lax.all_to_all(stacked, 'col', split_axis=1, concat_axis=2, tiled=True)]
    unnamed x30 -> x8, local copies, waits for them, and re-layouts: 5.25 us -> 1.97 us
    reduce_sum x5 -> x0, other arithmetic: 3.15 us -> none  [band(): total = jnp.sum(jnp.exp(-spread * spread / (2.0 * sigma * sigma)))]
  transfers between devices with their start and end apart: 8 -> 4, of which waited for: 2 -> 4; matrix products, arithmetic and copies ran while one was open for 10% -> 2% of each run, Pallas kernels for 0% -> 0%
where the time goes in v1:
time: 38.2 us; the launch traced here: 37.9 us
  Pallas kernels  16.6 us (43%)
  waiting for transfers between devices  9.85 us (26%)
  starting transfers between devices  7.34 us (19%)
  local copies, waits for them, and re-layouts  1.97 us (5%)
  other arithmetic  1.44 us (4%)
  between operations  0.67 us (2%)
    pallas_call x1, Pallas kernels, local(): pl.pallas_call(fine_kernel, out_shape=(jax.ShapeDtypeStruct((4, rows, col...  10.2 us
    ppermute x1, waiting for transfers between devices, local(): bot = lax.ppermute(up, 'row', [(i + 1, i) for i in range(row_count - 1)])  5.19 us
    pallas_call x1, Pallas kernels, local(): pl.pallas_call(coarse_kernel, out_shape=(jax.ShapeDtypeStruct((4, strip,...  4.35 us
    ppermute x1, starting transfers between devices, local(): top = lax.ppermute(down, 'row', [(i, i + 1) for i in range(row_count - 1)])  3.14 us
    ppermute x1, starting transfers between devices, local(): bot = lax.ppermute(up, 'row', [(i + 1, i) for i in range(row_count - 1)])  3.03 us
    ppermute x1, waiting for transfers between devices, local(): top = lax.ppermute(down, 'row', [(i, i + 1) for i in range(row_count - 1)])  2.52 us
    pallas_call x1, Pallas kernels, local(): pl.pallas_call(pack_kernel, out_shape=(jax.ShapeDtypeStruct((2 * rows, wi...  2.03 us
    unnamed x8, local copies, waits for them, and re-layouts  1.97 us
  transfers between devices with their start and end apart: 4, of which 4 were waited for; matrix products, arithmetic and copies ran while one was open for 2% of the time, Pallas kernels for 0%

profile of v1, /device:TPU:11, one launch (start us, length us, event | category | flops | bytes accessed | tf_op | source)
XLA Modules:
  0.0 37.9 jit_solution(10045683392149594019)
XLA Ops:
  0.6 0.8 %slice_select_fusion = f32[64,128]{1,0:T(8,128)S(1)} fusion(f32[64,2048]{1,0:T(8,128)} %x_ref.1, pred[]{:T(512)S(6)} %eq.3), kind=kLoop, calls=%fused_computation | loop fusion | flops 8192 | bytes 98305 | tf_op jit(solution)/shard_map/jit(_where)/select_n | solution.py:334
  1.4 0.7 %collective-permute-start = (f32[64,128]{1,0:T(8,128)S(1)}, f32[64,128]{1,0:T(8,128)S(1)}, u32[]{:S(2)}, u32[]{:S(2)}) collective-permute-start(f32[64,128]{1,0:T(8,128)S(1)} %slice_select_fusion), channel_id=1, source_target_pairs={{0,1},{1,0},{2,3},{3,2},{4,5},{5,4},{6,7},{7,6},{8,9},{9,8},{10,11... | collective-permute-start | bytes 98312 | tf_op jit(solution)/shard_map/ppermute | solution.py:335
  2.1 0.9 %collective-permute-done.side_ref = f32[64,128]{1,0:T(8,128)S(1)} collective-permute-done((f32[64,128]{1,0:T(8,128)S(1)}, f32[64,128]{1,0:T(8,128)S(1)}, u32[]{:S(2)}, u32[]{:S(2)}) %collective-permute-start) | collective-permute-done | bytes 32800 | tf_op jit(solution)/shard_map/ppermute | solution.py:335
  3.0 0.0 copy-start.3
  3.0 0.6 %copy-done.3 = f32[64,128]{1,0:T(8,128)} copy-done((f32[64,128]{1,0:T(8,128)}, f32[64,128]{1,0:T(8,128)S(1)}, u32[]{:S(2)}) %copy-start.3) | copy-done | bytes 32792
  3.6 2.0 %pack.1 = (bf16[128,2176]{1,0:T(8,128)(2,1)}, bf16[48,2176]{1,0:T(8,128)(2,1)}, bf16[48,2176]{1,0:T(8,128)(2,1)}) custom-call(f32[64,2048]{1,0:T(8,128)} %x_ref.1, f32[64,128]{1,0:T(8,128)} %copy-done.3), custom_call_target="tpu_custom_call" | custom-call | tf_op jit(solution)/shard_map/pack/pallas_call | solution.py:337
  5.6 3.1 %collective-permute-start.1 = (bf16[48,2176]{1,0:T(8,128)(2,1)}, bf16[48,2176]{1,0:T(8,128)(2,1)S(1)}, u32[]{:S(2)}, u32[]{:S(2)}) collective-permute-start(bf16[48,2176]{1,0:T(8,128)(2,1)} %get-tuple-element.14), channel_id=1, source_target_pairs={{0,2},{2,4},{4,6},{6,8},{8,10},{10,12},{12,14},{1,3},{3,5},{5,7},{... | collective-permute-start | bytes 626696 | tf_op jit(solution)/shard_map/ppermute | solution.py:349
  8.7 3.0 %collective-permute-start.2 = (bf16[48,2176]{1,0:T(8,128)(2,1)}, bf16[48,2176]{1,0:T(8,128)(2,1)S(1)}, u32[]{:S(2)}, u32[]{:S(2)}) collective-permute-start(bf16[48,2176]{1,0:T(8,128)(2,1)} %get-tuple-element.15), channel_id=1, source_target_pairs={{2,0},{4,2},{6,4},{8,6},{10,8},{12,10},{14,12},{3,1},{5,3},{7,5},{... | collective-permute-start | bytes 626696 | tf_op jit(solution)/shard_map/ppermute | solution.py:348
  11.8 0.7 %pad_add_fusion.place_ref = s32[4]{0:T(128)} fusion(s32[1]{0:T(128)} %constant.34.clone.1, s32[1]{0:T(128)} %constant.15.clone.1, s32[1]{0:T(128)} %bitcast.1, s32[1]{0:T(128)} %bitcast), kind=kLoop, calls=%fused_computation.1 | loop fusion | flops 12 | bytes 32 | tf_op jit(solution)/shard_map/stack | solution.py:332
  12.4 2.5 %collective-permute-done.1.top_ref = bf16[48,2176]{1,0:T(8,128)(2,1)S(1)} collective-permute-done((bf16[48,2176]{1,0:T(8,128)(2,1)}, bf16[48,2176]{1,0:T(8,128)(2,1)S(1)}, u32[]{:S(2)}, u32[]{:S(2)}) %collective-permute-start.1) | collective-permute-done | bytes 208928 | tf_op jit(solution)/shard_map/ppermute | solution.py:349
  15.0 0.0 copy-start
  15.0 5.2 %collective-permute-done.2.bot_ref = bf16[48,2176]{1,0:T(8,128)(2,1)S(1)} collective-permute-done((bf16[48,2176]{1,0:T(8,128)(2,1)}, bf16[48,2176]{1,0:T(8,128)(2,1)S(1)}, u32[]{:S(2)}, u32[]{:S(2)}) %collective-permute-start.2) | collective-permute-done | bytes 208928 | tf_op jit(solution)/shard_map/ppermute | solution.py:348
  20.2 0.0 copy-start.1
  20.2 0.0 copy-done
  20.2 0.7 %copy-done.1 = bf16[48,2176]{1,0:T(8,128)(2,1)} copy-done((bf16[48,2176]{1,0:T(8,128)(2,1)}, bf16[48,2176]{1,0:T(8,128)(2,1)S(1)}, u32[]{:S(2)}) %copy-start.1) | copy-done | bytes 208920
  20.8 10.2 %fine.1 = (bf16[4,64,2048]{2,1,0:T(8,128)(2,1)}, bf16[2,64,2048]{2,1,0:T(8,128)(2,1)}, f32[48,1024]{1,0:T(8,128)}, f32[48,1024]{1,0:T(8,128)}) custom-call(s32[4]{0:T(128)} %pad_add_fusion.place_ref, bf16[128,2176]{1,0:T(8,128)(2,1)} %get-tuple-element.13.own_ref, bf16[48,2176]{1,0:T(8,128)(2,1)} %copy-done, bf16[48,2176]{1,0:T(8,128)(2,1)} %copy-done.1, ...), custom_call_target="tpu_custom_call" | custom-call | tf_op jit(solution)/shard_map/fine/pallas_call | solution.py:353
  31.1 0.5 %collective-permute-start.3 = (f32[48,1024]{1,0:T(8,128)}, f32[48,1024]{1,0:T(8,128)S(1)}, u32[]{:S(2)}, u32[]{:S(2)}) collective-permute-start(f32[48,1024]{1,0:T(8,128)} %get-tuple-element.19), channel_id=1, source_target_pairs={{0,1},{1,0},{2,3},{3,2},{4,5},{5,4},{6,7},{7,6},{8,9},{9,8},{10,11... | collective-permute-start | bytes 589832 | tf_op jit(solution)/shard_map/ppermute | solution.py:375
  31.5 1.3 %collective-permute-done.3.other_ref = f32[48,1024]{1,0:T(8,128)S(1)} collective-permute-done((f32[48,1024]{1,0:T(8,128)}, f32[48,1024]{1,0:T(8,128)S(1)}, u32[]{:S(2)}, u32[]{:S(2)}) %collective-permute-start.3) | collective-permute-done | bytes 196640 | tf_op jit(solution)/shard_map/ppermute | solution.py:375
  32.8 0.0 copy-start.2
  32.8 0.7 %copy-done.2 = f32[48,1024]{1,0:T(8,128)} copy-done((f32[48,1024]{1,0:T(8,128)}, f32[48,1024]{1,0:T(8,128)S(1)}, u32[]{:S(2)}) %copy-start.2) | copy-done | bytes 196632
  33.5 4.4 %coarse.1 = (bf16[4,16,2048]{2,1,0:T(8,128)(2,1)}, bf16[2,16,2048]{2,1,0:T(8,128)(2,1)}) custom-call(s32[4]{0:T(128)} %pad_add_fusion.place_ref, f32[48,1024]{1,0:T(8,128)} %get-tuple-element.18.keep_ref, f32[48,1024]{1,0:T(8,128)} %copy-done.2, bf16[160,144]{1,0:T(8,128)(2,1)} %constant.46.clone.lh_ref, bf16[5,256,256]{2,1,0:T(8,128)(2,1)} %constant.40.clone.wc_ref, ...), custom_call_target="tpu_custom_call" | custom-call | tf_op jit(solution)/shard_map/coarse/pallas_call | solution.py:377
Async XLA Ops:
  1.4 1.5 %collective-permute-start = (f32[64,128]{1,0:T(8,128)S(1)}, f32[64,128]{1,0:T(8,128)S(1)}, u32[]{:S(2)}, u32[]{:S(2)}) collective-permute-start(f32[64,128]{1,0:T(8,128)S(1)} %slice_select_fusion), channel_id=1, source_target_pairs={{0,1},{1,0},{2,3},{3,2},{4,5},{5,4},{6,7},{7,6},{8,9},{9,8},{10,11... | collective-permute-start | bytes 98312 | tf_op jit(solution)/shard_map/ppermute | solution.py:335
  3.0 0.6 %copy-start.3 = (f32[64,128]{1,0:T(8,128)}, f32[64,128]{1,0:T(8,128)S(1)}, u32[]{:S(2)}) copy-start(f32[64,128]{1,0:T(8,128)S(1)} %collective-permute-done.side_ref) | copy-start | bytes 98308
  5.6 9.4 %collective-permute-start.1 = (bf16[48,2176]{1,0:T(8,128)(2,1)}, bf16[48,2176]{1,0:T(8,128)(2,1)S(1)}, u32[]{:S(2)}, u32[]{:S(2)}) collective-permute-start(bf16[48,2176]{1,0:T(8,128)(2,1)} %get-tuple-element.14), channel_id=1, source_target_pairs={{0,2},{2,4},{4,6},{6,8},{8,10},{10,12},{12,14},{1,3},{3,5},{5,7},{... | collective-permute-start | bytes 626696 | tf_op jit(solution)/shard_map/ppermute | solution.py:349
  8.7 11.4 %collective-permute-start.2 = (bf16[48,2176]{1,0:T(8,128)(2,1)}, bf16[48,2176]{1,0:T(8,128)(2,1)S(1)}, u32[]{:S(2)}, u32[]{:S(2)}) collective-permute-start(bf16[48,2176]{1,0:T(8,128)(2,1)} %get-tuple-element.15), channel_id=1, source_target_pairs={{2,0},{4,2},{6,4},{8,6},{10,8},{12,10},{14,12},{3,1},{5,3},{7,5},{... | collective-permute-start | bytes 626696 | tf_op jit(solution)/shard_map/ppermute | solution.py:348
  15.0 5.2 %copy-start = (bf16[48,2176]{1,0:T(8,128)(2,1)}, bf16[48,2176]{1,0:T(8,128)(2,1)S(1)}, u32[]{:S(2)}) copy-start(bf16[48,2176]{1,0:T(8,128)(2,1)S(1)} %collective-permute-done.1.top_ref) | copy-start | bytes 626692
  20.2 0.7 %copy-start.1 = (bf16[48,2176]{1,0:T(8,128)(2,1)}, bf16[48,2176]{1,0:T(8,128)(2,1)S(1)}, u32[]{:S(2)}) copy-start(bf16[48,2176]{1,0:T(8,128)(2,1)S(1)} %collective-permute-done.2.bot_ref) | copy-start | bytes 626692
  31.1 1.8 %collective-permute-start.3 = (f32[48,1024]{1,0:T(8,128)}, f32[48,1024]{1,0:T(8,128)S(1)}, u32[]{:S(2)}, u32[]{:S(2)}) collective-permute-start(f32[48,1024]{1,0:T(8,128)} %get-tuple-element.19), channel_id=1, source_target_pairs={{0,1},{1,0},{2,3},{3,2},{4,5},{5,4},{6,7},{7,6},{8,9},{9,8},{10,11... | collective-permute-start | bytes 589832 | tf_op jit(solution)/shard_map/ppermute | solution.py:375
  32.8 0.7 %copy-start.2 = (f32[48,1024]{1,0:T(8,128)}, f32[48,1024]{1,0:T(8,128)S(1)}, u32[]{:S(2)}) copy-start(f32[48,1024]{1,0:T(8,128)S(1)} %collective-permute-done.3.other_ref) | copy-start | bytes 589828

commit v2 on v1

v2 whole, which is shorter than its diff:
```python
import jax
import jax.numpy as jnp
import numpy as np
from jax import lax
from jax.experimental import pallas as pl
from jax.experimental.pallas import tpu as pltpu
from jax.sharding import PartitionSpec as P

SIGMAS = [1.6 * 2.0 ** (k / 4.0) for k in range(5)]
LEVELS = len(SIGMAS)
REACH = 12
LANES = 128
BLOCK = 256
PAD = 8
FAR = 40
NEAR = 8
BF16 = jnp.bfloat16
F32 = jnp.float32


def taps(sigma):
    offset = np.arange(2 * REACH + 1, dtype=np.float64) - REACH
    weights = np.exp(-offset * offset / (2.0 * sigma * sigma))
    return (weights / weights.sum()).astype(np.float32)


def two_parts(matrix):
    high = np.asarray(matrix, np.float32).astype(BF16)
    low = (np.asarray(matrix, np.float32) - high.astype(np.float32)).astype(BF16)
    return high, low


def tap_at(sigma, index):
    weights = taps(sigma)
    inside = (index >= 0) & (index <= 2 * REACH)
    return np.where(inside, weights[np.clip(index, 0, 2 * REACH)], np.float32(0.0))


def row_matrix(sigma, centres, inputs):
    return tap_at(sigma, inputs[None, :] - centres[:, None] + REACH)


def column_weights(sigma, step):
    width = BLOCK * step
    out = np.arange(BLOCK)[None, :] * step
    high, low = two_parts(tap_at(sigma, np.arange(width)[:, None] - out + REACH))
    lane = np.arange(LANES)[:, None]
    right = np.where(lane < REACH, tap_at(sigma, width + lane - out + REACH), 0.0)
    left = np.where(lane >= LANES - REACH, tap_at(sigma, lane - LANES - out + REACH), 0.0)
    edge_high, edge_low = two_parts(right + left)
    edge = np.concatenate([edge_high.astype(np.float32), edge_high.astype(np.float32)])
    edge[:LANES] += np.roll(edge_low.astype(np.float32), 32, axis=0)
    return high, low, edge.astype(BF16)


def split(value):
    high = value.astype(BF16)
    low = (value - high.astype(F32)).astype(BF16)
    return high, low


def mm(a, b):
    return jnp.dot(a, b, preferred_element_type=F32)


def edge_columns(high, low, at, width):
    def both(ref):
        left = ref[:, at - LANES : at].astype(F32)
        right = ref[:, at + width : at + width + LANES].astype(F32)
        lane = lax.broadcasted_iota(jnp.int32, left.shape, 1)
        return jnp.where(lane < LANES // 2, right, left), lane

    eh, lane = both(high)
    el, _ = both(low)
    again = pltpu.roll(eh, 32, 1)
    eh = jnp.where((lane >= 16) & (lane < 64), again, eh)
    return jnp.concatenate([eh.astype(BF16), el.astype(BF16)], axis=1)


def hess_tiles(d, rows, first_tile, count, gain, put):
    tall = rows + 2 * PAD
    lane = lax.broadcasted_iota(jnp.int32, (tall, LANES), 1)
    tile = lambda t: d[:, (first_tile + t + 1) * LANES : (first_tile + t + 2) * LANES]
    tiles = {-1: tile(-1), 0: tile(0)}
    back = {t: pltpu.roll(tiles[t], 1, 1) for t in (-1, 0)}
    ahead = {0: pltpu.roll(tiles[0], LANES - 1, 1)}
    for t in range(count):
        tiles[t + 1] = tile(t + 1)
        back[t + 1] = pltpu.roll(tiles[t + 1], 1, 1)
        ahead[t + 1] = pltpu.roll(tiles[t + 1], LANES - 1, 1)
        before = jnp.where(lane == 0, back[t - 1], back[t])
        after = jnp.where(lane == LANES - 1, ahead[t + 1], ahead[t])
        across = after - before
        mid = slice(PAD, PAD + rows)
        up, down = pltpu.roll(tiles[t], 1, 0)[mid], pltpu.roll(tiles[t], tall - 1, 0)[mid]
        twice = 2.0 * tiles[t][mid]
        dxx = after[mid] + before[mid] - twice
        dyy = up + down - twice
        dxy = (pltpu.roll(across, tall - 1, 0)[mid] - pltpu.roll(across, 1, 0)[mid]) * 0.25
        put(first_tile + t, (gain * (dxx * dyy - dxy * dxy)).astype(BF16))


def pack_kernel(x_hbm, own_ref, up_ref, down_ref, x_ref, sem):
    copy = pltpu.make_async_copy(x_hbm, x_ref, sem)
    copy.start()
    copy.wait()
    rows, cols = x_ref.shape
    for at in range(0, cols, BLOCK):
        to = slice(at, at + BLOCK)
        pack(x_ref[:, to], to, own_ref, up_ref, down_ref)


def pack(value, to, own_ref, up_ref, down_ref):
    rows = value.shape[0]
    high, low = split(value)
    own_ref[:rows, to] = high
    own_ref[rows:, to] = low
    near = 2 * NEAR
    up_ref[: 2 * near, to] = high[: 2 * near]
    up_ref[2 * near :, to] = jnp.concatenate([low[:NEAR], high[2 * near : FAR]], axis=0)
    down_ref[:near, to] = high[rows - near :]
    down_ref[near:FAR, to] = high[rows - FAR : rows - near]
    down_ref[FAR:, to] = low[rows - NEAR :]


def side_kernel(side_ref, own_in, up_in, down_in, own_ref, up_ref, down_ref):
    cols = own_ref.shape[1] - LANES
    pack(side_ref[...], slice(cols, cols + LANES), own_ref, up_ref, down_ref)


def stage_kernel(*refs):
    count = (len(refs) - 1) // 2
    sems = refs[-1]
    copies = [pltpu.make_async_copy(refs[i], refs[count + i], sems.at[i]) for i in range(count)]
    for copy in copies:
        copy.start()
    for copy in copies:
        copy.wait()


def base_kernel(place_ref, own_ref, top_ref, bot_ref, bh_ref, bl_ref, dc_ref, dl_ref, de_ref,
                keep_ref, send_ref, bvh, bvl):
    row, col, coarse_height = place_ref[0], place_ref[1], place_ref[3]
    tile_rows = own_ref.shape[0] // 2
    cols = own_ref.shape[1] - LANES
    base_rows = bh_ref.shape[1]
    is_left = col == 0
    bh, bl = bh_ref[col], bl_ref[col]

    def rows_of(at, width):
        part = slice(at, at + width)
        stack = jnp.concatenate([own_ref[:, part], top_ref[:, part], bot_ref[:, part]], axis=0)
        return mm(bh, stack) + mm(bl, stack)

    for at in range(0, cols, BLOCK):
        to = slice(LANES + at, LANES + at + BLOCK)
        bvh[:, to], bvl[:, to] = split(rows_of(at, BLOCK))
    value = rows_of(cols, LANES)
    bvh[:, :LANES], bvl[:, :LANES] = split(jnp.where(is_left, 0.0, value))
    bvh[:, LANES + cols :], bvl[:, LANES + cols :] = split(jnp.where(is_left, value, 0.0))

    first_keep = row * (tile_rows // 2) - REACH - 1 + col * (tile_rows // 4)
    first_send = row * (tile_rows // 2) - REACH - 1 + (1 - col) * (tile_rows // 4)
    half = base_rows // 2
    index = lax.broadcasted_iota(jnp.int32, (base_rows, BLOCK), 0)
    place = jnp.where(index < half, first_keep + index, first_send + index - half)
    inside = (place >= 0) & (place < coarse_height)
    for j in range(cols // (2 * BLOCK)):
        at = LANES + 2 * BLOCK * j
        high = bvh[:, at : at + 2 * BLOCK]
        low = bvl[:, at : at + 2 * BLOCK]
        edge = edge_columns(bvh, bvl, at, 2 * BLOCK)
        value = mm(high, dc_ref[...]) + mm(low, dc_ref[...]) + mm(high, dl_ref[...]) + mm(edge, de_ref[...])
        value = jnp.where(inside, value, 0.0)
        keep_ref[:, j * BLOCK : (j + 1) * BLOCK] = value[:half]
        send_ref[:, j * BLOCK : (j + 1) * BLOCK] = value[half:]


def filter_columns(vh, vl, w_refs, group, rows, cols, lev, diffs, gains, dog_ref, hess_ref, seam, border):
    wc_ref, wl_ref, we_ref = w_refs
    tall = rows + 2 * PAD
    tiles = group * BLOCK // LANES
    for s in range(LEVELS):
        k = s - 1
        for g in range(0, cols // BLOCK, group):
            ats = [LANES + BLOCK * (g + i) for i in range(group)]
            high = jnp.concatenate([vh[s, :, at : at + BLOCK] for at in ats], axis=0)
            low = jnp.concatenate([vl[s, :, at : at + BLOCK] for at in ats], axis=0)
            edge = jnp.concatenate([edge_columns(vh.at[s], vl.at[s], at, BLOCK) for at in ats], axis=0)
            value = mm(high, wc_ref[s]) + mm(low, wc_ref[s]) + mm(high, wl_ref[s]) + mm(edge, we_ref[s])
            for i, at in enumerate(ats):
                new = value[i * tall : (i + 1) * tall]
                if s > 0:
                    d = new - lev[:, at : at + BLOCK]
                    dog_ref[k, :, at - LANES : at - LANES + BLOCK] = (gains[0] * d[PAD : PAD + rows]).astype(BF16)
                    if k in diffs:
                        diffs[k][:, at : at + BLOCK] = d
                if s + 1 < LEVELS:
                    lev[:, at : at + BLOCK] = new
            m = s - 3
            if m >= 0:

                def put(t, value):
                    hess_ref[m, :, t * LANES : (t + 1) * LANES] = value

                hess_tiles(diffs[m + 1], rows, g * BLOCK // LANES, tiles, gains[1], put)
        if s in (1, 2, 3):
            seam(s)
        if k in diffs:
            d = diffs[k]
            d[:PAD, :] = jnp.where(border[0], 0.0, d[:PAD, :])
            d[PAD + rows :, :] = jnp.where(border[1], 0.0, d[PAD + rows :, :])


def fine_kernel(place_ref, own_ref, top_ref, bot_ref, lh_ref, wc_ref, wl_ref, we_ref,
                dog_ref, hess_ref, vh, vl, lev, d1, d2):
    _, rows, cols = dog_ref.shape
    row, col, last_row = place_ref[0], place_ref[1], place_ref[2]
    tall = rows + 2 * PAD
    diffs = {1: d1, 2: d2}
    is_left = col == 0
    near = 2 * NEAR

    def rows_of(at, width):
        part = slice(at, at + width)
        own = own_ref[:, part]
        top_near, bot_near = top_ref[:near, part], bot_ref[:near, part]
        lows = jnp.concatenate([bot_ref[2 * near : FAR, part], top_ref[FAR:, part]], axis=0)
        again = jnp.concatenate([bot_near[:NEAR], top_near[NEAR:]], axis=0)
        stack = jnp.concatenate([own, own[:rows], top_near, bot_near, lows, again], axis=0)
        return mm(lh_ref[...], stack)

    for at in range(0, cols, BLOCK):
        value = rows_of(at, BLOCK)
        to = slice(LANES + at, LANES + at + BLOCK)
        for s in range(LEVELS):
            vh[s, :, to], vl[s, :, to] = split(value[s * tall : (s + 1) * tall])
    value = rows_of(cols, LANES)
    for s in range(LEVELS):
        part = value[s * tall : (s + 1) * tall]
        left = slice(0, LANES)
        right = slice(LANES + cols, 2 * LANES + cols)
        vh[s, :, left], vl[s, :, left] = split(jnp.where(is_left, 0.0, part))
        vh[s, :, right], vl[s, :, right] = split(jnp.where(is_left, part, 0.0))

    start = pl.multiple_of(jnp.where(is_left, cols, 0), LANES)

    def seam(s):
        high = vh[s, :, pl.ds(start, BLOCK)]
        low = vl[s, :, pl.ds(start, BLOCK)]
        new = mm(high, wc_ref[s]) + mm(low, wc_ref[s]) + mm(high, wl_ref[s])
        if s > 1:
            d = new - lev[:, cols + 2 * LANES :]
            diffs[s - 1][:, :LANES] = jnp.where(is_left, 0.0, d[:, :LANES])
            diffs[s - 1][:, cols + LANES :] = jnp.where(is_left, d[:, LANES:], 0.0)
        lev[:, cols + 2 * LANES :] = new

    filter_columns(vh, vl, (wc_ref, wl_ref, we_ref), 4, rows, cols, lev, diffs, (20.0, 5000.0),
                   dog_ref, hess_ref, seam, (row == 0, row == last_row))


def coarse_kernel(place_ref, keep_ref, other_ref, fine_dog_ref, fine_hess_ref, lh_ref, wc_ref, wl_ref, we_ref,
                  fine_dog_hbm, fine_hess_hbm, dog_hbm, hess_hbm,
                  dog_ref, hess_ref, vh, vl, lev, d1, d2, sems):
    fine_copies = [
        pltpu.make_async_copy(fine_dog_ref, fine_dog_hbm, sems.at[0]),
        pltpu.make_async_copy(fine_hess_ref, fine_hess_hbm, sems.at[1]),
    ]
    for copy in fine_copies:
        copy.start()
    _, rows, cols = dog_ref.shape
    row, col, last_row = place_ref[0], place_ref[1], place_ref[2]
    tall = rows + 2 * PAD
    diffs = {1: d1, 2: d2}
    is_left = col == 0
    half = cols // 2
    zero = jnp.zeros((tall, LANES), BF16)
    for s in range(LEVELS):
        for ref in (vh, vl):
            ref[s, :, :LANES] = zero
            ref[s, :, LANES + cols :] = zero
    zero = jnp.zeros((tall, LANES), F32)
    for d in (d1, d2):
        d[:, :LANES] = zero
        d[:, LANES + cols :] = zero

    for at in range(0, cols, BLOCK):
        source = slice(at % half, at % half + BLOCK)
        first = is_left if at < half else jnp.logical_not(is_left)
        high, low = split(jnp.where(first, keep_ref[:, source], other_ref[:, source]))
        stack = jnp.concatenate([high, low, high], axis=0)
        value = mm(lh_ref[...], stack)
        to = slice(LANES + at, LANES + at + BLOCK)
        for s in range(LEVELS):
            vh[s, :, to], vl[s, :, to] = split(value[s * tall : (s + 1) * tall])

    filter_columns(vh, vl, (wc_ref, wl_ref, we_ref), 8, rows, cols, lev, diffs, (80.0, 200000.0),
                   dog_ref, hess_ref, lambda s: None,
                   ((row == 0) & (col == 0), (row == last_row) & (col == 1)))
    copies = [
        pltpu.make_async_copy(dog_ref, dog_hbm, sems.at[2]),
        pltpu.make_async_copy(hess_ref, hess_hbm, sems.at[3]),
    ]
    for copy in copies:
        copy.start()
    for copy in fine_copies + copies:
        copy.wait()


def fine_constants(rows):
    near = 2 * NEAR
    own = np.arange(rows)
    top = np.concatenate([np.arange(-near, 0), np.arange(-FAR, -near)])
    bot = rows + np.arange(FAR)
    inputs = np.concatenate([own, own, top, np.arange(-NEAR, 0), bot[: 2 * near], bot[:NEAR], bot[2 * near :]])
    is_high = np.ones(inputs.shape)
    is_high[rows : 2 * rows] = 0
    is_high[2 * rows + FAR : 2 * rows + FAR + NEAR] = 0
    is_high[2 * rows + FAR + NEAR + 2 * near : 2 * rows + FAR + NEAR + FAR] = 0
    low_part = np.zeros(rows * 3 + 2 * near + 2 * near, bool)
    low_part[2 * rows : 3 * rows] = True
    low_part[3 * rows + 3 * near :] = True
    near_inputs = np.concatenate(
        [own, own, own, top[:near], bot[:near], bot[:NEAR], top[NEAR:near], bot[:NEAR], top[NEAR:near]]
    )

    def level_matrix(sigma, centres, valid):
        high, low = two_parts(row_matrix(sigma, centres, near_inputs) * valid[:, None])
        return np.where(low_part[None, :], low.astype(np.float32), high.astype(np.float32)).astype(BF16)

    def matrices(sigma, centres, valid):
        high, low = two_parts(row_matrix(sigma, centres, inputs) * valid[:, None])
        return high, (low.astype(np.float32) * is_high[None, :]).astype(BF16)

    centres = np.arange(-PAD, rows + PAD)
    valid = ((centres >= -1) & (centres <= rows)).astype(np.float32)
    level = [level_matrix(s, centres, valid) for s in SIGMAS]
    strip = rows // 4
    count = strip + 2 * (REACH + 1)
    padded = -(-count // 16) * 16
    ok = (np.arange(padded) < count).astype(np.float32)
    base = []
    for core in range(2):
        both = [2 * (c * strip - REACH - 1 + np.arange(padded)) for c in (core, 1 - core)]
        base.append(matrices(SIGMAS[-1], np.concatenate(both), np.concatenate([ok, ok])))
    return (
        np.concatenate(level),
        np.stack([a for a, _ in base]),
        np.stack([b for _, b in base]),
        padded,
    )


def coarse_constants(strip, padded):
    inputs = np.arange(padded) - REACH - 1
    centres = np.arange(-PAD, strip + PAD)
    valid = ((centres >= -1) & (centres <= strip)).astype(np.float32)
    parts = []
    for s in SIGMAS:
        high, low = two_parts(row_matrix(s, centres, inputs) * valid[:, None])
        parts.append(np.concatenate([high, high, low], axis=1))
    return np.concatenate(parts)


def vmem_specs(count):
    return [pl.BlockSpec(memory_space=pltpu.VMEM) for _ in range(count)]


def far_specs(count):
    return [pl.BlockSpec(memory_space=pltpu.HBM) for _ in range(count)]


def limit(mib):
    return pltpu.CompilerParams(vmem_limit_bytes=mib * 2**20)


def like(value):
    return jax.ShapeDtypeStruct(value.shape, value.dtype)


def local(image):
    rows, cols = image.shape
    row_count = lax.axis_size("row")
    row = lax.axis_index("row")
    col = lax.axis_index("col")
    strip = rows // 4
    wide = cols + LANES
    tall = rows + 2 * PAD
    small = strip + 2 * PAD
    lh, bh, bl, padded = fine_constants(rows)
    cw = coarse_constants(strip, padded)
    bands = [column_weights(s, 1) for s in SIGMAS]
    wc, wl, we = (np.stack([b[i] for b in bands]) for i in range(3))
    dc, dl, de = column_weights(SIGMAS[-1], 2)
    place = jnp.stack([row, col, jnp.int32(row_count - 1), jnp.int32(row_count * rows // 2)]).astype(jnp.int32)
    smem = pl.BlockSpec(memory_space=pltpu.SMEM)

    side = jnp.where(col == 0, image[:, cols - LANES :], image[:, :LANES])
    side = lax.ppermute(side, "col", [(0, 1), (1, 0)])
    packed = (
        jax.ShapeDtypeStruct((2 * rows, wide), BF16),
        jax.ShapeDtypeStruct((FAR + NEAR, wide), BF16),
        jax.ShapeDtypeStruct((FAR + NEAR, wide), BF16),
    )
    own, up, down = pl.pallas_call(
        pack_kernel,
        out_shape=packed,
        in_specs=far_specs(1),
        out_specs=tuple(vmem_specs(3)),
        scratch_shapes=[pltpu.VMEM((rows, cols), F32), pltpu.SemaphoreType.DMA],
        compiler_params=limit(4),
        name="pack",
    )(pltpu.with_memory_space_constraint(image, pltpu.HBM))
    own, up, down = pl.pallas_call(
        side_kernel,
        out_shape=packed,
        in_specs=vmem_specs(4),
        out_specs=tuple(vmem_specs(3)),
        input_output_aliases={1: 0, 2: 1, 3: 2},
        compiler_params=limit(4),
        name="side",
    )(side, own, up, down)
    bot = lax.ppermute(up, "row", [(i + 1, i) for i in range(row_count - 1)])
    top = lax.ppermute(down, "row", [(i, i + 1) for i in range(row_count - 1)])

    constants = [pltpu.with_memory_space_constraint(jnp.asarray(c), pltpu.HBM) for c in (lh, bh, bl, wc, wl, we, dc, dl, de, cw)]
    lh, bh, bl, wc, wl, we, dc, dl, de, cw = pl.pallas_call(
        stage_kernel,
        out_shape=tuple(like(c) for c in constants),
        in_specs=far_specs(len(constants)),
        out_specs=tuple(vmem_specs(len(constants))),
        scratch_shapes=[pltpu.SemaphoreType.DMA((len(constants),))],
        compiler_params=limit(8),
        name="stage",
    )(*constants)

    keep, send = pl.pallas_call(
        base_kernel,
        out_shape=(
            jax.ShapeDtypeStruct((padded, cols // 2), F32),
            jax.ShapeDtypeStruct((padded, cols // 2), F32),
        ),
        in_specs=[smem] + vmem_specs(8),
        out_specs=tuple(vmem_specs(2)),
        scratch_shapes=[
            pltpu.VMEM((2 * padded, cols + 2 * LANES), BF16),
            pltpu.VMEM((2 * padded, cols + 2 * LANES), BF16),
        ],
        compiler_params=limit(8),
        name="base",
    )(place, own, top, bot, bh, bl, dc, dl, de)
    other = lax.ppermute(send, "col", [(0, 1), (1, 0)])
    fine_shapes = (
        jax.ShapeDtypeStruct((4, rows, cols), BF16),
        jax.ShapeDtypeStruct((2, rows, cols), BF16),
    )
    coarse_shapes = (
        jax.ShapeDtypeStruct((4, strip, cols), BF16),
        jax.ShapeDtypeStruct((2, strip, cols), BF16),
    )
    dog_fine, hess_fine = pl.pallas_call(
        fine_kernel,
        out_shape=fine_shapes,
        in_specs=[smem] + vmem_specs(7),
        out_specs=tuple(vmem_specs(2)),
        scratch_shapes=[
            pltpu.VMEM((LEVELS, tall, cols + 2 * LANES), BF16),
            pltpu.VMEM((LEVELS, tall, cols + 2 * LANES), BF16),
            pltpu.VMEM((tall, cols + 2 * LANES + BLOCK), F32),
            pltpu.VMEM((tall, cols + 2 * LANES), F32),
            pltpu.VMEM((tall, cols + 2 * LANES), F32),
        ],
        compiler_params=limit(16),
        name="fine",
    )(place, own, top, bot, lh, wc, wl, we)

    return pl.pallas_call(
        coarse_kernel,
        out_shape=fine_shapes + coarse_shapes,
        in_specs=[smem] + vmem_specs(8),
        out_specs=tuple(far_specs(4)),
        scratch_shapes=[
            pltpu.VMEM((4, strip, cols), BF16),
            pltpu.VMEM((2, strip, cols), BF16),
            pltpu.VMEM((LEVELS, small, cols + 2 * LANES), BF16),
            pltpu.VMEM((LEVELS, small, cols + 2 * LANES), BF16),
            pltpu.VMEM((small, cols + 2 * LANES), F32),
            pltpu.VMEM((small, cols + 2 * LANES), F32),
            pltpu.VMEM((small, cols + 2 * LANES), F32),
            pltpu.SemaphoreType.DMA((4,)),
        ],
        compiler_params=limit(12),
        name="coarse",
    )(place, keep, other, dog_fine, hess_fine, cw, wc, wl, we)


def solution(mesh):
    return jax.shard_map(
        local,
        mesh=mesh,
        in_specs=(P(("slab", "row"), "col"),),
        out_specs=(
            P(None, ("slab", "row"), "col"),
            P(None, ("slab", "row"), "col"),
            P(None, ("slab", "row", "col"), None),
            P(None, ("slab", "row", "col"), None),
        ),
        check_vma=False,
    )
```

time: 38.2 us -> 27 us (0.71)
  Pallas kernels: 16.6 us -> 11.6 us
  waiting for transfers between devices: 9.85 us -> 6.12 us
  local copies, waits for them, and re-layouts: 1.97 us -> 0 us
  other arithmetic: 1.44 us -> 0.86 us
    pallas_call x3 -> x6, Pallas kernels: 16.6 us -> 11.6 us  [the longest x1 3.83 us: local(): pl.pallas_call(fine_kernel, out_shape=fine_shapes, in_specs=[smem] + vmem...]
    unnamed x8 -> x0, local copies, waits for them, and re-layouts: 1.97 us -> none
    ppermute x1, waiting for transfers between devices: 2.52 us -> 1.21 us  [local(): top = lax.ppermute(down, 'row', [(i, i + 1) for i in range(row_count - 1)])]
    ppermute x1, waiting for transfers between devices: 1.28 us -> 0.01 us  [local(): other = lax.ppermute(send, 'col', [(0, 1), (1, 0)])]
    ppermute x1, waiting for transfers between devices: 0.86 us -> 0.01 us  [local(): side = lax.ppermute(side, 'col', [(0, 1), (1, 0)])]
    another operation x1, other arithmetic: 0.66 us -> 0.08 us  [local(): jnp.stack([row, col, jnp.int32(row_count - 1), jnp.int32(row_count * rows...]
  transfers between devices with their start and end apart: 4 -> 4, of which waited for: 4 -> 2; matrix products, arithmetic and copies ran while one was open for 2% -> 0% of each run, Pallas kernels for 0% -> 26%
where the time goes in v2:
time: 27 us; the launch traced here: 26.7 us
  Pallas kernels  11.6 us (43%)
  starting transfers between devices  7.39 us (27%)
  waiting for transfers between devices  6.12 us (23%)
  other arithmetic  0.86 us (3%)
  between operations  0.71 us (3%)
    ppermute x1, waiting for transfers between devices, local(): bot = lax.ppermute(up, 'row', [(i + 1, i) for i in range(row_count - 1)])  4.9 us
    pallas_call x1, Pallas kernels, local(): pl.pallas_call(fine_kernel, out_shape=fine_shapes, in_specs=[smem] + vmem...  3.83 us
    ppermute x1, starting transfers between devices, local(): top = lax.ppermute(down, 'row', [(i, i + 1) for i in range(row_count - 1)])  3.15 us
    pallas_call x1, Pallas kernels, local(): pl.pallas_call(coarse_kernel, out_shape=fine_shapes + coarse_shapes, in_s...  3.07 us
    ppermute x1, starting transfers between devices, local(): bot = lax.ppermute(up, 'row', [(i + 1, i) for i in range(row_count - 1)])  3.03 us
    pallas_call x1, Pallas kernels, local(): pl.pallas_call(stage_kernel, out_shape=tuple((like(c) for c in constants)...  1.97 us
    pallas_call x1, Pallas kernels, local(): pl.pallas_call(base_kernel, out_shape=(jax.ShapeDtypeStruct((padded, cols...  1.62 us
    ppermute x1, waiting for transfers between devices, local(): top = lax.ppermute(down, 'row', [(i, i + 1) for i in range(row_count - 1)])  1.21 us
  transfers between devices with their start and end apart: 4, of which 2 were waited for; matrix products, arithmetic and copies ran while one was open for 0% of the time, Pallas kernels for 26%

profile of v2, /device:TPU:11, one launch (start us, length us, event | category | flops | bytes accessed | tf_op | source)
XLA Modules:
  0.0 26.7 jit_solution(6620895993285590741)
XLA Ops:
  0.6 0.8 %slice_select_fusion = f32[64,128]{1,0:T(8,128)S(1)} fusion(f32[64,2048]{1,0:T(8,128)} %x_hbm.1, pred[]{:T(512)S(6)} %eq.3), kind=kLoop, calls=%fused_computation | loop fusion | flops 8192 | bytes 98305 | tf_op jit(solution)/shard_map/jit(_where)/select_n | solution.py:398
  1.4 0.7 %collective-permute-start = (f32[64,128]{1,0:T(8,128)S(1)}, f32[64,128]{1,0:T(8,128)S(1)}, u32[]{:S(2)}, u32[]{:S(2)}) collective-permute-start(f32[64,128]{1,0:T(8,128)S(1)} %slice_select_fusion), channel_id=1, source_target_pairs={{0,1},{1,0},{2,3},{3,2},{4,5},{5,4},{6,7},{7,6},{8,9},{9,8},{10,11... | collective-permute-start | bytes 98312 | tf_op jit(solution)/shard_map/ppermute | solution.py:399
  2.1 1.1 %pack.1 = (bf16[128,2176]{1,0:T(8,128)(2,1)S(1)}, bf16[48,2176]{1,0:T(8,128)(2,1)S(1)}, bf16[48,2176]{1,0:T(8,128)(2,1)S(1)}) custom-call(f32[64,2048]{1,0:T(8,128)} %x_hbm.1), custom_call_target="tpu_custom_call" | custom-call | tf_op jit(solution)/shard_map/pack/pallas_call | solution.py:405
  3.2 0.0 collective-permute-done.side_ref
  3.3 3.1 %collective-permute-start.1 = (bf16[48,2176]{1,0:T(8,128)(2,1)S(1)}, bf16[48,2176]{1,0:T(8,128)(2,1)S(1)}, u32[]{:S(2)}, u32[]{:S(2)}) collective-permute-start(bf16[48,2176]{1,0:T(8,128)(2,1)S(1)} %get-tuple-element.28), channel_id=1, source_target_pairs={{0,2},{2,4},{4,6},{6,8},{8,10},{10,12},{12,14},{1,3},{3,5},{5,7},{... | collective-permute-start | bytes 626696 | tf_op jit(solution)/shard_map/ppermute | solution.py:424
  6.4 3.0 %collective-permute-start.2 = (bf16[48,2176]{1,0:T(8,128)(2,1)S(1)}, bf16[48,2176]{1,0:T(8,128)(2,1)S(1)}, u32[]{:S(2)}, u32[]{:S(2)}) collective-permute-start(bf16[48,2176]{1,0:T(8,128)(2,1)S(1)} %get-tuple-element.29), channel_id=1, source_target_pairs={{2,0},{4,2},{6,4},{8,6},{10,8},{12,10},{14,12},{3,1},{5,3},{7,5},{... | collective-permute-start | bytes 626696 | tf_op jit(solution)/shard_map/ppermute | solution.py:423
  9.5 2.0 %stage.1 = (bf16[400,256]{1,0:T(8,128)(2,1)S(1)}, bf16[2,96,224]{2,1,0:T(8,128)(2,1)S(1)}, bf16[2,96,224]{2,1,0:T(8,128)(2,1)S(1)}, bf16[5,256,256]{2,1,0:T(8,12...) custom-call(bf16[400,256]{1,0:T(8,128)(2,1)} %constant.34.clone.refs, ...), custom_call_target="tpu_custom_call" | custom-call | tf_op jit(solution)/shard_map/stage/pallas_call | solution.py:427
  11.4 0.1 pad_add_fusion.place_ref
  11.5 1.2 %collective-permute-done.1.top_ref = bf16[48,2176]{1,0:T(8,128)(2,1)S(1)} collective-permute-done((bf16[48,2176]{1,0:T(8,128)(2,1)S(1)}, bf16[48,2176]{1,0:T(8,128)(2,1)S(1)}, u32[]{:S(2)}, u32[]{:S(2)}) %collective-permute-start.1) | collective-permute-done | bytes 208928 | tf_op jit(solution)/shard_map/ppermute | solution.py:424
  12.7 4.9 %collective-permute-done.2.bot_ref = bf16[48,2176]{1,0:T(8,128)(2,1)S(1)} collective-permute-done((bf16[48,2176]{1,0:T(8,128)(2,1)S(1)}, bf16[48,2176]{1,0:T(8,128)(2,1)S(1)}, u32[]{:S(2)}, u32[]{:S(2)}) %collective-permute-start.2) | collective-permute-done | bytes 208928 | tf_op jit(solution)/shard_map/ppermute | solution.py:423
  17.6 1.6 %base.1 = (f32[48,1024]{1,0:T(8,128)S(1)}, f32[48,1024]{1,0:T(8,128)S(1)}) custom-call(s32[4]{0:T(128)S(1)} %pad_add_fusion.place_ref, bf16[128,2176]{1,0:T(8,128)(2,1)S(1)} %get-tuple-element.27.own_ref, bf16[48,2176]{1,0:T(8,128)(2,1)S(1)} %collective-permute-done.1.top_ref, bf16[48,2176]{1,0:T(8,128)(2,1)S(1)} %collective-permute-done.2.bot_ref, ...), custom_call_target="tpu_custom_call" | custom-call | tf_op jit(solution)/shard_map/base/pallas_call | solution.py:437
  19.3 0.5 %collective-permute-start.3 = (f32[48,1024]{1,0:T(8,128)S(1)}, f32[48,1024]{1,0:T(8,128)S(1)}, u32[]{:S(2)}, u32[]{:S(2)}) collective-permute-start(f32[48,1024]{1,0:T(8,128)S(1)} %get-tuple-element.36), channel_id=1, source_target_pairs={{0,1},{1,0},{2,3},{3,2},{4,5},{5,4},{6,7},{7,6},{8,9},{9,8},{10,11... | collective-permute-start | bytes 589832 | tf_op jit(solution)/shard_map/ppermute | solution.py:452
  19.8 3.8 %fine.1 = (bf16[4,64,2048]{2,1,0:T(8,128)(2,1)S(1)}, bf16[2,64,2048]{2,1,0:T(8,128)(2,1)S(1)}) custom-call(s32[4]{0:T(128)S(1)} %pad_add_fusion.place_ref, bf16[128,2176]{1,0:T(8,128)(2,1)S(1)} %get-tuple-element.27.own_ref, bf16[48,2176]{1,0:T(8,128)(2,1)S(1)} %collective-permute-done.1.top_ref, bf16[48,2176]{1,0:T(8,128)(2,1)S(1)} %collective-permute-done.2.bot_ref, ...), custom_call_target="tpu_custom_call" | custom-call | tf_op jit(solution)/shard_map/fine/pallas_call | solution.py:461
  23.6 0.0 collective-permute-done.3.other_ref
  23.6 3.1 %coarse.1 = (bf16[4,64,2048]{2,1,0:T(8,128)(2,1)}, bf16[2,64,2048]{2,1,0:T(8,128)(2,1)}, bf16[4,16,2048]{2,1,0:T(8,128)(2,1)}, bf16[2,16,2048]{2,1,0:T(8,128)(2,1)}) custom-call(s32[4]{0:T(128)S(1)} %pad_add_fusion.place_ref, f32[48,1024]{1,0:T(8,128)S(1)} %get-tuple-element.35.keep_ref, f32[48,1024]{1,0:T(8,128)S(1)} %collective-permute-done.3.other_ref, ...), custom_call_target="tpu_custom_call" | custom-call | tf_op jit(solution)/shard_map/coarse/pallas_call | solution.py:477
  (1 shorter events, 0.0 us)
Async XLA Ops:
  1.4 1.8 %collective-permute-start = (f32[64,128]{1,0:T(8,128)S(1)}, f32[64,128]{1,0:T(8,128)S(1)}, u32[]{:S(2)}, u32[]{:S(2)}) collective-permute-start(f32[64,128]{1,0:T(8,128)S(1)} %slice_select_fusion), channel_id=1, source_target_pairs={{0,1},{1,0},{2,3},{3,2},{4,5},{5,4},{6,7},{7,6},{8,9},{9,8},{10,11... | collective-permute-start | bytes 98312 | tf_op jit(solution)/shard_map/ppermute | solution.py:399
  3.3 9.5 %collective-permute-start.1 = (bf16[48,2176]{1,0:T(8,128)(2,1)S(1)}, bf16[48,2176]{1,0:T(8,128)(2,1)S(1)}, u32[]{:S(2)}, u32[]{:S(2)}) collective-permute-start(bf16[48,2176]{1,0:T(8,128)(2,1)S(1)} %get-tuple-element.28), channel_id=1, source_target_pairs={{0,2},{2,4},{4,6},{6,8},{8,10},{10,12},{12,14},{1,3},{3,5},{5,7},{... | collective-permute-start | bytes 626696 | tf_op jit(solution)/shard_map/ppermute | solution.py:424
  6.4 11.2 %collective-permute-start.2 = (bf16[48,2176]{1,0:T(8,128)(2,1)S(1)}, bf16[48,2176]{1,0:T(8,128)(2,1)S(1)}, u32[]{:S(2)}, u32[]{:S(2)}) collective-permute-start(bf16[48,2176]{1,0:T(8,128)(2,1)S(1)} %get-tuple-element.29), channel_id=1, source_target_pairs={{2,0},{4,2},{6,4},{8,6},{10,8},{12,10},{14,12},{3,1},{5,3},{7,5},{... | collective-permute-start | bytes 626696 | tf_op jit(solution)/shard_map/ppermute | solution.py:423
  19.3 4.4 %collective-permute-start.3 = (f32[48,1024]{1,0:T(8,128)S(1)}, f32[48,1024]{1,0:T(8,128)S(1)}, u32[]{:S(2)}, u32[]{:S(2)}) collective-permute-start(f32[48,1024]{1,0:T(8,128)S(1)} %get-tuple-element.36), channel_id=1, source_target_pairs={{0,1},{1,0},{2,3},{3,2},{4,5},{5,4},{6,7},{7,6},{8,9},{9,8},{10,11... | collective-permute-start | bytes 589832 | tf_op jit(solution)/shard_map/ppermute | solution.py:452

commit v3 on v2

--- a/solution.py
+++ b/solution.py
@@ -1,3 +1,5 @@
+import functools
+
 import jax
 import jax.numpy as jnp
 import numpy as np
@@ -12,8 +14,11 @@
 LANES = 128
 BLOCK = 256
 PAD = 8
-FAR = 40
-NEAR = 8
+NEAR = 16
+LOW = 4
+SPAN = 19
+PART = 10
+FINE = 4
 BF16 = jnp.bfloat16
 F32 = jnp.float32
 
@@ -100,32 +105,82 @@
         put(first_tile + t, (gain * (dxx * dyy - dxy * dxy)).astype(BF16))
 
 
-def pack_kernel(x_hbm, own_ref, up_ref, down_ref, x_ref, sem):
-    copy = pltpu.make_async_copy(x_hbm, x_ref, sem)
-    copy.start()
-    copy.wait()
+def mesh_place():
+    return lax.axis_index("row"), lax.axis_index("col")
+
+
+def pack_kernel(x_hbm, *refs):
+    count = (len(refs) - 3) // 2
+    far, own_ref, near, x_ref, sems = refs[:count], refs[count], refs[count + 1 : -2], refs[-2], refs[-1]
+    copies = [pltpu.make_async_copy(x_hbm, x_ref, sems.at[0])]
+    copies += [pltpu.make_async_copy(f, n, sems.at[i + 1]) for i, (f, n) in enumerate(zip(far, near))]
+    for copy in copies:
+        copy.start()
+    copies[0].wait()
     rows, cols = x_ref.shape
     for at in range(0, cols, BLOCK):
         to = slice(at, at + BLOCK)
-        pack(x_ref[:, to], to, own_ref, up_ref, down_ref)
-
-
-def pack(value, to, own_ref, up_ref, down_ref):
-    rows = value.shape[0]
-    high, low = split(value)
-    own_ref[:rows, to] = high
-    own_ref[rows:, to] = low
-    near = 2 * NEAR
-    up_ref[: 2 * near, to] = high[: 2 * near]
-    up_ref[2 * near :, to] = jnp.concatenate([low[:NEAR], high[2 * near : FAR]], axis=0)
-    down_ref[:near, to] = high[rows - near :]
-    down_ref[near:FAR, to] = high[rows - FAR : rows - near]
-    down_ref[FAR:, to] = low[rows - NEAR :]
-
-
-def side_kernel(side_ref, own_in, up_in, down_in, own_ref, up_ref, down_ref):
+        own_ref[:rows, to], own_ref[rows:, to] = split(x_ref[:, to])
+    for copy in copies[1:]:
+        copy.wait()
+
+
+def send_kernel(side_ref, own_in, bm_ref, dc_ref, dl_ref, de_ref,
+                own_ref, even_ref, odd_ref, base_ref, bvh, bvl):
+    row, col = mesh_place()
+    rows = own_ref.shape[0] // 2
     cols = own_ref.shape[1] - LANES
-    pack(side_ref[...], slice(cols, cols + LANES), own_ref, up_ref, down_ref)
+    is_left = col == 0
+    even = row % 2 == 0
+    own_ref[:rows, cols:], own_ref[rows:, cols:] = split(side_ref[...])
+
+    def rows_of(part):
+        own = own_ref[:, part]
+        return mm(bm_ref[...], jnp.concatenate([own, own[:rows]], axis=0))
+
+    for at in range(0, cols, BLOCK):
+        to = slice(LANES + at, LANES + at + BLOCK)
+        bvh[:, to], bvl[:, to] = split(rows_of(slice(at, at + BLOCK)))
+    value = rows_of(slice(cols, cols + LANES))
+    bvh[:, :LANES], bvl[:, :LANES] = split(jnp.where(is_left, 0.0, value))
+    bvh[:, LANES + cols :], bvl[:, LANES + cols :] = split(jnp.where(is_left, value, 0.0))
+    for j in range(cols // (2 * BLOCK)):
+        at = LANES + 2 * BLOCK * j
+        high = bvh[:, at : at + 2 * BLOCK]
+        low = bvl[:, at : at + 2 * BLOCK]
+        edge = edge_columns(bvh, bvl, at, 2 * BLOCK)
+        base_ref[:, j * BLOCK : (j + 1) * BLOCK] = (
+            mm(high, dc_ref[...]) + mm(low, dc_ref[...]) + mm(high, dl_ref[...]) + mm(edge, de_ref[...])
+        )
+
+    half = cols // 2
+    first_up = REACH + 1 - 6
+    first_down = REACH + 1 + SPAN
+    for at in range(0, cols + LANES, LANES):
+        to = slice(at, at + LANES)
+        up_near, down_near = own_ref[:NEAR, to].astype(F32), own_ref[rows - NEAR : rows, to].astype(F32)
+        up_low = own_ref[rows : rows + NEAR, to].astype(F32)[:LOW]
+        down_low = own_ref[2 * rows - NEAR :, to].astype(F32)[NEAR - LOW :]
+        if at < cols:
+            lanes = slice(at % half, at % half + LANES)
+            skip = PART * (at // half)
+            up_part = base_ref[first_up + skip : first_up + skip + PART, lanes]
+            down_part = base_ref[first_down + skip : first_down + skip + PART, lanes]
+            skip = FINE // 2 * (at // half)
+
+            def low_of(start):
+                value = base_ref[start + skip : start + skip + FINE // 2, lanes]
+                return value - value.astype(BF16).astype(F32)
+
+            up_fine = low_of(first_up + SPAN - 13)
+            down_fine = low_of(first_down + 13 - FINE)
+        else:
+            up_part = down_part = jnp.zeros((PART, LANES), F32)
+            up_fine = down_fine = jnp.zeros((FINE // 2, LANES), F32)
+        up = jnp.concatenate([up_near, up_low, up_fine, up_part], axis=0)
+        down = jnp.concatenate([down_near, down_part, down_fine, down_low], axis=0)
+        even_ref[:, to] = jnp.where(even, down, up).astype(BF16)
+        odd_ref[:, to] = jnp.where(even, up, down).astype(BF16)
 
 
 def stage_kernel(*refs):
@@ -138,42 +193,42 @@
         copy.wait()
 
 
-def base_kernel(place_ref, own_ref, top_ref, bot_ref, bh_ref, bl_ref, dc_ref, dl_ref, de_ref,
-                keep_ref, send_ref, bvh, bvl):
-    row, col, coarse_height = place_ref[0], place_ref[1], place_ref[3]
-    tile_rows = own_ref.shape[0] // 2
-    cols = own_ref.shape[1] - LANES
-    base_rows = bh_ref.shape[1]
+def base_kernel(row_count, tile_base, base_ref, even_ref, odd_ref, _, keep_ref, send_ref, sum_ref):
+    row, col = mesh_place()
+    base_rows, half = base_ref.shape
+    count = keep_ref.shape[0]
+    shift = tile_base // 2
+    even = row % 2 == 0
     is_left = col == 0
-    bh, bl = bh_ref[col], bl_ref[col]
-
-    def rows_of(at, width):
-        part = slice(at, at + width)
-        stack = jnp.concatenate([own_ref[:, part], top_ref[:, part], bot_ref[:, part]], axis=0)
-        return mm(bh, stack) + mm(bl, stack)
-
-    for at in range(0, cols, BLOCK):
-        to = slice(LANES + at, LANES + at + BLOCK)
-        bvh[:, to], bvl[:, to] = split(rows_of(at, BLOCK))
-    value = rows_of(cols, LANES)
-    bvh[:, :LANES], bvl[:, :LANES] = split(jnp.where(is_left, 0.0, value))
-    bvh[:, LANES + cols :], bvl[:, LANES + cols :] = split(jnp.where(is_left, value, 0.0))
-
-    first_keep = row * (tile_rows // 2) - REACH - 1 + col * (tile_rows // 4)
-    first_send = row * (tile_rows // 2) - REACH - 1 + (1 - col) * (tile_rows // 4)
-    half = base_rows // 2
-    index = lax.broadcasted_iota(jnp.int32, (base_rows, BLOCK), 0)
-    place = jnp.where(index < half, first_keep + index, first_send + index - half)
-    inside = (place >= 0) & (place < coarse_height)
-    for j in range(cols // (2 * BLOCK)):
-        at = LANES + 2 * BLOCK * j
-        high = bvh[:, at : at + 2 * BLOCK]
-        low = bvl[:, at : at + 2 * BLOCK]
-        edge = edge_columns(bvh, bvl, at, 2 * BLOCK)
-        value = mm(high, dc_ref[...]) + mm(low, dc_ref[...]) + mm(high, dl_ref[...]) + mm(edge, de_ref[...])
-        value = jnp.where(inside, value, 0.0)
-        keep_ref[:, j * BLOCK : (j + 1) * BLOCK] = value[:half]
-        send_ref[:, j * BLOCK : (j + 1) * BLOCK] = value[half:]
+    index = lax.broadcasted_iota(jnp.int32, (base_rows, LANES), 0)
+    place = row * tile_base - REACH - 1 + index
+    inside = (place >= 0) & (place < row_count * tile_base)
+    first_bot = tile_base + REACH + 1 - 6
+    for at in range(0, half, LANES):
+        def message(ref_a, ref_b):
+            both = []
+            for lanes in (slice(at, at + LANES), slice(half + at, half + at + LANES)):
+                a, b = ref_a[NEAR:, lanes].astype(F32), ref_b[NEAR:, lanes].astype(F32)
+                both.append(jnp.where(even, a, b))
+            return both
+
+        to = slice(at, at + LANES)
+        left, right = message(odd_ref, even_ref)
+        top = jnp.concatenate([left[:PART], right[: SPAN - PART]], axis=0)
+        top_fine = jnp.concatenate([left[PART : PART + FINE // 2], right[PART : PART + FINE // 2]], axis=0)
+        left, right = message(even_ref, odd_ref)
+        skip = LOW + FINE // 2
+        bot = jnp.concatenate([left[skip:], right[skip : skip + SPAN - PART]], axis=0)
+        bot_fine = jnp.concatenate([left[LOW:skip], right[LOW:skip]], axis=0)
+        sum_ref[...] = base_ref[:, to]
+        sum_ref[:SPAN, :] += top
+        sum_ref[13 - FINE : 13, :] += top_fine
+        sum_ref[first_bot : first_bot + SPAN, :] += bot
+        first_fine = first_bot + SPAN - 13
+        sum_ref[first_fine : first_fine + FINE, :] += bot_fine
+        total = jnp.where(inside, sum_ref[...], 0.0)
+        keep_ref[:, to] = jnp.where(is_left, total[:count], total[shift : shift + count])
+        send_ref[:, to] = jnp.where(is_left, total[shift : shift + count], total[:count])
 
 
 def filter_columns(vh, vl, w_refs, group, rows, cols, lev, diffs, gains, dog_ref, hess_ref, seam, border):
@@ -212,22 +267,23 @@
             d[PAD + rows :, :] = jnp.where(border[1], 0.0, d[PAD + rows :, :])
 
 
-def fine_kernel(place_ref, own_ref, top_ref, bot_ref, lh_ref, wc_ref, wl_ref, we_ref,
+def fine_kernel(last_row, own_ref, even_ref, odd_ref, lh_ref, wc_ref, wl_ref, we_ref,
                 dog_ref, hess_ref, vh, vl, lev, d1, d2):
     _, rows, cols = dog_ref.shape
-    row, col, last_row = place_ref[0], place_ref[1], place_ref[2]
+    row, col = mesh_place()
     tall = rows + 2 * PAD
     diffs = {1: d1, 2: d2}
     is_left = col == 0
-    near = 2 * NEAR
+    even = row % 2 == 0
 
     def rows_of(at, width):
         part = slice(at, at + width)
         own = own_ref[:, part]
-        top_near, bot_near = top_ref[:near, part], bot_ref[:near, part]
-        lows = jnp.concatenate([bot_ref[2 * near : FAR, part], top_ref[FAR:, part]], axis=0)
-        again = jnp.concatenate([bot_near[:NEAR], top_near[NEAR:]], axis=0)
-        stack = jnp.concatenate([own, own[:rows], top_near, bot_near, lows, again], axis=0)
+        a, b = even_ref[:, part], odd_ref[:, part]
+        bot, top = jnp.where(even, a, b), jnp.where(even, b, a)
+        lows = jnp.concatenate([bot[NEAR : NEAR + 8], top[NEAR + 8 :]], axis=0)
+        again = jnp.concatenate([bot[:8], top[8:NEAR]], axis=0)
+        stack = jnp.concatenate([own, own[:rows], top[:NEAR], bot[:NEAR], lows, again], axis=0)
         return mm(lh_ref[...], stack)
 
     for at in range(0, cols, BLOCK):
@@ -259,7 +315,7 @@
                    dog_ref, hess_ref, seam, (row == 0, row == last_row))
 
 
-def coarse_kernel(place_ref, keep_ref, other_ref, fine_dog_ref, fine_hess_ref, lh_ref, wc_ref, wl_ref, we_ref,
+def coarse_kernel(last_row, keep_ref, other_ref, fine_dog_ref, fine_hess_ref, lh_ref, wc_ref, wl_ref, we_ref,
                   fine_dog_hbm, fine_hess_hbm, dog_hbm, hess_hbm,
                   dog_ref, hess_ref, vh, vl, lev, d1, d2, sems):
     fine_copies = [
@@ -269,7 +325,7 @@
     for copy in fine_copies:
         copy.start()
     _, rows, cols = dog_ref.shape
-    row, col, last_row = place_ref[0], place_ref[1], place_ref[2]
+    row, col = mesh_place()
     tall = rows + 2 * PAD
     diffs = {1: d1, 2: d2}
     is_left = col == 0
@@ -308,47 +364,32 @@
 
 
 def fine_constants(rows):
-    near = 2 * NEAR
     own = np.arange(rows)
-    top = np.concatenate([np.arange(-near, 0), np.arange(-FAR, -near)])
-    bot = rows + np.arange(FAR)
-    inputs = np.concatenate([own, own, top, np.arange(-NEAR, 0), bot[: 2 * near], bot[:NEAR], bot[2 * near :]])
-    is_high = np.ones(inputs.shape)
-    is_high[rows : 2 * rows] = 0
-    is_high[2 * rows + FAR : 2 * rows + FAR + NEAR] = 0
-    is_high[2 * rows + FAR + NEAR + 2 * near : 2 * rows + FAR + NEAR + FAR] = 0
-    low_part = np.zeros(rows * 3 + 2 * near + 2 * near, bool)
-    low_part[2 * rows : 3 * rows] = True
-    low_part[3 * rows + 3 * near :] = True
-    near_inputs = np.concatenate(
-        [own, own, own, top[:near], bot[:near], bot[:NEAR], top[NEAR:near], bot[:NEAR], top[NEAR:near]]
-    )
-
-    def level_matrix(sigma, centres, valid):
-        high, low = two_parts(row_matrix(sigma, centres, near_inputs) * valid[:, None])
-        return np.where(low_part[None, :], low.astype(np.float32), high.astype(np.float32)).astype(BF16)
-
-    def matrices(sigma, centres, valid):
+    top, bot = np.arange(-NEAR, 0), rows + np.arange(NEAR)
+    nowhere = -1000
+    lows = np.full(NEAR, nowhere)
+    lows[:LOW] = bot[:LOW]
+    lows[NEAR - LOW :] = top[NEAR - LOW :]
+    again = np.concatenate([bot[:8], top[8:]])
+    inputs = np.concatenate([own, own, own, top, bot, lows, again])
+    use_low = np.zeros(inputs.shape, bool)
+    use_low[2 * rows : 3 * rows] = True
+    use_low[-NEAR:] = True
+
+    def matrix(sigma, centres, valid, inputs, use_low):
         high, low = two_parts(row_matrix(sigma, centres, inputs) * valid[:, None])
-        return high, (low.astype(np.float32) * is_high[None, :]).astype(BF16)
+        return np.where(use_low[None, :], low.astype(np.float32), high.astype(np.float32)).astype(BF16)
 
     centres = np.arange(-PAD, rows + PAD)
     valid = ((centres >= -1) & (centres <= rows)).astype(np.float32)
-    level = [level_matrix(s, centres, valid) for s in SIGMAS]
-    strip = rows // 4
-    count = strip + 2 * (REACH + 1)
-    padded = -(-count // 16) * 16
-    ok = (np.arange(padded) < count).astype(np.float32)
-    base = []
-    for core in range(2):
-        both = [2 * (c * strip - REACH - 1 + np.arange(padded)) for c in (core, 1 - core)]
-        base.append(matrices(SIGMAS[-1], np.concatenate(both), np.concatenate([ok, ok])))
-    return (
-        np.concatenate(level),
-        np.stack([a for a, _ in base]),
-        np.stack([b for _, b in base]),
-        padded,
+    level = [matrix(s, centres, valid, inputs, use_low) for s in SIGMAS]
+    count = rows // 2 + 2 * (REACH + 1)
+    index = np.arange(-(-count // 8) * 8)
+    base = matrix(
+        SIGMAS[-1], 2 * (index - REACH - 1), (index < count).astype(np.float32), inputs[: 3 * rows], use_low[: 3 * rows]
     )
+    strip_rows = -(-(rows // 4 + 2 * (REACH + 1)) // 16) * 16
+    return np.concatenate(level), base, strip_rows
 
 
 def coarse_constants(strip, padded):
@@ -378,77 +419,86 @@
     return jax.ShapeDtypeStruct(value.shape, value.dtype)
 
 
+def far(value):
+    return pltpu.with_memory_space_constraint(jnp.asarray(value), pltpu.HBM)
+
+
 def local(image):
     rows, cols = image.shape
     row_count = lax.axis_size("row")
-    row = lax.axis_index("row")
     col = lax.axis_index("col")
     strip = rows // 4
     wide = cols + LANES
     tall = rows + 2 * PAD
     small = strip + 2 * PAD
-    lh, bh, bl, padded = fine_constants(rows)
-    cw = coarse_constants(strip, padded)
+    lh, bm, strip_rows = fine_constants(rows)
+    cw = coarse_constants(strip, strip_rows)
     bands = [column_weights(s, 1) for s in SIGMAS]
     wc, wl, we = (np.stack([b[i] for b in bands]) for i in range(3))
-    dc, dl, de = column_weights(SIGMAS[-1], 2)
-    place = jnp.stack([row, col, jnp.int32(row_count - 1), jnp.int32(row_count * rows // 2)]).astype(jnp.int32)
-    smem = pl.BlockSpec(memory_space=pltpu.SMEM)
+    early = [far(c) for c in (bm, *column_weights(SIGMAS[-1], 2))]
+    late = [far(c) for c in (lh, wc, wl, we, cw)]
 
     side = jnp.where(col == 0, image[:, cols - LANES :], image[:, :LANES])
     side = lax.ppermute(side, "col", [(0, 1), (1, 0)])
-    packed = (
-        jax.ShapeDtypeStruct((2 * rows, wide), BF16),
-        jax.ShapeDtypeStruct((FAR + NEAR, wide), BF16),
-        jax.ShapeDtypeStruct((FAR + NEAR, wide), BF16),
-    )
-    own, up, down = pl.pallas_call(
+    own, bm, dc, dl, de = pl.pallas_call(
         pack_kernel,
-        out_shape=packed,
-        in_specs=far_specs(1),
-        out_specs=tuple(vmem_specs(3)),
-        scratch_shapes=[pltpu.VMEM((rows, cols), F32), pltpu.SemaphoreType.DMA],
+        out_shape=(jax.ShapeDtypeStruct((2 * rows, wide), BF16), *(like(c) for c in early)),
+        in_specs=far_specs(1 + len(early)),
+        out_specs=tuple(vmem_specs(1 + len(early))),
+        scratch_shapes=[pltpu.VMEM((rows, cols), F32), pltpu.SemaphoreType.DMA((1 + len(early),))],
         compiler_params=limit(4),
         name="pack",
-    )(pltpu.with_memory_space_constraint(image, pltpu.HBM))
-    own, up, down = pl.pallas_call(
-        side_kernel,
-        out_shape=packed,
-        in_specs=vmem_specs(4),
-        out_specs=tuple(vmem_specs(3)),
-        input_output_aliases={1: 0, 2: 1, 3: 2},
+    )(far(image), *early)
+    message = jax.ShapeDtypeStruct((2 * NEAR, wide), BF16)
+    base_rows = bm.shape[0]
+    own, to_even, to_odd, base = pl.pallas_call(
+        send_kernel,
+        out_shape=(
+            jax.ShapeDtypeStruct((2 * rows, wide), BF16),
+            message,
+            message,
+            jax.ShapeDtypeStruct((base_rows, cols // 2), F32),
+        ),
+        in_specs=vmem_specs(6),
+        out_specs=tuple(vmem_specs(4)),
+        scratch_shapes=[
+            pltpu.VMEM((base_rows, cols + 2 * LANES), BF16),
+            pltpu.VMEM((base_rows, cols + 2 * LANES), BF16),
+        ],
+        input_output_aliases={1: 0},
+        compiler_params=limit(6),
+        name="send",
+    )(side, own, bm, dc, dl, de)
+
+    def swap(value, first):
+        pairs = [(i, i + 1) for i in range(first, row_count - 1, 2)]
+        return lax.ppermute(value, "row", pairs + [(j, i) for i, j in pairs])
+
+    even, odd = swap(to_even, 0), swap(to_odd, 1)
+
+    lh, wc, wl, we, cw = pl.pallas_call(
+        stage_kernel,
+        out_shape=tuple(like(c) for c in late),
+        in_specs=far_specs(len(late)),
+        out_specs=tuple(vmem_specs(len(late))),
+        scratch_shapes=[pltpu.SemaphoreType.DMA((len(late),))],
+        compiler_params=limit(6),
+        cost_estimate=pl.CostEstimate(flops=10**8, bytes_accessed=10**7, transcendentals=0),
+        name="stage",
+    )(*late)
+
+    keep, send = pl.pallas_call(
+        functools.partial(base_kernel, row_count, rows // 2),
+        out_shape=(
+            jax.ShapeDtypeStruct((strip_rows, cols // 2), F32),
+            jax.ShapeDtypeStruct((strip_rows, cols // 2), F32),
+        ),
+        in_specs=vmem_specs(3) + [pl.BlockSpec(memory_space=pl.ANY)],
+        out_specs=tuple(vmem_specs(2)),
+        scratch_shapes=[pltpu.VMEM((base_rows, LANES), F32)],
         compiler_params=limit(4),
-        name="side",
-    )(side, own, up, down)
-    bot = lax.ppermute(up, "row", [(i + 1, i) for i in range(row_count - 1)])
-    top = lax.ppermute(down, "row", [(i, i + 1) for i in range(row_count - 1)])
-
-    constants = [pltpu.with_memory_space_constraint(jnp.asarray(c), pltpu.HBM) for c in (lh, bh, bl, wc, wl, we, dc, dl, de, cw)]
-    lh, bh, bl, wc, wl, we, dc, dl, de, cw = pl.pallas_call(
-        stage_kernel,
-        out_shape=tuple(like(c) for c in constants),
-        in_specs=far_specs(len(constants)),
-        out_specs=tuple(vmem_specs(len(constants))),
-        scratch_shapes=[pltpu.SemaphoreType.DMA((len(constants),))],
-        compiler_params=limit(8),
-        name="stage",
-    )(*constants)
-
-    keep, send = pl.pallas_call(
-        base_kernel,
-        out_shape=(
-            jax.ShapeDtypeStruct((padded, cols // 2), F32),
-            jax.ShapeDtypeStruct((padded, cols // 2), F32),
-        ),
-        in_specs=[smem] + vmem_specs(8),
-        out_specs=tuple(vmem_specs(2)),
-        scratch_shapes=[
-            pltpu.VMEM((2 * padded, cols + 2 * LANES), BF16),
-            pltpu.VMEM((2 * padded, cols + 2 * LANES), BF16),
-        ],
-        compiler_params=limit(8),
         name="base",
-    )(place, own, top, bot, bh, bl, dc, dl, de)
+    )(base, even, odd, cw)
     other = lax.ppermute(send, "col", [(0, 1), (1, 0)])
     fine_shapes = (
         jax.ShapeDtypeStruct((4, rows, cols), BF16),
@@ -459,9 +509,9 @@
         jax.ShapeDtypeStruct((2, strip, cols), BF16),
     )
     dog_fine, hess_fine = pl.pallas_call(
-        fine_kernel,
+        functools.partial(fine_kernel, row_count - 1),
         out_shape=fine_shapes,
-        in_specs=[smem] + vmem_specs(7),
+        in_specs=vmem_specs(7),
         out_specs=tuple(vmem_specs(2)),
         scratch_shapes=[
             pltpu.VMEM((LEVELS, tall, cols + 2 * LANES), BF16),
@@ -472,12 +522,12 @@
         ],
         compiler_params=limit(16),
         name="fine",
-    )(place, own, top, bot, lh, wc, wl, we)
+    )(own, even, odd, lh, wc, wl, we)
 
     return pl.pallas_call(
-        coarse_kernel,
+        functools.partial(coarse_kernel, row_count - 1),
         out_shape=fine_shapes + coarse_shapes,
-        in_specs=[smem] + vmem_specs(8),
+        in_specs=vmem_specs(8),
         out_specs=tuple(far_specs(4)),
         scratch_shapes=[
             pltpu.VMEM((4, strip, cols), BF16),
@@ -491,7 +541,7 @@
         ],
         compiler_params=limit(12),
         name="coarse",
-    )(place, keep, other, dog_fine, hess_fine, cw, wc, wl, we)
+    )(keep, other, dog_fine, hess_fine, cw, wc, wl, we)
 
 
 def solution(mesh):

time: 27 us -> 20.9 us (0.77)
  starting transfers between devices: 7.39 us -> 5.19 us
  waiting for transfers between devices: 6.12 us -> 4.06 us
  Pallas kernels: 11.6 us -> 9.89 us
    ppermute x2, starting transfers between devices: 6.18 us -> 3.31 us  [swap(): return lax.ppermute(value, 'row', pairs + [(j, i) for i, j in pairs])]
    ppermute x2, waiting for transfers between devices: 6.11 us -> 4.06 us  [swap(): return lax.ppermute(value, 'row', pairs + [(j, i) for i, j in pairs])]
    pallas_call x6, Pallas kernels: 11.6 us -> 9.89 us  [the longest x1 3.32 us: local(): pl.pallas_call(functools.partial(fine_kernel, row_count - 1), out_shape=f...]
    ppermute x1, starting transfers between devices: 0.54 us -> 1.2 us  [local(): other = lax.ppermute(send, 'col', [(0, 1), (1, 0)])]
  transfers between devices with their start and end apart: 4 -> 4, of which waited for: 2 -> 2; matrix products, arithmetic and copies ran while one was open for 0% -> 0% of each run, Pallas kernels for 26% -> 30%
where the time goes in v3:
time: 20.9 us; the launch traced here: 20.6 us
  Pallas kernels  9.89 us (47%)
  starting transfers between devices  5.19 us (25%)
  waiting for transfers between devices  4.06 us (19%)
  other arithmetic  0.78 us (4%)
  between operations  0.69 us (3%)
    ppermute x2, waiting for transfers between devices, swap(): return lax.ppermute(value, 'row', pairs + [(j, i) for i, j in pairs])  4.06 us
    pallas_call x1, Pallas kernels, local(): pl.pallas_call(functools.partial(fine_kernel, row_count - 1), out_shape=f...  3.32 us
    ppermute x2, starting transfers between devices, swap(): return lax.ppermute(value, 'row', pairs + [(j, i) for i, j in pairs])  3.31 us
    pallas_call x1, Pallas kernels, local(): pl.pallas_call(functools.partial(coarse_kernel, row_count - 1), out_shape...  2.54 us
    pallas_call x1, Pallas kernels, local(): pl.pallas_call(stage_kernel, out_shape=tuple((like(c) for c in late)), in...  1.64 us
    pallas_call x1, Pallas kernels, local(): pl.pallas_call(pack_kernel, out_shape=(jax.ShapeDtypeStruct((2 * rows, wi...  1.28 us
    ppermute x1, starting transfers between devices, local(): other = lax.ppermute(send, 'col', [(0, 1), (1, 0)])  1.2 us
    pallas_call x1, Pallas kernels, local(): pl.pallas_call(send_kernel, out_shape=(jax.ShapeDtypeStruct((2 * rows, wi...  0.92 us
  transfers between devices with their start and end apart: 4, of which 2 were waited for; matrix products, arithmetic and copies ran while one was open for 0% of the time, Pallas kernels for 30%

profile of v3, /device:TPU:11, one launch (start us, length us, event | category | flops | bytes accessed | tf_op | source)
XLA Modules:
  0.0 20.6 jit_solution(16314543851665273077)
XLA Ops:
  0.6 0.8 %slice_select_fusion = f32[64,128]{1,0:T(8,128)S(1)} fusion(f32[64,2048]{1,0:T(8,128)} %x_hbm.1, pred[]{:T(512)S(6)} %eq.3), kind=kLoop, calls=%fused_computation | loop fusion | flops 8192 | bytes 98305 | tf_op jit(solution)/shard_map/jit(_where)/select_n | solution.py:441
  1.4 0.7 %collective-permute-start = (f32[64,128]{1,0:T(8,128)S(1)}, f32[64,128]{1,0:T(8,128)S(1)}, u32[]{:S(2)}, u32[]{:S(2)}) collective-permute-start(f32[64,128]{1,0:T(8,128)S(1)} %slice_select_fusion), channel_id=1, source_target_pairs={{0,1},{1,0},{2,3},{3,2},{4,5},{5,4},{6,7},{7,6},{8,9},{9,8},{10,11... | collective-permute-start | bytes 98312 | tf_op jit(solution)/shard_map/ppermute | solution.py:442
  2.1 1.3 %pack.1 = (bf16[128,2176]{1,0:T(8,128)(2,1)S(1)}, bf16[64,192]{1,0:T(8,128)(2,1)S(1)}, bf16[512,256]{1,0:T(8,128)(2,1)S(1)}, bf16[512,256]{1,0:T(8,128)(2,1)S(1)}, bf16[256,256]{1,0:T(8,128)(2,1)S(1)}) custom-call(f32[64,2048]{1,0:T(8,128)} %x_hbm.1, bf16[64,192]{1,0:T(8,128)(2,1)} %constant.24.clone.refs_0_, bf16[512,256]{1,0:T(8,128)(2,1)} %constant.25.clone.refs_1_, ...), custom_call_target="tpu_custom_call" | custom-call | tf_op jit(solution)/shard_map/pack/pallas_call | solution.py:443
  3.4 0.0 collective-permute-done.side_ref
  3.4 0.9 %send.1 = (bf16[128,2176]{1,0:T(8,128)(2,1)S(1)}, bf16[32,2176]{1,0:T(8,128)(2,1)S(1)}, bf16[32,2176]{1,0:T(8,128)(2,1)S(1)}, f32[64,1024]{1,0:T(8,128)S(1)}) custom-call(f32[64,128]{1,0:T(8,128)S(1)} %collective-permute-done.side_ref, bf16[128,2176]{1,0:T(8,128)(2,1)S(1)} %get-tuple-element.22.own_in, ...), custom_call_target="tpu_custom_call", output_to_operand_aliasing={{0}: (1, {})} | custom-call | tf_op jit(solution)/shard_map/send/pallas_call | solution.py:454
  4.3 1.3 %collective-permute-start.1 = (bf16[32,2176]{1,0:T(8,128)(2,1)S(1)}, bf16[32,2176]{1,0:T(8,128)(2,1)S(1)}, u32[]{:S(2)}, u32[]{:S(2)}) collective-permute-start(bf16[32,2176]{1,0:T(8,128)(2,1)S(1)} %get-tuple-element.28), channel_id=1, source_target_pairs={{0,2},{4,6},{8,10},{12,14},{2,0},{6,4},{10,8},{14,12},{1,3},{5,7},... | collective-permute-start | bytes 417800 | tf_op jit(solution)/shard_map/ppermute | solution.py:475
  5.6 2.0 %collective-permute-start.2 = (bf16[32,2176]{1,0:T(8,128)(2,1)S(1)}, bf16[32,2176]{1,0:T(8,128)(2,1)S(1)}, u32[]{:S(2)}, u32[]{:S(2)}) collective-permute-start(bf16[32,2176]{1,0:T(8,128)(2,1)S(1)} %get-tuple-element.29), channel_id=1, source_target_pairs={{2,4},{6,8},{10,12},{4,2},{8,6},{12,10},{3,5},{7,9},{11,13},{5,3},... | collective-permute-start | bytes 417800 | tf_op jit(solution)/shard_map/ppermute | solution.py:475
  7.6 1.6 %stage.1 = (bf16[400,256]{1,0:T(8,128)(2,1)S(1)}, bf16[5,256,256]{2,1,0:T(8,128)(2,1)S(1)}, bf16[5,256,256]{2,1,0:T(8,128)(2,1)S(1)}, bf16[5,256,256]{2,1,0:T(8,128)(2,1)S(1)}, bf16[160,144]{1,0:T(8,128)(2,1)S(1)}) custom-call(bf16[400,256]{1,0:T(8,128)(2,1)} %constant.28.clone.refs_0_, bf16[5,256,256]{2,1,0:T(8,128)(2,1)} %constant.29.clone.refs_1_, ...), custom_call_target="tpu_custom_call" | custom-call | flops 100000000 | bytes 10000000 | tf_op jit(solution)/shard_map/stage/pallas_call | solution.py:479
  9.3 0.3 %collective-permute-done.1.even_ref = bf16[32,2176]{1,0:T(8,128)(2,1)S(1)} collective-permute-done((bf16[32,2176]{1,0:T(8,128)(2,1)S(1)}, bf16[32,2176]{1,0:T(8,128)(2,1)S(1)}, u32[]{:S(2)}, u32[]{:S(2)}) %collective-permute-start.1) | collective-permute-done | bytes 139296 | tf_op jit(solution)/shard_map/ppermute | solution.py:475
  9.6 3.7 %collective-permute-done.2.odd_ref = bf16[32,2176]{1,0:T(8,128)(2,1)S(1)} collective-permute-done((bf16[32,2176]{1,0:T(8,128)(2,1)S(1)}, bf16[32,2176]{1,0:T(8,128)(2,1)S(1)}, u32[]{:S(2)}, u32[]{:S(2)}) %collective-permute-start.2) | collective-permute-done | bytes 139296 | tf_op jit(solution)/shard_map/ppermute | solution.py:475
  13.4 0.2 base.1
  13.5 1.2 %collective-permute-start.3 = (f32[48,1024]{1,0:T(8,128)S(1)}, f32[48,1024]{1,0:T(8,128)S(1)}, u32[]{:S(2)}, u32[]{:S(2)}) collective-permute-start(f32[48,1024]{1,0:T(8,128)S(1)} %get-tuple-element.32), channel_id=1, source_target_pairs={{0,1},{1,0},{2,3},{3,2},{4,5},{5,4},{6,7},{7,6},{8,9},{9,8},{10,11... | collective-permute-start | bytes 589832 | tf_op jit(solution)/shard_map/ppermute | solution.py:502
  14.7 3.3 %fine.1 = (bf16[4,64,2048]{2,1,0:T(8,128)(2,1)S(1)}, bf16[2,64,2048]{2,1,0:T(8,128)(2,1)S(1)}) custom-call(bf16[128,2176]{1,0:T(8,128)(2,1)S(1)} %get-tuple-element.33.own_ref, bf16[32,2176]{1,0:T(8,128)(2,1)S(1)} %collective-permute-done.1.even_ref, bf16[32,2176]{1,0:T(8,128)(2,1)S(1)} %collective-permute-done.2.odd_ref, ...), custom_call_target="tpu_custom_call" | custom-call | tf_op jit(solution)/shard_map/fine/pallas_call | solution.py:511
  18.1 0.0 collective-permute-done.3.other_ref
  18.1 2.5 %coarse.1 = (bf16[4,64,2048]{2,1,0:T(8,128)(2,1)}, bf16[2,64,2048]{2,1,0:T(8,128)(2,1)}, bf16[4,16,2048]{2,1,0:T(8,128)(2,1)}, bf16[2,16,2048]{2,1,0:T(8,128)(2,1)}) custom-call(f32[48,1024]{1,0:T(8,128)S(1)} %get-tuple-element.31.keep_ref, f32[48,1024]{1,0:T(8,128)S(1)} %collective-permute-done.3.other_ref, ...), custom_call_target="tpu_custom_call" | custom-call | tf_op jit(solution)/shard_map/coarse/pallas_call | solution.py:527
Async XLA Ops:
  1.4 2.0 %collective-permute-start = (f32[64,128]{1,0:T(8,128)S(1)}, f32[64,128]{1,0:T(8,128)S(1)}, u32[]{:S(2)}, u32[]{:S(2)}) collective-permute-start(f32[64,128]{1,0:T(8,128)S(1)} %slice_select_fusion), channel_id=1, source_target_pairs={{0,1},{1,0},{2,3},{3,2},{4,5},{5,4},{6,7},{7,6},{8,9},{9,8},{10,11... | collective-permute-start | bytes 98312 | tf_op jit(solution)/shard_map/ppermute | solution.py:442
  4.3 5.3 %collective-permute-start.1 = (bf16[32,2176]{1,0:T(8,128)(2,1)S(1)}, bf16[32,2176]{1,0:T(8,128)(2,1)S(1)}, u32[]{:S(2)}, u32[]{:S(2)}) collective-permute-start(bf16[32,2176]{1,0:T(8,128)(2,1)S(1)} %get-tuple-element.28), channel_id=1, source_target_pairs={{0,2},{4,6},{8,10},{12,14},{2,0},{6,4},{10,8},{14,12},{1,3},{5,7},... | collective-permute-start | bytes 417800 | tf_op jit(solution)/shard_map/ppermute | solution.py:475
  5.6 7.7 %collective-permute-start.2 = (bf16[32,2176]{1,0:T(8,128)(2,1)S(1)}, bf16[32,2176]{1,0:T(8,128)(2,1)S(1)}, u32[]{:S(2)}, u32[]{:S(2)}) collective-permute-start(bf16[32,2176]{1,0:T(8,128)(2,1)S(1)} %get-tuple-element.29), channel_id=1, source_target_pairs={{2,4},{6,8},{10,12},{4,2},{8,6},{12,10},{3,5},{7,9},{11,13},{5,3},... | collective-permute-start | bytes 417800 | tf_op jit(solution)/shard_map/ppermute | solution.py:475
  13.5 4.5 %collective-permute-start.3 = (f32[48,1024]{1,0:T(8,128)S(1)}, f32[48,1024]{1,0:T(8,128)S(1)}, u32[]{:S(2)}, u32[]{:S(2)}) collective-permute-start(f32[48,1024]{1,0:T(8,128)S(1)} %get-tuple-element.32), channel_id=1, source_target_pairs={{0,1},{1,0},{2,3},{3,2},{4,5},{5,4},{6,7},{7,6},{8,9},{9,8},{10,11... | collective-permute-start | bytes 589832 | tf_op jit(solution)/shard_map/ppermute | solution.py:502

commit v4 on v3

--- a/solution.py
+++ b/solution.py
@@ -14,6 +14,7 @@
 LANES = 128
 BLOCK = 256
 PAD = 8
+RIM = 16
 NEAR = 16
 LOW = 4
 SPAN = 19
@@ -82,10 +83,10 @@
     return jnp.concatenate([eh.astype(BF16), el.astype(BF16)], axis=1)
 
 
-def hess_tiles(d, rows, first_tile, count, gain, put):
+def hess_tiles(d, top, rows, first_tile, count, gain, put):
     tall = rows + 2 * PAD
     lane = lax.broadcasted_iota(jnp.int32, (tall, LANES), 1)
-    tile = lambda t: d[:, (first_tile + t + 1) * LANES : (first_tile + t + 2) * LANES]
+    tile = lambda t: d[top : top + tall, (first_tile + t + 1) * LANES : (first_tile + t + 2) * LANES]
     tiles = {-1: tile(-1), 0: tile(0)}
     back = {t: pltpu.roll(tiles[t], 1, 1) for t in (-1, 0)}
     ahead = {0: pltpu.roll(tiles[0], LANES - 1, 1)}
@@ -181,16 +182,6 @@
         down = jnp.concatenate([down_near, down_part, down_fine, down_low], axis=0)
         even_ref[:, to] = jnp.where(even, down, up).astype(BF16)
         odd_ref[:, to] = jnp.where(even, up, down).astype(BF16)
-
-
-def stage_kernel(*refs):
-    count = (len(refs) - 1) // 2
-    sems = refs[-1]
-    copies = [pltpu.make_async_copy(refs[i], refs[count + i], sems.at[i]) for i in range(count)]
-    for copy in copies:
-        copy.start()
-    for copy in copies:
-        copy.wait()
 
 
 def base_kernel(row_count, tile_base, base_ref, even_ref, odd_ref, _, keep_ref, send_ref, sum_ref):
@@ -231,12 +222,10 @@
         send_ref[:, to] = jnp.where(is_left, total[shift : shift + count], total[:count])
 
 
-def filter_columns(vh, vl, w_refs, group, rows, cols, lev, diffs, gains, dog_ref, hess_ref, seam, border):
+def filter_columns(vh, vl, w_refs, group, cols, lev, emit, after_group, after_level):
     wc_ref, wl_ref, we_ref = w_refs
-    tall = rows + 2 * PAD
-    tiles = group * BLOCK // LANES
+    tall = vh.shape[1]
     for s in range(LEVELS):
-        k = s - 1
         for g in range(0, cols // BLOCK, group):
             ats = [LANES + BLOCK * (g + i) for i in range(group)]
             high = jnp.concatenate([vh[s, :, at : at + BLOCK] for at in ats], axis=0)
@@ -246,73 +235,142 @@
             for i, at in enumerate(ats):
                 new = value[i * tall : (i + 1) * tall]
                 if s > 0:
-                    d = new - lev[:, at : at + BLOCK]
-                    dog_ref[k, :, at - LANES : at - LANES + BLOCK] = (gains[0] * d[PAD : PAD + rows]).astype(BF16)
-                    if k in diffs:
-                        diffs[k][:, at : at + BLOCK] = d
+                    emit(s - 1, at, new - lev[:, at : at + BLOCK])
                 if s + 1 < LEVELS:
                     lev[:, at : at + BLOCK] = new
-            m = s - 3
-            if m >= 0:
-
-                def put(t, value):
-                    hess_ref[m, :, t * LANES : (t + 1) * LANES] = value
-
-                hess_tiles(diffs[m + 1], rows, g * BLOCK // LANES, tiles, gains[1], put)
-        if s in (1, 2, 3):
-            seam(s)
-        if k in diffs:
-            d = diffs[k]
-            d[:PAD, :] = jnp.where(border[0], 0.0, d[:PAD, :])
-            d[PAD + rows :, :] = jnp.where(border[1], 0.0, d[PAD + rows :, :])
-
-
-def fine_kernel(last_row, own_ref, even_ref, odd_ref, lh_ref, wc_ref, wl_ref, we_ref,
-                dog_ref, hess_ref, vh, vl, lev, d1, d2):
-    _, rows, cols = dog_ref.shape
-    row, col = mesh_place()
-    tall = rows + 2 * PAD
-    diffs = {1: d1, 2: d2}
-    is_left = col == 0
-    even = row % 2 == 0
-
-    def rows_of(at, width):
-        part = slice(at, at + width)
-        own = own_ref[:, part]
-        a, b = even_ref[:, part], odd_ref[:, part]
-        bot, top = jnp.where(even, a, b), jnp.where(even, b, a)
-        lows = jnp.concatenate([bot[NEAR : NEAR + 8], top[NEAR + 8 :]], axis=0)
-        again = jnp.concatenate([bot[:8], top[8:NEAR]], axis=0)
-        stack = jnp.concatenate([own, own[:rows], top[:NEAR], bot[:NEAR], lows, again], axis=0)
-        return mm(lh_ref[...], stack)
-
+            if s >= 3:
+                after_group(s - 3, g * BLOCK // LANES, group * BLOCK // LANES)
+        after_level(s)
+
+
+def place_rows(vh, vl, rows_of, cols, is_left):
+    tall = vh.shape[1]
     for at in range(0, cols, BLOCK):
-        value = rows_of(at, BLOCK)
+        value = rows_of(slice(at, at + BLOCK))
         to = slice(LANES + at, LANES + at + BLOCK)
         for s in range(LEVELS):
             vh[s, :, to], vl[s, :, to] = split(value[s * tall : (s + 1) * tall])
-    value = rows_of(cols, LANES)
+    value = rows_of(slice(cols, cols + LANES))
+    left, right = slice(0, LANES), slice(LANES + cols, 2 * LANES + cols)
     for s in range(LEVELS):
         part = value[s * tall : (s + 1) * tall]
-        left = slice(0, LANES)
-        right = slice(LANES + cols, 2 * LANES + cols)
         vh[s, :, left], vl[s, :, left] = split(jnp.where(is_left, 0.0, part))
         vh[s, :, right], vl[s, :, right] = split(jnp.where(is_left, part, 0.0))
 
+
+def seam_filter(vh, vl, w_refs, cols, lev, is_left, emit):
+    wc_ref, wl_ref, _ = w_refs
     start = pl.multiple_of(jnp.where(is_left, cols, 0), LANES)
 
     def seam(s):
+        if s not in (1, 2, 3):
+            return
         high = vh[s, :, pl.ds(start, BLOCK)]
         low = vl[s, :, pl.ds(start, BLOCK)]
         new = mm(high, wc_ref[s]) + mm(low, wc_ref[s]) + mm(high, wl_ref[s])
         if s > 1:
             d = new - lev[:, cols + 2 * LANES :]
-            diffs[s - 1][:, :LANES] = jnp.where(is_left, 0.0, d[:, :LANES])
-            diffs[s - 1][:, cols + LANES :] = jnp.where(is_left, d[:, LANES:], 0.0)
-        lev[:, cols + 2 * LANES :] = new
-
-    filter_columns(vh, vl, (wc_ref, wl_ref, we_ref), 4, rows, cols, lev, diffs, (20.0, 5000.0),
-                   dog_ref, hess_ref, seam, (row == 0, row == last_row))
+            emit(s - 1, 0, jnp.where(is_left, 0.0, d[:, :LANES]))
+            emit(s - 1, cols + LANES, jnp.where(is_left, d[:, LANES:], 0.0))
+        if s < 3:
+            lev[:, cols + 2 * LANES :] = new
+
+    return seam
+
+
+def inner_kernel(own_ref, lh_hbm, wc_hbm, wl_hbm, we_hbm, cw_hbm, lt_hbm,
+                 dog_ref, hess_ref, rim_ref, wc_ref, wl_ref, we_ref, cw_ref, lt_ref,
+                 lh_ref, vh, vl, lev, d1, d2, sems):
+    far = (lh_hbm, wc_hbm, wl_hbm, we_hbm, cw_hbm, lt_hbm)
+    near = (lh_ref, wc_ref, wl_ref, we_ref, cw_ref, lt_ref)
+    copies = [pltpu.make_async_copy(f, n, sems.at[i]) for i, (f, n) in enumerate(zip(far, near))]
+    for copy in copies:
+        copy.start()
+    _, rows, cols = dog_ref.shape
+    _, col = mesh_place()
+    is_left = col == 0
+    diffs = {1: d1, 2: d2}
+    tall = rows + 2 * PAD
+    mid_rows = rows - 2 * RIM
+    rim_tall = RIM + 2 * PAD
+
+    def rows_of(part):
+        own = own_ref[:, part]
+        return mm(lh_ref[...], jnp.concatenate([own, own[:rows]], axis=0))
+
+    def emit(k, at, d):
+        to = slice(at, at + d.shape[1])
+        rim_ref[k, :rim_tall, to] = d[:rim_tall]
+        rim_ref[k, rim_tall:, to] = d[tall - rim_tall :]
+        if 0 < at <= cols:
+            mid = d[PAD + RIM : PAD + RIM + mid_rows]
+            dog_ref[k, RIM : RIM + mid_rows, at - LANES : at - LANES + BLOCK] = (20.0 * mid).astype(BF16)
+        if k in diffs:
+            diffs[k][:, to] = d
+
+    def after_group(m, first, count):
+        def put(t, value):
+            hess_ref[m, RIM : RIM + mid_rows, t * LANES : (t + 1) * LANES] = value
+
+        hess_tiles(diffs[m + 1], RIM, mid_rows, first, count, 5000.0, put)
+
+    copies[0].wait()
+    place_rows(vh, vl, rows_of, cols, is_left)
+    for copy in copies[1:]:
+        copy.wait()
+    w_refs = (wc_ref, wl_ref, we_ref)
+    seam = seam_filter(vh, vl, w_refs, cols, lev, is_left, emit)
+    filter_columns(vh, vl, w_refs, 4, cols, lev, emit, after_group, seam)
+
+
+def outer_kernel(last_row, even_ref, odd_ref, lt_ref, wc_ref, wl_ref, we_ref, rim_ref, dog_in, hess_in,
+                 dog_ref, hess_ref, vh, vl, lev, d1, d2):
+    _, rows, cols = dog_ref.shape
+    row, col = mesh_place()
+    is_left = col == 0
+    even = row % 2 == 0
+    diffs = {1: d1, 2: d2}
+    rim_tall = RIM + 2 * PAD
+
+    def rows_of(part):
+        a, b = even_ref[:, part], odd_ref[:, part]
+        bot, top = jnp.where(even, a, b), jnp.where(even, b, a)
+        lows = jnp.concatenate([bot[NEAR : NEAR + 8], top[NEAR + 8 :]], axis=0)
+        again = jnp.concatenate([bot[:8], top[8:NEAR]], axis=0)
+        return mm(lt_ref[...], jnp.concatenate([top[:NEAR], bot[:NEAR], lows, again], axis=0))
+
+    def emit(k, at, d):
+        to = slice(at, at + d.shape[1])
+        zero = lambda count: jnp.zeros((count, d.shape[1]), F32)
+        top = rim_ref[k, :rim_tall, to] + jnp.concatenate(
+            [zero(PAD - 1), d[:RIM], zero(rim_tall - RIM - PAD + 1)], axis=0
+        )
+        bot = rim_ref[k, rim_tall:, to] + jnp.concatenate(
+            [zero(rim_tall - RIM - PAD + 1), d[RIM:], zero(PAD - 1)], axis=0
+        )
+        if 0 < at <= cols:
+            out = slice(at - LANES, at - LANES + BLOCK)
+            dog_ref[k, :RIM, out] = (20.0 * top[PAD : PAD + RIM]).astype(BF16)
+            dog_ref[k, rows - RIM :, out] = (20.0 * bot[PAD : PAD + RIM]).astype(BF16)
+        if k in diffs:
+            d = diffs[k]
+            d[:PAD, to] = jnp.where(row == 0, 0.0, top[:PAD])
+            d[PAD:rim_tall, to] = top[PAD:]
+            d[rim_tall : 2 * rim_tall - PAD, to] = bot[: rim_tall - PAD]
+            d[2 * rim_tall - PAD :, to] = jnp.where(row == last_row, 0.0, bot[rim_tall - PAD :])
+
+    def after_group(m, first, count):
+        for top, to in ((0, slice(0, RIM)), (rim_tall, slice(rows - RIM, rows))):
+
+            def put(t, value):
+                hess_ref[m, to, t * LANES : (t + 1) * LANES] = value
+
+            hess_tiles(diffs[m + 1], top, RIM, first, count, 5000.0, put)
+
+    place_rows(vh, vl, rows_of, cols, is_left)
+    w_refs = (wc_ref, wl_ref, we_ref)
+    seam = seam_filter(vh, vl, w_refs, cols, lev, is_left, emit)
+    filter_columns(vh, vl, w_refs, 8, cols, lev, emit, after_group, seam)
 
 
 def coarse_kernel(last_row, keep_ref, other_ref, fine_dog_ref, fine_hess_ref, lh_ref, wc_ref, wl_ref, we_ref,
@@ -350,9 +408,21 @@
         for s in range(LEVELS):
             vh[s, :, to], vl[s, :, to] = split(value[s * tall : (s + 1) * tall])
 
-    filter_columns(vh, vl, (wc_ref, wl_ref, we_ref), 8, rows, cols, lev, diffs, (80.0, 200000.0),
-                   dog_ref, hess_ref, lambda s: None,
-                   ((row == 0) & (col == 0), (row == last_row) & (col == 1)))
+    def emit(k, at, d):
+        dog_ref[k, :, at - LANES : at - LANES + BLOCK] = (80.0 * d[PAD : PAD + rows]).astype(BF16)
+        if k in diffs:
+            to = slice(at, at + BLOCK)
+            diffs[k][:PAD, to] = jnp.where((row == 0) & (col == 0), 0.0, d[:PAD])
+            diffs[k][PAD : PAD + rows, to] = d[PAD : PAD + rows]
+            diffs[k][PAD + rows :, to] = jnp.where((row == last_row) & (col == 1), 0.0, d[PAD + rows :])
+
+    def after_group(m, first, count):
+        def put(t, value):
+            hess_ref[m, :, t * LANES : (t + 1) * LANES] = value
+
+        hess_tiles(diffs[m + 1], 0, rows, first, count, 200000.0, put)
+
+    filter_columns(vh, vl, (wc_ref, wl_ref, we_ref), 8, cols, lev, emit, after_group, lambda s: None)
     copies = [
         pltpu.make_async_copy(dog_ref, dog_hbm, sems.at[2]),
         pltpu.make_async_copy(hess_ref, hess_hbm, sems.at[3]),
@@ -371,10 +441,10 @@
     lows[:LOW] = bot[:LOW]
     lows[NEAR - LOW :] = top[NEAR - LOW :]
     again = np.concatenate([bot[:8], top[8:]])
-    inputs = np.concatenate([own, own, own, top, bot, lows, again])
-    use_low = np.zeros(inputs.shape, bool)
-    use_low[2 * rows : 3 * rows] = True
-    use_low[-NEAR:] = True
+    own_inputs = np.concatenate([own, own, own])
+    own_low = np.arange(3 * rows) >= 2 * rows
+    far_inputs = np.concatenate([top, bot, lows, again])
+    far_low = np.arange(4 * NEAR) >= 3 * NEAR
 
     def matrix(sigma, centres, valid, inputs, use_low):
         high, low = two_parts(row_matrix(sigma, centres, inputs) * valid[:, None])
@@ -382,14 +452,14 @@
 
     centres = np.arange(-PAD, rows + PAD)
     valid = ((centres >= -1) & (centres <= rows)).astype(np.float32)
-    level = [matrix(s, centres, valid, inputs, use_low) for s in SIGMAS]
+    level = [matrix(s, centres, valid, own_inputs, own_low) for s in SIGMAS]
+    rim = np.concatenate([np.arange(-1, RIM - 1), np.arange(rows + 1 - RIM, rows + 1)])
+    halo = [matrix(s, rim, np.ones(rim.shape, np.float32), far_inputs, far_low) for s in SIGMAS]
     count = rows // 2 + 2 * (REACH + 1)
     index = np.arange(-(-count // 8) * 8)
-    base = matrix(
-        SIGMAS[-1], 2 * (index - REACH - 1), (index < count).astype(np.float32), inputs[: 3 * rows], use_low[: 3 * rows]
-    )
+    base = matrix(SIGMAS[-1], 2 * (index - REACH - 1), (index < count).astype(np.float32), own_inputs, own_low)
     strip_rows = -(-(rows // 4 + 2 * (REACH + 1)) // 16) * 16
-    return np.concatenate(level), base, strip_rows
+    return np.concatenate(level), np.concatenate(halo), base, strip_rows
 
 
 def coarse_constants(strip, padded):
@@ -431,12 +501,12 @@
     wide = cols + LANES
     tall = rows + 2 * PAD
     small = strip + 2 * PAD
-    lh, bm, strip_rows = fine_constants(rows)
+    lh, lt, bm, strip_rows = fine_constants(rows)
     cw = coarse_constants(strip, strip_rows)
     bands = [column_weights(s, 1) for s in SIGMAS]
     wc, wl, we = (np.stack([b[i] for b in bands]) for i in range(3))
     early = [far(c) for c in (bm, *column_weights(SIGMAS[-1], 2))]
-    late = [far(c) for c in (lh, wc, wl, we, cw)]
+    late = [far(c) for c in (lh, wc, wl, we, cw, lt)]
 
     side = jnp.where(col == 0, image[:, cols - LANES :], image[:, :LANES])
     side = lax.ppermute(side, "col", [(0, 1), (1, 0)])
@@ -476,16 +546,44 @@
 
     even, odd = swap(to_even, 0), swap(to_odd, 1)
 
-    lh, wc, wl, we, cw = pl.pallas_call(
-        stage_kernel,
-        out_shape=tuple(like(c) for c in late),
-        in_specs=far_specs(len(late)),
-        out_specs=tuple(vmem_specs(len(late))),
-        scratch_shapes=[pltpu.SemaphoreType.DMA((len(late),))],
-        compiler_params=limit(6),
-        cost_estimate=pl.CostEstimate(flops=10**8, bytes_accessed=10**7, transcendentals=0),
-        name="stage",
-    )(*late)
+    fine_shapes = (
+        jax.ShapeDtypeStruct((4, rows, cols), BF16),
+        jax.ShapeDtypeStruct((2, rows, cols), BF16),
+    )
+    coarse_shapes = (
+        jax.ShapeDtypeStruct((4, strip, cols), BF16),
+        jax.ShapeDtypeStruct((2, strip, cols), BF16),
+    )
+
+    def scratch(count, height, seam):
+        padded_cols = cols + 2 * LANES
+        return [
+            pltpu.VMEM((LEVELS, height, padded_cols), BF16),
+            pltpu.VMEM((LEVELS, height, padded_cols), BF16),
+            pltpu.VMEM((height, padded_cols + seam), F32),
+            pltpu.VMEM((count, padded_cols), F32),
+            pltpu.VMEM((count, padded_cols), F32),
+        ]
+
+    rim_tall = RIM + 2 * PAD
+    dog_fine, hess_fine, rim, wc, wl, we, cw, lt = pl.pallas_call(
+        inner_kernel,
+        out_shape=(
+            *fine_shapes,
+            jax.ShapeDtypeStruct((4, 2 * rim_tall, cols + 2 * LANES), F32),
+            *(like(c) for c in late[1:]),
+        ),
+        in_specs=vmem_specs(1) + far_specs(len(late)),
+        out_specs=tuple(vmem_specs(3 + len(late) - 1)),
+        scratch_shapes=[
+            pltpu.VMEM(late[0].shape, late[0].dtype),
+            *scratch(tall, tall, BLOCK),
+            pltpu.SemaphoreType.DMA((len(late),)),
+        ],
+        compiler_params=limit(18),
+        cost_estimate=pl.CostEstimate(flops=2 * 10**9, bytes_accessed=10**7, transcendentals=0),
+        name="inner",
+    )(own, *late)
 
     keep, send = pl.pallas_call(
         functools.partial(base_kernel, row_count, rows // 2),
@@ -500,29 +598,17 @@
         name="base",
     )(base, even, odd, cw)
     other = lax.ppermute(send, "col", [(0, 1), (1, 0)])
-    fine_shapes = (
-        jax.ShapeDtypeStruct((4, rows, cols), BF16),
-        jax.ShapeDtypeStruct((2, rows, cols), BF16),
-    )
-    coarse_shapes = (
-        jax.ShapeDtypeStruct((4, strip, cols), BF16),
-        jax.ShapeDtypeStruct((2, strip, cols), BF16),
-    )
     dog_fine, hess_fine = pl.pallas_call(
-        functools.partial(fine_kernel, row_count - 1),
+        functools.partial(outer_kernel, row_count - 1),
         out_shape=fine_shapes,
-        in_specs=vmem_specs(7),
+        in_specs=vmem_specs(9),
         out_specs=tuple(vmem_specs(2)),
-        scratch_shapes=[
-            pltpu.VMEM((LEVELS, tall, cols + 2 * LANES), BF16),
-            pltpu.VMEM((LEVELS, tall, cols + 2 * LANES), BF16),
-            pltpu.VMEM((tall, cols + 2 * LANES + BLOCK), F32),
-            pltpu.VMEM((tall, cols + 2 * LANES), F32),
-            pltpu.VMEM((tall, cols + 2 * LANES), F32),
-        ],
-        compiler_params=limit(16),
-        name="fine",
-    )(own, even, odd, lh, wc, wl, we)
+        scratch_shapes=scratch(2 * rim_tall, 2 * RIM, BLOCK),
+        input_output_aliases={7: 0, 8: 1},
+        compiler_params=limit(14),
+        cost_estimate=pl.CostEstimate(flops=10**9, bytes_accessed=10**6, transcendentals=0),
+        name="outer",
+    )(even, odd, lt, wc, wl, we, rim, dog_fine, hess_fine)
 
     return pl.pallas_call(
         functools.partial(coarse_kernel, row_count - 1),
@@ -532,11 +618,7 @@
         scratch_shapes=[
             pltpu.VMEM((4, strip, cols), BF16),
             pltpu.VMEM((2, strip, cols), BF16),
-            pltpu.VMEM((LEVELS, small, cols + 2 * LANES), BF16),
-            pltpu.VMEM((LEVELS, small, cols + 2 * LANES), BF16),
-            pltpu.VMEM((small, cols + 2 * LANES), F32),
-            pltpu.VMEM((small, cols + 2 * LANES), F32),
-            pltpu.VMEM((small, cols + 2 * LANES), F32),
+            *scratch(small, small, 0),
             pltpu.SemaphoreType.DMA((4,)),
         ],
         compiler_params=limit(12),

time: 20.9 us -> 19.1 us (0.914)
  waiting for transfers between devices: 4.06 us -> 1.8 us
  Pallas kernels: 9.89 us -> 10.4 us
    ppermute x2, waiting for transfers between devices: 4.06 us -> 1.79 us  [swap(): return lax.ppermute(value, 'row', pairs + [(j, i) for i, j in pairs])]
    pallas_call x2, Pallas kernels: 4.97 us -> 5.52 us  [the longest x1 3.91 us: local(): pl.pallas_call(inner_kernel, out_shape=(*fine_shapes, jax.ShapeDtypeStruc...]
  transfers between devices with their start and end apart: 4 -> 4, of which waited for: 2 -> 1; matrix products, arithmetic and copies ran while one was open for 0% -> 0% of each run, Pallas kernels for 30% -> 36%
where the time goes in v4:
time: 19.1 us; the launch traced here: 18.8 us
  Pallas kernels  10.4 us (54%)
  starting transfers between devices  5.18 us (27%)
  waiting for transfers between devices  1.8 us (9%)
  other arithmetic  0.78 us (4%)
  between operations  0.7 us (4%)
    pallas_call x1, Pallas kernels, local(): pl.pallas_call(inner_kernel, out_shape=(*fine_shapes, jax.ShapeDtypeStruc...  3.91 us
    ppermute x2, starting transfers between devices, swap(): return lax.ppermute(value, 'row', pairs + [(j, i) for i, j in pairs])  3.31 us
    pallas_call x1, Pallas kernels, local(): pl.pallas_call(functools.partial(coarse_kernel, row_count - 1), out_shape...  2.48 us
    ppermute x2, waiting for transfers between devices, swap(): return lax.ppermute(value, 'row', pairs + [(j, i) for i, j in pairs])  1.79 us
    pallas_call x1, Pallas kernels, local(): pl.pallas_call(functools.partial(outer_kernel, row_count - 1), out_shape=...  1.61 us
    pallas_call x1, Pallas kernels, local(): pl.pallas_call(pack_kernel, out_shape=(jax.ShapeDtypeStruct((2 * rows, wi...  1.28 us
    ppermute x1, starting transfers between devices, local(): other = lax.ppermute(send, 'col', [(0, 1), (1, 0)])  1.19 us
    pallas_call x1, Pallas kernels, local(): pl.pallas_call(send_kernel, out_shape=(jax.ShapeDtypeStruct((2 * rows, wi...  0.93 us
  transfers between devices with their start and end apart: 4, of which 1 were waited for; matrix products, arithmetic and copies ran while one was open for 0% of the time, Pallas kernels for 36%

profile of v4, /device:TPU:11, one launch (start us, length us, event | category | flops | bytes accessed | tf_op | source)
XLA Modules:
  0.0 18.8 jit_solution(9450897474083004881)
XLA Ops:
  0.6 0.8 %slice_select_fusion = f32[64,128]{1,0:T(8,128)S(1)} fusion(f32[64,2048]{1,0:T(8,128)} %x_hbm.1, pred[]{:T(512)S(6)} %eq.3), kind=kLoop, calls=%fused_computation | loop fusion | flops 8192 | bytes 98305 | tf_op jit(solution)/shard_map/jit(_where)/select_n | solution.py:511
  1.4 0.7 %collective-permute-start = (f32[64,128]{1,0:T(8,128)S(1)}, f32[64,128]{1,0:T(8,128)S(1)}, u32[]{:S(2)}, u32[]{:S(2)}) collective-permute-start(f32[64,128]{1,0:T(8,128)S(1)} %slice_select_fusion), channel_id=1, source_target_pairs={{0,1},{1,0},{2,3},{3,2},{4,5},{5,4},{6,7},{7,6},{8,9},{9,8},{10,11... | collective-permute-start | bytes 98312 | tf_op jit(solution)/shard_map/ppermute | solution.py:512
  2.1 1.3 %pack.1 = (bf16[128,2176]{1,0:T(8,128)(2,1)S(1)}, bf16[64,192]{1,0:T(8,128)(2,1)S(1)}, bf16[512,256]{1,0:T(8,128)(2,1)S(1)}, bf16[512,256]{1,0:T(8,128)(2,1)S(1)}, bf16[256,256]{1,0:T(8,128)(2,1)S(1)}) custom-call(f32[64,2048]{1,0:T(8,128)} %x_hbm.1, bf16[64,192]{1,0:T(8,128)(2,1)} %constant.26.clone.refs_0_, bf16[512,256]{1,0:T(8,128)(2,1)} %constant.27.clone.refs_1_, ...), custom_call_target="tpu_custom_call" | custom-call | tf_op jit(solution)/shard_map/pack/pallas_call | solution.py:513
  3.4 0.0 collective-permute-done.side_ref
  3.4 0.9 %send.1 = (bf16[128,2176]{1,0:T(8,128)(2,1)S(1)}, bf16[32,2176]{1,0:T(8,128)(2,1)S(1)}, bf16[32,2176]{1,0:T(8,128)(2,1)S(1)}, f32[64,1024]{1,0:T(8,128)S(1)}) custom-call(f32[64,128]{1,0:T(8,128)S(1)} %collective-permute-done.side_ref, bf16[128,2176]{1,0:T(8,128)(2,1)S(1)} %get-tuple-element.25.own_in, ...), custom_call_target="tpu_custom_call", output_to_operand_aliasing={{0}: (1, {})} | custom-call | tf_op jit(solution)/shard_map/send/pallas_call | solution.py:524
  4.3 1.3 %collective-permute-start.1 = (bf16[32,2176]{1,0:T(8,128)(2,1)S(1)}, bf16[32,2176]{1,0:T(8,128)(2,1)S(1)}, u32[]{:S(2)}, u32[]{:S(2)}) collective-permute-start(bf16[32,2176]{1,0:T(8,128)(2,1)S(1)} %get-tuple-element.31), channel_id=1, source_target_pairs={{0,2},{4,6},{8,10},{12,14},{2,0},{6,4},{10,8},{14,12},{1,3},{5,7},... | collective-permute-start | bytes 417800 | tf_op jit(solution)/shard_map/ppermute | solution.py:545
  5.6 2.0 %collective-permute-start.2 = (bf16[32,2176]{1,0:T(8,128)(2,1)S(1)}, bf16[32,2176]{1,0:T(8,128)(2,1)S(1)}, u32[]{:S(2)}, u32[]{:S(2)}) collective-permute-start(bf16[32,2176]{1,0:T(8,128)(2,1)S(1)} %get-tuple-element.32), channel_id=1, source_target_pairs={{2,4},{6,8},{10,12},{4,2},{8,6},{12,10},{3,5},{7,9},{11,13},{5,3},... | collective-permute-start | bytes 417800 | tf_op jit(solution)/shard_map/ppermute | solution.py:545
  7.6 3.9 %inner.1 = (bf16[4,64,2048]{2,1,0:T(8,128)(2,1)S(1)}, bf16[2,64,2048]{2,1,0:T(8,128)(2,1)S(1)}, f32[4,64,2304]{2,1,0:T(8,128)S(1)}, bf16[5,256,256]{2,1,0:T(8,12...) custom-call(bf16[128,2176]{1,0:T(8,128)(2,1)S(1)} %get-tuple-element, ...), custom_call_target="tpu_custom_call" | custom-call | flops 2000000000 | bytes 10000000 | tf_op jit(solution)/shard_map/inner/pallas_call | solution.py:569
  11.6 0.0 collective-permute-done.1.even_ref
  11.6 1.8 %collective-permute-done.2.odd_ref = bf16[32,2176]{1,0:T(8,128)(2,1)S(1)} collective-permute-done((bf16[32,2176]{1,0:T(8,128)(2,1)S(1)}, bf16[32,2176]{1,0:T(8,128)(2,1)S(1)}, u32[]{:S(2)}, u32[]{:S(2)}) %collective-permute-start.2) | collective-permute-done | bytes 139296 | tf_op jit(solution)/shard_map/ppermute | solution.py:545
  13.4 0.2 base.1
  13.5 1.2 %collective-permute-start.3 = (f32[48,1024]{1,0:T(8,128)S(1)}, f32[48,1024]{1,0:T(8,128)S(1)}, u32[]{:S(2)}, u32[]{:S(2)}) collective-permute-start(f32[48,1024]{1,0:T(8,128)S(1)} %get-tuple-element.36), channel_id=1, source_target_pairs={{0,1},{1,0},{2,3},{3,2},{4,5},{5,4},{6,7},{7,6},{8,9},{9,8},{10,11... | collective-permute-start | bytes 589832 | tf_op jit(solution)/shard_map/ppermute | solution.py:600
  14.7 1.6 %outer.1 = (bf16[4,64,2048]{2,1,0:T(8,128)(2,1)S(1)}, bf16[2,64,2048]{2,1,0:T(8,128)(2,1)S(1)}) custom-call(bf16[32,2176]{1,0:T(8,128)(2,1)S(1)} %collective-permute-done.1.even_ref, bf16[32,2176]{1,0:T(8,128)(2,1)S(1)} %collective-permute-done.2.odd_ref, ...), custom_call_target="tpu_custom_call", output_to_operand_aliasing={{0}: (7, {}), {1}: (8, {})} | custom-call | flops 1000000000 | bytes 1000000 | tf_op jit(solution)/shard_map/outer/pallas_call | solution.py:601
  16.4 0.0 collective-permute-done.3.other_ref
  16.4 2.5 %coarse.1 = (bf16[4,64,2048]{2,1,0:T(8,128)(2,1)}, bf16[2,64,2048]{2,1,0:T(8,128)(2,1)}, bf16[4,16,2048]{2,1,0:T(8,128)(2,1)}, bf16[2,16,2048]{2,1,0:T(8,128)(2,1)}) custom-call(f32[48,1024]{1,0:T(8,128)S(1)} %get-tuple-element.35.keep_ref, f32[48,1024]{1,0:T(8,128)S(1)} %collective-permute-done.3.other_ref, ...), custom_call_target="tpu_custom_call" | custom-call | tf_op jit(solution)/shard_map/coarse/pallas_call | solution.py:613
Async XLA Ops:
  1.4 2.0 %collective-permute-start = (f32[64,128]{1,0:T(8,128)S(1)}, f32[64,128]{1,0:T(8,128)S(1)}, u32[]{:S(2)}, u32[]{:S(2)}) collective-permute-start(f32[64,128]{1,0:T(8,128)S(1)} %slice_select_fusion), channel_id=1, source_target_pairs={{0,1},{1,0},{2,3},{3,2},{4,5},{5,4},{6,7},{7,6},{8,9},{9,8},{10,11... | collective-permute-start | bytes 98312 | tf_op jit(solution)/shard_map/ppermute | solution.py:512
  4.3 7.2 %collective-permute-start.1 = (bf16[32,2176]{1,0:T(8,128)(2,1)S(1)}, bf16[32,2176]{1,0:T(8,128)(2,1)S(1)}, u32[]{:S(2)}, u32[]{:S(2)}) collective-permute-start(bf16[32,2176]{1,0:T(8,128)(2,1)S(1)} %get-tuple-element.31), channel_id=1, source_target_pairs={{0,2},{4,6},{8,10},{12,14},{2,0},{6,4},{10,8},{14,12},{1,3},{5,7},... | collective-permute-start | bytes 417800 | tf_op jit(solution)/shard_map/ppermute | solution.py:545
  5.6 7.7 %collective-permute-start.2 = (bf16[32,2176]{1,0:T(8,128)(2,1)S(1)}, bf16[32,2176]{1,0:T(8,128)(2,1)S(1)}, u32[]{:S(2)}, u32[]{:S(2)}) collective-permute-start(bf16[32,2176]{1,0:T(8,128)(2,1)S(1)} %get-tuple-element.32), channel_id=1, source_target_pairs={{2,4},{6,8},{10,12},{4,2},{8,6},{12,10},{3,5},{7,9},{11,13},{5,3},... | collective-permute-start | bytes 417800 | tf_op jit(solution)/shard_map/ppermute | solution.py:545
  13.5 2.8 %collective-permute-start.3 = (f32[48,1024]{1,0:T(8,128)S(1)}, f32[48,1024]{1,0:T(8,128)S(1)}, u32[]{:S(2)}, u32[]{:S(2)}) collective-permute-start(f32[48,1024]{1,0:T(8,128)S(1)} %get-tuple-element.36), channel_id=1, source_target_pairs={{0,1},{1,0},{2,3},{3,2},{4,5},{5,4},{6,7},{7,6},{8,9},{9,8},{10,11... | collective-permute-start | bytes 589832 | tf_op jit(solution)/shard_map/ppermute | solution.py:600

commit v5 on v4

--- a/solution.py
+++ b/solution.py
@@ -15,11 +15,10 @@
 BLOCK = 256
 PAD = 8
 RIM = 16
-NEAR = 16
-LOW = 4
+NEAR = REACH + 1
 SPAN = 19
 PART = 10
-FINE = 4
+MESSAGE = NEAR + 1 + PART
 BF16 = jnp.bfloat16
 F32 = jnp.float32
 
@@ -69,18 +68,18 @@
     return jnp.dot(a, b, preferred_element_type=F32)
 
 
-def edge_columns(high, low, at, width):
-    def both(ref):
-        left = ref[:, at - LANES : at].astype(F32)
-        right = ref[:, at + width : at + width + LANES].astype(F32)
-        lane = lax.broadcasted_iota(jnp.int32, left.shape, 1)
-        return jnp.where(lane < LANES // 2, right, left), lane
-
-    eh, lane = both(high)
-    el, _ = both(low)
+def edge_pair(high_left, high_right, low_left, low_right):
+    lane = lax.broadcasted_iota(jnp.int32, high_left.shape, 1)
+    eh = jnp.where(lane < LANES // 2, high_right.astype(F32), high_left.astype(F32))
+    el = jnp.where(lane < LANES // 2, low_right.astype(F32), low_left.astype(F32))
     again = pltpu.roll(eh, 32, 1)
     eh = jnp.where((lane >= 16) & (lane < 64), again, eh)
     return jnp.concatenate([eh.astype(BF16), el.astype(BF16)], axis=1)
+
+
+def edge_columns(high, low, at, width):
+    left, right = slice(at - LANES, at), slice(at + width, at + width + LANES)
+    return edge_pair(high[:, left], high[:, right], low[:, left], low[:, right])
 
 
 def hess_tiles(d, top, rows, first_tile, count, gain, put):
@@ -110,113 +109,140 @@
     return lax.axis_index("row"), lax.axis_index("col")
 
 
-def pack_kernel(x_hbm, *refs):
-    count = (len(refs) - 3) // 2
-    far, own_ref, near, x_ref, sems = refs[:count], refs[count], refs[count + 1 : -2], refs[-2], refs[-1]
-    copies = [pltpu.make_async_copy(x_hbm, x_ref, sems.at[0])]
-    copies += [pltpu.make_async_copy(f, n, sems.at[i + 1]) for i, (f, n) in enumerate(zip(far, near))]
-    for copy in copies:
-        copy.start()
-    copies[0].wait()
+def pack_kernel(x_hbm, early_hbm, own_ref, side_ref, early_ref, x_ref, sems):
+    copy = pltpu.make_async_copy(x_hbm, x_ref, sems.at[0])
+    constants = pltpu.make_async_copy(early_hbm, early_ref, sems.at[1])
+    copy.start()
+    constants.start()
+    _, col = mesh_place()
     rows, cols = x_ref.shape
+    copy.wait()
+    side_ref[...] = jnp.where(col == 0, x_ref[:, cols - LANES :], x_ref[:, :LANES])
     for at in range(0, cols, BLOCK):
         to = slice(at, at + BLOCK)
         own_ref[:rows, to], own_ref[rows:, to] = split(x_ref[:, to])
-    for copy in copies[1:]:
-        copy.wait()
-
-
-def send_kernel(side_ref, own_in, bm_ref, dc_ref, dl_ref, de_ref,
-                own_ref, even_ref, odd_ref, base_ref, bvh, bvl):
+    constants.wait()
+
+
+def build_message(own_ref, part, rows, to):
+    up_near = own_ref[:rows, to].astype(F32)[:NEAR]
+    down_near = own_ref[:rows, to].astype(F32)[rows - NEAR :]
+    up_low = own_ref[rows:, to].astype(F32)[:1]
+    down_low = own_ref[rows:, to].astype(F32)[rows - 1 :]
+    up = jnp.concatenate([up_near, up_low, part[0]], axis=0)
+    down = jnp.concatenate([down_near, down_low, part[1]], axis=0)
+    return up, down
+
+
+def send_kernel(own_ref, early_ref, even_ref, odd_ref, base_ref, bvh, bvl):
     row, col = mesh_place()
     rows = own_ref.shape[0] // 2
     cols = own_ref.shape[1] - LANES
+    half = cols // 2
+    base_rows = base_ref.shape[0]
     is_left = col == 0
     even = row % 2 == 0
-    own_ref[:rows, cols:], own_ref[rows:, cols:] = split(side_ref[...])
-
-    def rows_of(part):
-        own = own_ref[:, part]
-        return mm(bm_ref[...], jnp.concatenate([own, own[:rows]], axis=0))
-
+    bm = early_ref[:base_rows, : 3 * rows]
+    dc = early_ref[base_rows : base_rows + 2 * BLOCK]
+    dl = early_ref[base_rows + 2 * BLOCK : base_rows + 4 * BLOCK]
+    de = early_ref[base_rows + 4 * BLOCK :]
+
+    zero = jnp.zeros((base_rows, LANES), BF16)
+    for ref in (bvh, bvl):
+        ref[:, :LANES] = zero
+        ref[:, LANES + cols :] = zero
     for at in range(0, cols, BLOCK):
+        own = own_ref[:, at : at + BLOCK]
+        value = mm(bm, jnp.concatenate([own, own[:rows]], axis=0))
         to = slice(LANES + at, LANES + at + BLOCK)
-        bvh[:, to], bvl[:, to] = split(rows_of(slice(at, at + BLOCK)))
-    value = rows_of(slice(cols, cols + LANES))
-    bvh[:, :LANES], bvl[:, :LANES] = split(jnp.where(is_left, 0.0, value))
-    bvh[:, LANES + cols :], bvl[:, LANES + cols :] = split(jnp.where(is_left, value, 0.0))
+        bvh[:, to], bvl[:, to] = split(value)
     for j in range(cols // (2 * BLOCK)):
         at = LANES + 2 * BLOCK * j
         high = bvh[:, at : at + 2 * BLOCK]
         low = bvl[:, at : at + 2 * BLOCK]
         edge = edge_columns(bvh, bvl, at, 2 * BLOCK)
-        base_ref[:, j * BLOCK : (j + 1) * BLOCK] = (
-            mm(high, dc_ref[...]) + mm(low, dc_ref[...]) + mm(high, dl_ref[...]) + mm(edge, de_ref[...])
-        )
-
-    half = cols // 2
+        base_ref[:, j * BLOCK : (j + 1) * BLOCK] = mm(high, dc) + mm(low, dc) + mm(high, dl) + mm(edge, de)
+    first, last = slice(LANES, 2 * LANES), slice(cols, cols + LANES)
+    none = jnp.zeros((base_rows, LANES), BF16)
+    pick = lambda ref: (
+        jnp.where(is_left, ref[:, last].astype(F32), 0.0),
+        jnp.where(is_left, 0.0, ref[:, first].astype(F32)),
+    )
+    value = mm(edge_pair(*pick(bvh), *pick(bvl)), de)
+    base_ref[:, half:] = jnp.where(is_left, value[:, :LANES], value[:, LANES:])
+
     first_up = REACH + 1 - 6
     first_down = REACH + 1 + SPAN
     for at in range(0, cols + LANES, LANES):
         to = slice(at, at + LANES)
-        up_near, down_near = own_ref[:NEAR, to].astype(F32), own_ref[rows - NEAR : rows, to].astype(F32)
-        up_low = own_ref[rows : rows + NEAR, to].astype(F32)[:LOW]
-        down_low = own_ref[2 * rows - NEAR :, to].astype(F32)[NEAR - LOW :]
         if at < cols:
             lanes = slice(at % half, at % half + LANES)
             skip = PART * (at // half)
-            up_part = base_ref[first_up + skip : first_up + skip + PART, lanes]
-            down_part = base_ref[first_down + skip : first_down + skip + PART, lanes]
-            skip = FINE // 2 * (at // half)
-
-            def low_of(start):
-                value = base_ref[start + skip : start + skip + FINE // 2, lanes]
-                return value - value.astype(BF16).astype(F32)
-
-            up_fine = low_of(first_up + SPAN - 13)
-            down_fine = low_of(first_down + 13 - FINE)
+            part = [base_ref[f + skip : f + skip + PART, lanes] for f in (first_up, first_down)]
         else:
-            up_part = down_part = jnp.zeros((PART, LANES), F32)
-            up_fine = down_fine = jnp.zeros((FINE // 2, LANES), F32)
-        up = jnp.concatenate([up_near, up_low, up_fine, up_part], axis=0)
-        down = jnp.concatenate([down_near, down_part, down_fine, down_low], axis=0)
+            part = [
+                base_ref[f : f + PART, half:] + pltpu.roll(base_ref[f + PART : f + 2 * PART, half:], LANES // 2, 1)
+                for f in (first_up, first_down)
+            ]
+        up, down = build_message(own_ref, part, rows, to)
+        if at == cols:
+            index = lax.broadcasted_iota(jnp.int32, up.shape, 0)
+            up = jnp.where(index > NEAR, up, 0.0)
+            down = jnp.where(index > NEAR, down, 0.0)
         even_ref[:, to] = jnp.where(even, down, up).astype(BF16)
         odd_ref[:, to] = jnp.where(even, up, down).astype(BF16)
 
 
+def side_kernel(side_ref, own_in, even_in, odd_in, own_ref, even_ref, odd_ref):
+    row, _ = mesh_place()
+    rows = own_ref.shape[0] // 2
+    cols = own_ref.shape[1] - LANES
+    even = row % 2 == 0
+    high, low = split(side_ref[...])
+    own_ref[:rows, cols:] = high
+    own_ref[rows:, cols:] = low
+    high, low = high.astype(F32), low.astype(F32)
+    none = jnp.zeros((PART, LANES), F32)
+    up = jnp.concatenate([high[:NEAR], low[:1], none], axis=0)
+    down = jnp.concatenate([high[rows - NEAR :], low[rows - 1 :], none], axis=0)
+    index = lax.broadcasted_iota(jnp.int32, up.shape, 0)
+    for old, ref, a, b in ((even_in, even_ref, down, up), (odd_in, odd_ref, up, down)):
+        kept = old[:, cols:].astype(F32)
+        ref[:, cols:] = jnp.where(index > NEAR, kept, jnp.where(even, a, b)).astype(BF16)
+
+
 def base_kernel(row_count, tile_base, base_ref, even_ref, odd_ref, _, keep_ref, send_ref, sum_ref):
     row, col = mesh_place()
-    base_rows, half = base_ref.shape
+    base_rows, wide = base_ref.shape
+    half = wide - LANES
     count = keep_ref.shape[0]
     shift = tile_base // 2
     even = row % 2 == 0
     is_left = col == 0
     index = lax.broadcasted_iota(jnp.int32, (base_rows, LANES), 0)
+    lane = lax.broadcasted_iota(jnp.int32, (PART, LANES), 1)
+    outside = (lane >= LANES // 4) & (lane < 3 * LANES // 4)
     place = row * tile_base - REACH - 1 + index
     inside = (place >= 0) & (place < row_count * tile_base)
     first_bot = tile_base + REACH + 1 - 6
-    for at in range(0, half, LANES):
-        def message(ref_a, ref_b):
-            both = []
-            for lanes in (slice(at, at + LANES), slice(half + at, half + at + LANES)):
-                a, b = ref_a[NEAR:, lanes].astype(F32), ref_b[NEAR:, lanes].astype(F32)
-                both.append(jnp.where(even, a, b))
-            return both
-
+
+    def parts(ref_a, ref_b, at):
+        def rows_of(lanes):
+            a, b = ref_a[:, lanes].astype(F32), ref_b[:, lanes].astype(F32)
+            return jnp.where(even, a, b)[NEAR + 1 :]
+
+        if at < half:
+            both = [rows_of(slice(at, at + LANES)), rows_of(slice(half + at, half + at + LANES))]
+        else:
+            value = rows_of(slice(2 * half, 2 * half + LANES))
+            both = [jnp.where(outside, 0.0, v) for v in (value, pltpu.roll(value, LANES // 2, 1))]
+        return jnp.concatenate([both[0], both[1][: SPAN - PART]], axis=0)
+
+    for at in range(0, wide, LANES):
         to = slice(at, at + LANES)
-        left, right = message(odd_ref, even_ref)
-        top = jnp.concatenate([left[:PART], right[: SPAN - PART]], axis=0)
-        top_fine = jnp.concatenate([left[PART : PART + FINE // 2], right[PART : PART + FINE // 2]], axis=0)
-        left, right = message(even_ref, odd_ref)
-        skip = LOW + FINE // 2
-        bot = jnp.concatenate([left[skip:], right[skip : skip + SPAN - PART]], axis=0)
-        bot_fine = jnp.concatenate([left[LOW:skip], right[LOW:skip]], axis=0)
         sum_ref[...] = base_ref[:, to]
-        sum_ref[:SPAN, :] += top
-        sum_ref[13 - FINE : 13, :] += top_fine
-        sum_ref[first_bot : first_bot + SPAN, :] += bot
-        first_fine = first_bot + SPAN - 13
-        sum_ref[first_fine : first_fine + FINE, :] += bot_fine
+        sum_ref[:SPAN, :] += parts(odd_ref, even_ref, at)
+        sum_ref[first_bot : first_bot + SPAN, :] += parts(even_ref, odd_ref, at)
         total = jnp.where(inside, sum_ref[...], 0.0)
         keep_ref[:, to] = jnp.where(is_left, total[:count], total[shift : shift + count])
         send_ref[:, to] = jnp.where(is_left, total[shift : shift + count], total[:count])
@@ -226,12 +252,15 @@
     wc_ref, wl_ref, we_ref = w_refs
     tall = vh.shape[1]
     for s in range(LEVELS):
+        band = slice(s * BLOCK, (s + 1) * BLOCK)
         for g in range(0, cols // BLOCK, group):
             ats = [LANES + BLOCK * (g + i) for i in range(group)]
             high = jnp.concatenate([vh[s, :, at : at + BLOCK] for at in ats], axis=0)
             low = jnp.concatenate([vl[s, :, at : at + BLOCK] for at in ats], axis=0)
             edge = jnp.concatenate([edge_columns(vh.at[s], vl.at[s], at, BLOCK) for at in ats], axis=0)
-            value = mm(high, wc_ref[s]) + mm(low, wc_ref[s]) + mm(high, wl_ref[s]) + mm(edge, we_ref[s])
+            value = (
+                mm(high, wc_ref[band]) + mm(low, wc_ref[band]) + mm(high, wl_ref[band]) + mm(edge, we_ref[band])
+            )
             for i, at in enumerate(ats):
                 new = value[i * tall : (i + 1) * tall]
                 if s > 0:
@@ -267,7 +296,8 @@
             return
         high = vh[s, :, pl.ds(start, BLOCK)]
         low = vl[s, :, pl.ds(start, BLOCK)]
-        new = mm(high, wc_ref[s]) + mm(low, wc_ref[s]) + mm(high, wl_ref[s])
+        band = slice(s * BLOCK, (s + 1) * BLOCK)
+        new = mm(high, wc_ref[band]) + mm(low, wc_ref[band]) + mm(high, wl_ref[band])
         if s > 1:
             d = new - lev[:, cols + 2 * LANES :]
             emit(s - 1, 0, jnp.where(is_left, 0.0, d[:, :LANES]))
@@ -278,14 +308,12 @@
     return seam
 
 
-def inner_kernel(own_ref, lh_hbm, wc_hbm, wl_hbm, we_hbm, cw_hbm, lt_hbm,
-                 dog_ref, hess_ref, rim_ref, wc_ref, wl_ref, we_ref, cw_ref, lt_ref,
-                 lh_ref, vh, vl, lev, d1, d2, sems):
-    far = (lh_hbm, wc_hbm, wl_hbm, we_hbm, cw_hbm, lt_hbm)
-    near = (lh_ref, wc_ref, wl_ref, we_ref, cw_ref, lt_ref)
-    copies = [pltpu.make_async_copy(f, n, sems.at[i]) for i, (f, n) in enumerate(zip(far, near))]
-    for copy in copies:
-        copy.start()
+def band_refs(late_ref):
+    size = LEVELS * BLOCK
+    return [late_ref.at[i * size : (i + 1) * size] for i in range(3)]
+
+
+def inner_kernel(own_ref, late_ref, dog_ref, hess_ref, rim_ref, vh, vl, lev, d1, d2):
     _, rows, cols = dog_ref.shape
     _, col = mesh_place()
     is_left = col == 0
@@ -296,7 +324,7 @@
 
     def rows_of(part):
         own = own_ref[:, part]
-        return mm(lh_ref[...], jnp.concatenate([own, own[:rows]], axis=0))
+        return mm(lh, jnp.concatenate([own, own[:rows]], axis=0))
 
     def emit(k, at, d):
         to = slice(at, at + d.shape[1])
@@ -314,16 +342,15 @@
 
         hess_tiles(diffs[m + 1], RIM, mid_rows, first, count, 5000.0, put)
 
-    copies[0].wait()
+    first = 3 * LEVELS * BLOCK
+    lh = late_ref[first : first + LEVELS * tall, : 3 * rows]
     place_rows(vh, vl, rows_of, cols, is_left)
-    for copy in copies[1:]:
-        copy.wait()
-    w_refs = (wc_ref, wl_ref, we_ref)
+    w_refs = band_refs(late_ref)
     seam = seam_filter(vh, vl, w_refs, cols, lev, is_left, emit)
     filter_columns(vh, vl, w_refs, 4, cols, lev, emit, after_group, seam)
 
 
-def outer_kernel(last_row, even_ref, odd_ref, lt_ref, wc_ref, wl_ref, we_ref, rim_ref, dog_in, hess_in,
+def outer_kernel(last_row, even_ref, odd_ref, late_ref, rim_ref, dog_in, hess_in,
                  dog_ref, hess_ref, vh, vl, lev, d1, d2):
     _, rows, cols = dog_ref.shape
     row, col = mesh_place()
@@ -335,9 +362,9 @@
     def rows_of(part):
         a, b = even_ref[:, part], odd_ref[:, part]
         bot, top = jnp.where(even, a, b), jnp.where(even, b, a)
-        lows = jnp.concatenate([bot[NEAR : NEAR + 8], top[NEAR + 8 :]], axis=0)
-        again = jnp.concatenate([bot[:8], top[8:NEAR]], axis=0)
-        return mm(lt_ref[...], jnp.concatenate([top[:NEAR], bot[:NEAR], lows, again], axis=0))
+        ends = jnp.concatenate([top[16:], bot[16:]], axis=0)
+        stack = jnp.concatenate([top[:16], bot[:16], ends], axis=0)
+        return mm(lt, jnp.concatenate([stack, stack], axis=0))
 
     def emit(k, at, d):
         to = slice(at, at + d.shape[1])
@@ -367,13 +394,15 @@
 
             hess_tiles(diffs[m + 1], top, RIM, first, count, 5000.0, put)
 
+    first = 3 * LEVELS * BLOCK + LEVELS * (rows + 2 * PAD)
+    lt = late_ref[first : first + LEVELS * 2 * RIM, : 4 * MESSAGE]
     place_rows(vh, vl, rows_of, cols, is_left)
-    w_refs = (wc_ref, wl_ref, we_ref)
+    w_refs = band_refs(late_ref)
     seam = seam_filter(vh, vl, w_refs, cols, lev, is_left, emit)
     filter_columns(vh, vl, w_refs, 8, cols, lev, emit, after_group, seam)
 
 
-def coarse_kernel(last_row, keep_ref, other_ref, fine_dog_ref, fine_hess_ref, lh_ref, wc_ref, wl_ref, we_ref,
+def coarse_kernel(last_row, keep_ref, other_ref, fine_dog_ref, fine_hess_ref, late_ref,
                   fine_dog_hbm, fine_hess_hbm, dog_hbm, hess_hbm,
                   dog_ref, hess_ref, vh, vl, lev, d1, d2, sems):
     fine_copies = [
@@ -398,12 +427,19 @@
         d[:, :LANES] = zero
         d[:, LANES + cols :] = zero
 
+    strip_rows = keep_ref.shape[0]
+    lh = late_ref[late_ref.shape[0] - LEVELS * tall :, : 3 * strip_rows]
     for at in range(0, cols, BLOCK):
         source = slice(at % half, at % half + BLOCK)
         first = is_left if at < half else jnp.logical_not(is_left)
-        high, low = split(jnp.where(first, keep_ref[:, source], other_ref[:, source]))
+        value = jnp.where(first, keep_ref[:, source], other_ref[:, source])
+        if at in (half - BLOCK, half):
+            extra = jnp.where(first, other_ref[:, half:], keep_ref[:, half:])
+            none = jnp.zeros(extra.shape, F32)
+            value = value + jnp.concatenate([none, extra] if at < half else [extra, none], axis=1)
+        high, low = split(value)
         stack = jnp.concatenate([high, low, high], axis=0)
-        value = mm(lh_ref[...], stack)
+        value = mm(lh, stack)
         to = slice(LANES + at, LANES + at + BLOCK)
         for s in range(LEVELS):
             vh[s, :, to], vl[s, :, to] = split(value[s * tall : (s + 1) * tall])
@@ -422,7 +458,7 @@
 
         hess_tiles(diffs[m + 1], 0, rows, first, count, 200000.0, put)
 
-    filter_columns(vh, vl, (wc_ref, wl_ref, we_ref), 8, cols, lev, emit, after_group, lambda s: None)
+    filter_columns(vh, vl, band_refs(late_ref), 8, cols, lev, emit, after_group, lambda s: None)
     copies = [
         pltpu.make_async_copy(dog_ref, dog_hbm, sems.at[2]),
         pltpu.make_async_copy(hess_ref, hess_hbm, sems.at[3]),
@@ -435,16 +471,18 @@
 
 def fine_constants(rows):
     own = np.arange(rows)
-    top, bot = np.arange(-NEAR, 0), rows + np.arange(NEAR)
-    nowhere = -1000
-    lows = np.full(NEAR, nowhere)
-    lows[:LOW] = bot[:LOW]
-    lows[NEAR - LOW :] = top[NEAR - LOW :]
-    again = np.concatenate([bot[:8], top[8:]])
     own_inputs = np.concatenate([own, own, own])
     own_low = np.arange(3 * rows) >= 2 * rows
-    far_inputs = np.concatenate([top, bot, lows, again])
-    far_low = np.arange(4 * NEAR) >= 3 * NEAR
+    nowhere = -1000
+    top = np.full(MESSAGE, nowhere)
+    top[: NEAR + 1] = np.append(np.arange(-NEAR, 0), -1)
+    bot = np.full(MESSAGE, nowhere)
+    bot[: NEAR + 1] = rows + np.append(np.arange(NEAR), 0)
+    inputs = np.concatenate([top[:16], bot[:16], top[16:], bot[16:]])
+    again = inputs.copy()
+    again[[NEAR, 16 + NEAR]] = nowhere
+    far_inputs = np.concatenate([inputs, again])
+    far_low = np.arange(4 * MESSAGE) >= 2 * MESSAGE
 
     def matrix(sigma, centres, valid, inputs, use_low):
         high, low = two_parts(row_matrix(sigma, centres, inputs) * valid[:, None])
@@ -473,6 +511,12 @@
     return np.concatenate(parts)
 
 
+def joined(matrices):
+    return np.concatenate(
+        [np.pad(m.reshape(-1, m.shape[-1]).astype(np.float32), ((0, 0), (0, BLOCK - m.shape[-1]))) for m in matrices]
+    ).astype(BF16)
+
+
 def vmem_specs(count):
     return [pl.BlockSpec(memory_space=pltpu.VMEM) for _ in range(count)]
 
@@ -496,7 +540,6 @@
 def local(image):
     rows, cols = image.shape
     row_count = lax.axis_size("row")
-    col = lax.axis_index("col")
     strip = rows // 4
     wide = cols + LANES
     tall = rows + 2 * PAD
@@ -505,40 +548,44 @@
     cw = coarse_constants(strip, strip_rows)
     bands = [column_weights(s, 1) for s in SIGMAS]
     wc, wl, we = (np.stack([b[i] for b in bands]) for i in range(3))
-    early = [far(c) for c in (bm, *column_weights(SIGMAS[-1], 2))]
-    late = [far(c) for c in (lh, wc, wl, we, cw, lt)]
-
-    side = jnp.where(col == 0, image[:, cols - LANES :], image[:, :LANES])
-    side = lax.ppermute(side, "col", [(0, 1), (1, 0)])
-    own, bm, dc, dl, de = pl.pallas_call(
+    early = far(joined([bm, *column_weights(SIGMAS[-1], 2)]))
+    late = jnp.asarray(joined([wc, wl, we, lh, lt, cw]))
+    base_rows = bm.shape[0]
+    own_shape = jax.ShapeDtypeStruct((2 * rows, wide), BF16)
+    message = jax.ShapeDtypeStruct((MESSAGE, wide), BF16)
+
+    own, side, early = pl.pallas_call(
         pack_kernel,
-        out_shape=(jax.ShapeDtypeStruct((2 * rows, wide), BF16), *(like(c) for c in early)),
-        in_specs=far_specs(1 + len(early)),
-        out_specs=tuple(vmem_specs(1 + len(early))),
-        scratch_shapes=[pltpu.VMEM((rows, cols), F32), pltpu.SemaphoreType.DMA((1 + len(early),))],
+        out_shape=(own_shape, jax.ShapeDtypeStruct((rows, LANES), F32), like(early)),
+        in_specs=far_specs(2),
+        out_specs=tuple(vmem_specs(3)),
+        scratch_shapes=[pltpu.VMEM((rows, cols), F32), pltpu.SemaphoreType.DMA((2,))],
         compiler_params=limit(4),
         name="pack",
-    )(far(image), *early)
-    message = jax.ShapeDtypeStruct((2 * NEAR, wide), BF16)
-    base_rows = bm.shape[0]
-    own, to_even, to_odd, base = pl.pallas_call(
+    )(far(image), early)
+    side = lax.ppermute(side, "col", [(0, 1), (1, 0)])
+    to_even, to_odd, base = pl.pallas_call(
         send_kernel,
-        out_shape=(
-            jax.ShapeDtypeStruct((2 * rows, wide), BF16),
-            message,
-            message,
-            jax.ShapeDtypeStruct((base_rows, cols // 2), F32),
-        ),
-        in_specs=vmem_specs(6),
-        out_specs=tuple(vmem_specs(4)),
+        out_shape=(message, message, jax.ShapeDtypeStruct((base_rows, cols // 2 + LANES), F32)),
+        in_specs=vmem_specs(2),
+        out_specs=tuple(vmem_specs(3)),
         scratch_shapes=[
             pltpu.VMEM((base_rows, cols + 2 * LANES), BF16),
             pltpu.VMEM((base_rows, cols + 2 * LANES), BF16),
         ],
-        input_output_aliases={1: 0},
         compiler_params=limit(6),
+        cost_estimate=pl.CostEstimate(flops=10**9, bytes_accessed=10**6, transcendentals=0),
         name="send",
-    )(side, own, bm, dc, dl, de)
+    )(own, early)
+    own, to_even, to_odd = pl.pallas_call(
+        side_kernel,
+        out_shape=(own_shape, message, message),
+        in_specs=vmem_specs(4),
+        out_specs=tuple(vmem_specs(3)),
+        input_output_aliases={1: 0, 2: 1, 3: 2},
+        compiler_params=limit(4),
+        name="side",
+    )(side, own, to_even, to_odd)
 
     def swap(value, first):
         pairs = [(i, i + 1) for i in range(first, row_count - 1, 2)]
@@ -566,54 +613,46 @@
         ]
 
     rim_tall = RIM + 2 * PAD
-    dog_fine, hess_fine, rim, wc, wl, we, cw, lt = pl.pallas_call(
+    dog_fine, hess_fine, rim = pl.pallas_call(
         inner_kernel,
-        out_shape=(
-            *fine_shapes,
-            jax.ShapeDtypeStruct((4, 2 * rim_tall, cols + 2 * LANES), F32),
-            *(like(c) for c in late[1:]),
-        ),
-        in_specs=vmem_specs(1) + far_specs(len(late)),
-        out_specs=tuple(vmem_specs(3 + len(late) - 1)),
-        scratch_shapes=[
-            pltpu.VMEM(late[0].shape, late[0].dtype),
-            *scratch(tall, tall, BLOCK),
-            pltpu.SemaphoreType.DMA((len(late),)),
-        ],
+        out_shape=(*fine_shapes, jax.ShapeDtypeStruct((4, 2 * rim_tall, cols + 2 * LANES), F32)),
+        in_specs=vmem_specs(2),
+        out_specs=tuple(vmem_specs(3)),
+        scratch_shapes=scratch(tall, tall, BLOCK),
         compiler_params=limit(18),
         cost_estimate=pl.CostEstimate(flops=2 * 10**9, bytes_accessed=10**7, transcendentals=0),
         name="inner",
-    )(own, *late)
+    )(own, late)
 
     keep, send = pl.pallas_call(
         functools.partial(base_kernel, row_count, rows // 2),
         out_shape=(
-            jax.ShapeDtypeStruct((strip_rows, cols // 2), F32),
-            jax.ShapeDtypeStruct((strip_rows, cols // 2), F32),
+            jax.ShapeDtypeStruct((strip_rows, cols // 2 + LANES), F32),
+            jax.ShapeDtypeStruct((strip_rows, cols // 2 + LANES), F32),
         ),
         in_specs=vmem_specs(3) + [pl.BlockSpec(memory_space=pl.ANY)],
         out_specs=tuple(vmem_specs(2)),
         scratch_shapes=[pltpu.VMEM((base_rows, LANES), F32)],
         compiler_params=limit(4),
         name="base",
-    )(base, even, odd, cw)
+    )(base, even, odd, rim)
     other = lax.ppermute(send, "col", [(0, 1), (1, 0)])
     dog_fine, hess_fine = pl.pallas_call(
         functools.partial(outer_kernel, row_count - 1),
         out_shape=fine_shapes,
-        in_specs=vmem_specs(9),
+        in_specs=vmem_specs(6),
         out_specs=tuple(vmem_specs(2)),
         scratch_shapes=scratch(2 * rim_tall, 2 * RIM, BLOCK),
-        input_output_aliases={7: 0, 8: 1},
+        input_output_aliases={4: 0, 5: 1},
         compiler_params=limit(14),
         cost_estimate=pl.CostEstimate(flops=10**9, bytes_accessed=10**6, transcendentals=0),
         name="outer",
-    )(even, odd, lt, wc, wl, we, rim, dog_fine, hess_fine)
+    )(even, odd, late, rim, dog_fine, hess_fine)
 
     return pl.pallas_call(
         functools.partial(coarse_kernel, row_count - 1),
         out_shape=fine_shapes + coarse_shapes,
-        in_specs=vmem_specs(8),
+        in_specs=vmem_specs(5),
         out_specs=tuple(far_specs(4)),
         scratch_shapes=[
             pltpu.VMEM((4, strip, cols), BF16),
@@ -623,7 +662,7 @@
         ],
         compiler_params=limit(12),
         name="coarse",
-    )(keep, other, dog_fine, hess_fine, cw, wc, wl, we)
+    )(keep, other, dog_fine, hess_fine, late)
 
 
 def solution(mesh):

time: 19.1 us -> 17.8 us (0.932)
  other arithmetic: 0.78 us -> 0 us
  Pallas kernels: 10.4 us -> 9.64 us
  starting transfers between devices: 5.18 us -> 5.52 us
    pallas_call x1, Pallas kernels: 3.91 us -> 2.95 us  [local(): pl.pallas_call(inner_kernel, out_shape=(*fine_shapes, jax.ShapeDtypeStruc...]
    select_n x1 -> x0, other arithmetic: 0.78 us -> none  [local(): side = jnp.where(col == 0, image[:, cols - LANES:], image[:, :LANES])]
    ppermute x1, starting transfers between devices: 1.19 us -> 1.47 us  [local(): other = lax.ppermute(send, 'col', [(0, 1), (1, 0)])]
    pallas_call x2 -> x3, Pallas kernels: 2.21 us -> 2.22 us  [the longest x1 1.28 us: local(): pl.pallas_call(pack_kernel, out_shape=(own_shape, jax.ShapeDtypeStruct((r...]
  transfers between devices with their start and end apart: 4 -> 4, of which waited for: 1 -> 1; matrix products, arithmetic and copies ran while one was open for 0% -> 0% of each run, Pallas kernels for 36% -> 27%
where the time goes in v5:
time: 17.8 us; the launch traced here: 17.6 us
  Pallas kernels  9.64 us (54%)
  starting transfers between devices  5.52 us (31%)
  waiting for transfers between devices  1.74 us (10%)
  between operations  0.71 us (4%)
    ppermute x2, starting transfers between devices, swap(): return lax.ppermute(value, 'row', pairs + [(j, i) for i, j in pairs])  3.31 us
    pallas_call x1, Pallas kernels, local(): pl.pallas_call(inner_kernel, out_shape=(*fine_shapes, jax.ShapeDtypeStruc...  2.95 us
    pallas_call x1, Pallas kernels, local(): pl.pallas_call(functools.partial(coarse_kernel, row_count - 1), out_shape...  2.58 us
    pallas_call x1, Pallas kernels, local(): pl.pallas_call(functools.partial(outer_kernel, row_count - 1), out_shape=...  1.75 us
    ppermute x2, waiting for transfers between devices, swap(): return lax.ppermute(value, 'row', pairs + [(j, i) for i, j in pairs])  1.73 us
    ppermute x1, starting transfers between devices, local(): other = lax.ppermute(send, 'col', [(0, 1), (1, 0)])  1.47 us
    pallas_call x1, Pallas kernels, local(): pl.pallas_call(pack_kernel, out_shape=(own_shape, jax.ShapeDtypeStruct((r...  1.28 us
    pallas_call x1, Pallas kernels, local(): pl.pallas_call(send_kernel, out_shape=(message, message, jax.ShapeDtypeSt...  0.92 us
  transfers between devices with their start and end apart: 4, of which 1 were waited for; matrix products, arithmetic and copies ran while one was open for 0% of the time, Pallas kernels for 27%

profile of v5, /device:TPU:11, one launch (start us, length us, event | category | flops | bytes accessed | tf_op | source)
XLA Modules:
  0.0 17.6 jit_solution(8758439930428687153)
XLA Ops:
  0.6 1.3 %pack.1 = (bf16[128,2176]{1,0:T(8,128)(2,1)S(1)}, f32[64,128]{1,0:T(8,128)S(1)}, bf16[1344,256]{1,0:T(8,128)(2,1)S(1)}) custom-call(f32[64,2048]{1,0:T(8,128)} %x_hbm.1, bf16[1344,256]{1,0:T(8,128)(2,1)} %constant.4.clone.early_hbm), custom_call_target="tpu_custom_call" | custom-call | tf_op jit(solution)/shard_map/pack/pallas_call | solution.py:557
  1.9 0.0 copy-start
  1.9 0.7 %collective-permute-start = (f32[64,128]{1,0:T(8,128)S(1)}, f32[64,128]{1,0:T(8,128)S(1)}, u32[]{:S(2)}, u32[]{:S(2)}) collective-permute-start(f32[64,128]{1,0:T(8,128)S(1)} %get-tuple-element.23), channel_id=1, source_target_pairs={{0,1},{1,0},{2,3},{3,2},{4,5},{5,4},{6,7},{7,6},{8,9},{9,8},{10,11... | collective-permute-start | bytes 98312 | tf_op jit(solution)/shard_map/ppermute | solution.py:566
  2.7 0.9 %send.1 = (bf16[24,2176]{1,0:T(8,128)(2,1)S(1)}, bf16[24,2176]{1,0:T(8,128)(2,1)S(1)}, f32[64,1152]{1,0:T(8,128)S(1)}) custom-call(bf16[128,2176]{1,0:T(8,128)(2,1)S(1)} %get-tuple-element.20.own_ref.own_in, bf16[1344,256]{1,0:T(8,128)(2,1)S(1)} %get-tuple-element.21.early_ref), custom_call_target="tpu_custom_call" | custom-call | flops 1000000000 | bytes 1000000 | tf_op jit(solution)/shard_map/send/pallas_call | solution.py:567
  3.6 0.0 collective-permute-done.side_ref
  3.6 1.3 %collective-permute-start.1 = (bf16[24,2176]{1,0:T(8,128)(2,1)S(1)}, bf16[24,2176]{1,0:T(8,128)(2,1)S(1)}, u32[]{:S(2)}, u32[]{:S(2)}) collective-permute-start(bf16[24,2176]{1,0:T(8,128)(2,1)S(1)} %get-tuple-element.26), channel_id=1, source_target_pairs={{0,2},{4,6},{8,10},{12,14},{2,0},{6,4},{10,8},{14,12},{1,3},{5,7},... | collective-permute-start | bytes 313352 | tf_op jit(solution)/shard_map/ppermute | solution.py:592
  4.9 2.0 %collective-permute-start.2 = (bf16[24,2176]{1,0:T(8,128)(2,1)S(1)}, bf16[24,2176]{1,0:T(8,128)(2,1)S(1)}, u32[]{:S(2)}, u32[]{:S(2)}) collective-permute-start(bf16[24,2176]{1,0:T(8,128)(2,1)S(1)} %get-tuple-element.27), channel_id=1, source_target_pairs={{2,4},{6,8},{10,12},{4,2},{8,6},{12,10},{3,5},{7,9},{11,13},{5,3},... | collective-permute-start | bytes 313352 | tf_op jit(solution)/shard_map/ppermute | solution.py:592
  7.0 0.0 copy-done
  7.0 2.9 %inner.1 = (bf16[4,64,2048]{2,1,0:T(8,128)(2,1)S(1)}, bf16[2,64,2048]{2,1,0:T(8,128)(2,1)S(1)}, f32[4,64,2304]{2,1,0:T(8,128)S(1)}) custom-call(bf16[128,2176]{1,0:T(8,128)(2,1)S(1)} %get-tuple-element.28.own_ref, bf16[4560,256]{1,0:T(8,128)(2,1)S(1)} %copy-done), custom_call_target="tpu_custom_call" | custom-call | flops 2000000000 | bytes 10000000 | tf_op jit(solution)/shard_map/inner/pallas_call | solution.py:616
  9.9 0.0 collective-permute-done.1.even_ref
  9.9 1.7 %collective-permute-done.2.odd_ref = bf16[24,2176]{1,0:T(8,128)(2,1)S(1)} collective-permute-done((bf16[24,2176]{1,0:T(8,128)(2,1)S(1)}, bf16[24,2176]{1,0:T(8,128)(2,1)S(1)}, u32[]{:S(2)}, u32[]{:S(2)}) %collective-permute-start.2) | collective-permute-done | bytes 104480 | tf_op jit(solution)/shard_map/ppermute | solution.py:592
  11.7 0.1 base.1
  11.8 1.5 %collective-permute-start.3 = (f32[48,1152]{1,0:T(8,128)S(1)}, f32[48,1152]{1,0:T(8,128)S(1)}, u32[]{:S(2)}, u32[]{:S(2)}) collective-permute-start(f32[48,1152]{1,0:T(8,128)S(1)} %get-tuple-element.31), channel_id=1, source_target_pairs={{0,1},{1,0},{2,3},{3,2},{4,5},{5,4},{6,7},{7,6},{8,9},{9,8},{10,11... | collective-permute-start | bytes 663560 | tf_op jit(solution)/shard_map/ppermute | solution.py:639
  13.3 1.8 %outer.1 = (bf16[4,64,2048]{2,1,0:T(8,128)(2,1)S(1)}, bf16[2,64,2048]{2,1,0:T(8,128)(2,1)S(1)}) custom-call(bf16[24,2176]{1,0:T(8,128)(2,1)S(1)} %collective-permute-done.1.even_ref, bf16[24,2176]{1,0:T(8,128)(2,1)S(1)} %collective-permute-done.2.odd_ref, bf16[4560,256]{1,0:T(8,128)(2,1)S(1)} %copy-done, ...), custom_call_target="tpu_custom_call", output_to_operand_aliasing={{0}: (4, {}), {1}: (5, {})} | custom-call | flops 1000000000 | bytes 1000000 | tf_op jit(solution)/shard_map/outer/pallas_call | solution.py:640
  15.0 0.0 collective-permute-done.3.other_ref
  15.0 2.6 %coarse.1 = (bf16[4,64,2048]{2,1,0:T(8,128)(2,1)}, bf16[2,64,2048]{2,1,0:T(8,128)(2,1)}, bf16[4,16,2048]{2,1,0:T(8,128)(2,1)}, bf16[2,16,2048]{2,1,0:T(8,128)(2,1)}) custom-call(f32[48,1152]{1,0:T(8,128)S(1)} %get-tuple-element.30.keep_ref, f32[48,1152]{1,0:T(8,128)S(1)} %collective-permute-done.3.other_ref, ...), custom_call_target="tpu_custom_call" | custom-call | tf_op jit(solution)/shard_map/coarse/pallas_call | solution.py:652
  (1 shorter events, 0.0 us)
Async XLA Ops:
  1.9 5.0 %copy-start = (bf16[4560,256]{1,0:T(8,128)(2,1)S(1)}, bf16[4560,256]{1,0:T(8,128)(2,1)}, u32[]{:S(2)}) copy-start(bf16[4560,256]{1,0:T(8,128)(2,1)} %constant.5.clone.late_ref) | copy-start | bytes 7004164
  1.9 1.7 %collective-permute-start = (f32[64,128]{1,0:T(8,128)S(1)}, f32[64,128]{1,0:T(8,128)S(1)}, u32[]{:S(2)}, u32[]{:S(2)}) collective-permute-start(f32[64,128]{1,0:T(8,128)S(1)} %get-tuple-element.23), channel_id=1, source_target_pairs={{0,1},{1,0},{2,3},{3,2},{4,5},{5,4},{6,7},{7,6},{8,9},{9,8},{10,11... | collective-permute-start | bytes 98312 | tf_op jit(solution)/shard_map/ppermute | solution.py:566
  3.6 6.3 %collective-permute-start.1 = (bf16[24,2176]{1,0:T(8,128)(2,1)S(1)}, bf16[24,2176]{1,0:T(8,128)(2,1)S(1)}, u32[]{:S(2)}, u32[]{:S(2)}) collective-permute-start(bf16[24,2176]{1,0:T(8,128)(2,1)S(1)} %get-tuple-element.26), channel_id=1, source_target_pairs={{0,2},{4,6},{8,10},{12,14},{2,0},{6,4},{10,8},{14,12},{1,3},{5,7},... | collective-permute-start | bytes 313352 | tf_op jit(solution)/shard_map/ppermute | solution.py:592
  4.9 6.7 %collective-permute-start.2 = (bf16[24,2176]{1,0:T(8,128)(2,1)S(1)}, bf16[24,2176]{1,0:T(8,128)(2,1)S(1)}, u32[]{:S(2)}, u32[]{:S(2)}) collective-permute-start(bf16[24,2176]{1,0:T(8,128)(2,1)S(1)} %get-tuple-element.27), channel_id=1, source_target_pairs={{2,4},{6,8},{10,12},{4,2},{8,6},{12,10},{3,5},{7,9},{11,13},{5,3},... | collective-permute-start | bytes 313352 | tf_op jit(solution)/shard_map/ppermute | solution.py:592
  11.8 3.2 %collective-permute-start.3 = (f32[48,1152]{1,0:T(8,128)S(1)}, f32[48,1152]{1,0:T(8,128)S(1)}, u32[]{:S(2)}, u32[]{:S(2)}) collective-permute-start(f32[48,1152]{1,0:T(8,128)S(1)} %get-tuple-element.31), channel_id=1, source_target_pairs={{0,1},{1,0},{2,3},{3,2},{4,5},{5,4},{6,7},{7,6},{8,9},{9,8},{10,11... | collective-permute-start | bytes 663560 | tf_op jit(solution)/shard_map/ppermute | solution.py:639

commit v6 on v5

--- a/solution.py
+++ b/solution.py
@@ -46,8 +46,8 @@
 
 
 def column_weights(sigma, step):
-    width = BLOCK * step
-    out = np.arange(BLOCK)[None, :] * step
+    width = BLOCK
+    out = np.arange(BLOCK // step)[None, :] * step
     high, low = two_parts(tap_at(sigma, np.arange(width)[:, None] - out + REACH))
     lane = np.arange(LANES)[:, None]
     right = np.where(lane < REACH, tap_at(sigma, width + lane - out + REACH), 0.0)
@@ -70,11 +70,11 @@
 
 def edge_pair(high_left, high_right, low_left, low_right):
     lane = lax.broadcasted_iota(jnp.int32, high_left.shape, 1)
-    eh = jnp.where(lane < LANES // 2, high_right.astype(F32), high_left.astype(F32))
-    el = jnp.where(lane < LANES // 2, low_right.astype(F32), low_left.astype(F32))
-    again = pltpu.roll(eh, 32, 1)
+    eh = jnp.where(lane < LANES // 2, high_right, high_left)
+    el = jnp.where(lane < LANES // 2, low_right, low_left)
+    again = pltpu.roll(eh.astype(F32), 32, 1).astype(BF16)
     eh = jnp.where((lane >= 16) & (lane < 64), again, eh)
-    return jnp.concatenate([eh.astype(BF16), el.astype(BF16)], axis=1)
+    return jnp.concatenate([eh, el], axis=1)
 
 
 def edge_columns(high, low, at, width):
@@ -84,24 +84,31 @@
 
 def hess_tiles(d, top, rows, first_tile, count, gain, put):
     tall = rows + 2 * PAD
-    lane = lax.broadcasted_iota(jnp.int32, (tall, LANES), 1)
-    tile = lambda t: d[top : top + tall, (first_tile + t + 1) * LANES : (first_tile + t + 2) * LANES]
-    tiles = {-1: tile(-1), 0: tile(0)}
-    back = {t: pltpu.roll(tiles[t], 1, 1) for t in (-1, 0)}
-    ahead = {0: pltpu.roll(tiles[0], LANES - 1, 1)}
+    lane = lax.broadcasted_iota(jnp.int32, (rows, LANES), 1)
+    mid, slope, total = {}, {}, {}
+    back, ahead = {}, {}
+
+    def load(t):
+        lanes = slice((first_tile + t + 1) * LANES, (first_tile + t + 2) * LANES)
+        value = d[top : top + tall, lanes]
+        up, down = pltpu.roll(value, 1, 0)[PAD : PAD + rows], pltpu.roll(value, tall - 1, 0)[PAD : PAD + rows]
+        mid[t] = value[PAD : PAD + rows]
+        slope[t], total[t] = down - up, up + down
+        if t < count:
+            back[t] = [pltpu.roll(v, 1, 1) for v in (mid[t], slope[t])]
+        if t >= 0:
+            ahead[t] = [pltpu.roll(v, LANES - 1, 1) for v in (mid[t], slope[t])]
+
+    load(-1)
+    load(0)
     for t in range(count):
-        tiles[t + 1] = tile(t + 1)
-        back[t + 1] = pltpu.roll(tiles[t + 1], 1, 1)
-        ahead[t + 1] = pltpu.roll(tiles[t + 1], LANES - 1, 1)
-        before = jnp.where(lane == 0, back[t - 1], back[t])
-        after = jnp.where(lane == LANES - 1, ahead[t + 1], ahead[t])
-        across = after - before
-        mid = slice(PAD, PAD + rows)
-        up, down = pltpu.roll(tiles[t], 1, 0)[mid], pltpu.roll(tiles[t], tall - 1, 0)[mid]
-        twice = 2.0 * tiles[t][mid]
-        dxx = after[mid] + before[mid] - twice
-        dyy = up + down - twice
-        dxy = (pltpu.roll(across, tall - 1, 0)[mid] - pltpu.roll(across, 1, 0)[mid]) * 0.25
+        load(t + 1)
+        before = [jnp.where(lane == 0, a, b) for a, b in zip(back[t - 1], back[t])]
+        after = [jnp.where(lane == LANES - 1, a, b) for a, b in zip(ahead[t + 1], ahead[t])]
+        twice = 2.0 * mid[t]
+        dxx = after[0] + before[0] - twice
+        dyy = total[t] - twice
+        dxy = (after[1] - before[1]) * 0.25
         put(first_tile + t, (gain * (dxx * dyy - dxy * dxy)).astype(BF16))
 
 
@@ -109,18 +116,15 @@
     return lax.axis_index("row"), lax.axis_index("col")
 
 
-def pack_kernel(x_hbm, early_hbm, own_ref, side_ref, early_ref, x_ref, sems):
+def pack_kernel(x_hbm, early_hbm, x_ref, side_ref, early_ref, sems):
     copy = pltpu.make_async_copy(x_hbm, x_ref, sems.at[0])
     constants = pltpu.make_async_copy(early_hbm, early_ref, sems.at[1])
     copy.start()
     constants.start()
     _, col = mesh_place()
-    rows, cols = x_ref.shape
+    cols = x_ref.shape[1]
     copy.wait()
     side_ref[...] = jnp.where(col == 0, x_ref[:, cols - LANES :], x_ref[:, :LANES])
-    for at in range(0, cols, BLOCK):
-        to = slice(at, at + BLOCK)
-        own_ref[:rows, to], own_ref[rows:, to] = split(x_ref[:, to])
     constants.wait()
 
 
@@ -134,42 +138,43 @@
     return up, down
 
 
-def send_kernel(own_ref, early_ref, even_ref, odd_ref, base_ref, bvh, bvl):
+def send_kernel(x_ref, early_ref, own_ref, even_ref, odd_ref, base_ref, bvh, bvl):
     row, col = mesh_place()
-    rows = own_ref.shape[0] // 2
-    cols = own_ref.shape[1] - LANES
+    rows, cols = x_ref.shape
     half = cols // 2
     base_rows = base_ref.shape[0]
     is_left = col == 0
     even = row % 2 == 0
     bm = early_ref[:base_rows, : 3 * rows]
-    dc = early_ref[base_rows : base_rows + 2 * BLOCK]
-    dl = early_ref[base_rows + 2 * BLOCK : base_rows + 4 * BLOCK]
-    de = early_ref[base_rows + 4 * BLOCK :]
+    dc, dl, de = (early_ref[base_rows + i * BLOCK : base_rows + (i + 1) * BLOCK, : BLOCK // 2] for i in range(3))
 
     zero = jnp.zeros((base_rows, LANES), BF16)
     for ref in (bvh, bvl):
         ref[:, :LANES] = zero
         ref[:, LANES + cols :] = zero
     for at in range(0, cols, BLOCK):
-        own = own_ref[:, at : at + BLOCK]
-        value = mm(bm, jnp.concatenate([own, own[:rows]], axis=0))
+        high, low = split(x_ref[:, at : at + BLOCK])
+        own_ref[:rows, at : at + BLOCK] = high
+        own_ref[rows:, at : at + BLOCK] = low
+        value = mm(bm, jnp.concatenate([high, low, high], axis=0))
         to = slice(LANES + at, LANES + at + BLOCK)
         bvh[:, to], bvl[:, to] = split(value)
-    for j in range(cols // (2 * BLOCK)):
-        at = LANES + 2 * BLOCK * j
-        high = bvh[:, at : at + 2 * BLOCK]
-        low = bvl[:, at : at + 2 * BLOCK]
-        edge = edge_columns(bvh, bvl, at, 2 * BLOCK)
-        base_ref[:, j * BLOCK : (j + 1) * BLOCK] = mm(high, dc) + mm(low, dc) + mm(high, dl) + mm(edge, de)
     first, last = slice(LANES, 2 * LANES), slice(cols, cols + LANES)
-    none = jnp.zeros((base_rows, LANES), BF16)
     pick = lambda ref: (
-        jnp.where(is_left, ref[:, last].astype(F32), 0.0),
-        jnp.where(is_left, 0.0, ref[:, first].astype(F32)),
+        jnp.where(is_left, ref[:, last].astype(F32), 0.0).astype(BF16),
+        jnp.where(is_left, 0.0, ref[:, first].astype(F32)).astype(BF16),
     )
-    value = mm(edge_pair(*pick(bvh), *pick(bvl)), de)
-    base_ref[:, half:] = jnp.where(is_left, value[:, :LANES], value[:, LANES:])
+    beyond = edge_pair(*pick(bvh), *pick(bvl))
+    group = 4
+    for g in range(0, cols // BLOCK, group):
+        ats = [LANES + BLOCK * (g + i) for i in range(group)]
+        high = jnp.concatenate([bvh[:, at : at + BLOCK] for at in ats], axis=0)
+        low = jnp.concatenate([bvl[:, at : at + BLOCK] for at in ats], axis=0)
+        edge = jnp.concatenate([edge_columns(bvh, bvl, at, BLOCK) for at in ats], axis=0)
+        value = mm(high, dc) + mm(low, dc) + mm(high, dl) + mm(edge, de)
+        for i in range(group):
+            base_ref[:, (g + i) * LANES : (g + i + 1) * LANES] = value[i * base_rows : (i + 1) * base_rows]
+    base_ref[:, half:] = mm(beyond, de)
 
     first_up = REACH + 1 - 6
     first_down = REACH + 1 + SPAN
@@ -511,9 +516,9 @@
     return np.concatenate(parts)
 
 
-def joined(matrices):
+def joined(matrices, columns=BLOCK):
     return np.concatenate(
-        [np.pad(m.reshape(-1, m.shape[-1]).astype(np.float32), ((0, 0), (0, BLOCK - m.shape[-1]))) for m in matrices]
+        [np.pad(m.reshape(-1, m.shape[-1]).astype(np.float32), ((0, 0), (0, columns - m.shape[-1]))) for m in matrices]
     ).astype(BF16)
 
 
@@ -554,21 +559,21 @@
     own_shape = jax.ShapeDtypeStruct((2 * rows, wide), BF16)
     message = jax.ShapeDtypeStruct((MESSAGE, wide), BF16)
 
-    own, side, early = pl.pallas_call(
+    tile, side, early = pl.pallas_call(
         pack_kernel,
-        out_shape=(own_shape, jax.ShapeDtypeStruct((rows, LANES), F32), like(early)),
+        out_shape=(like(image), jax.ShapeDtypeStruct((rows, LANES), F32), like(early)),
         in_specs=far_specs(2),
         out_specs=tuple(vmem_specs(3)),
-        scratch_shapes=[pltpu.VMEM((rows, cols), F32), pltpu.SemaphoreType.DMA((2,))],
+        scratch_shapes=[pltpu.SemaphoreType.DMA((2,))],
         compiler_params=limit(4),
         name="pack",
     )(far(image), early)
     side = lax.ppermute(side, "col", [(0, 1), (1, 0)])
-    to_even, to_odd, base = pl.pallas_call(
+    own, to_even, to_odd, base = pl.pallas_call(
         send_kernel,
-        out_shape=(message, message, jax.ShapeDtypeStruct((base_rows, cols // 2 + LANES), F32)),
+        out_shape=(own_shape, message, message, jax.ShapeDtypeStruct((base_rows, cols // 2 + LANES), F32)),
         in_specs=vmem_specs(2),
-        out_specs=tuple(vmem_specs(3)),
+        out_specs=tuple(vmem_specs(4)),
         scratch_shapes=[
             pltpu.VMEM((base_rows, cols + 2 * LANES), BF16),
             pltpu.VMEM((base_rows, cols + 2 * LANES), BF16),
@@ -576,7 +581,7 @@
         compiler_params=limit(6),
         cost_estimate=pl.CostEstimate(flops=10**9, bytes_accessed=10**6, transcendentals=0),
         name="send",
-    )(own, early)
+    )(tile, early)
     own, to_even, to_odd = pl.pallas_call(
         side_kernel,
         out_shape=(own_shape, message, message),

time: 17.8 us -> 17.5 us (0.983)
  Pallas kernels: 9.64 us -> 9.29 us
    pallas_call x2, Pallas kernels: 2.2 us -> 1.94 us  [the longest x1 1.19 us: local(): pl.pallas_call(pack_kernel, out_shape=(like(image), jax.ShapeDtypeStruct(...]
  transfers between devices with their start and end apart: 4 -> 4, of which waited for: 1 -> 2; matrix products, arithmetic and copies ran while one was open for 0% -> 0% of each run, Pallas kernels for 27% -> 27%
where the time goes in v6:
time: 17.5 us; the launch traced here: 17.4 us
  Pallas kernels  9.29 us (53%)
  starting transfers between devices  5.61 us (32%)
  waiting for transfers between devices  1.79 us (10%)
  between operations  0.71 us (4%)
    ppermute x2, starting transfers between devices, swap(): return lax.ppermute(value, 'row', pairs + [(j, i) for i, j in pairs])  3.31 us
    pallas_call x1, Pallas kernels, local(): pl.pallas_call(inner_kernel, out_shape=(*fine_shapes, jax.ShapeDtypeStruc...  2.92 us
    pallas_call x1, Pallas kernels, local(): pl.pallas_call(functools.partial(coarse_kernel, row_count - 1), out_shape...  2.51 us
    pallas_call x1, Pallas kernels, local(): pl.pallas_call(functools.partial(outer_kernel, row_count - 1), out_shape=...  1.76 us
    ppermute x2, waiting for transfers between devices, swap(): return lax.ppermute(value, 'row', pairs + [(j, i) for i, j in pairs])  1.68 us
    ppermute x1, starting transfers between devices, local(): other = lax.ppermute(send, 'col', [(0, 1), (1, 0)])  1.55 us
    pallas_call x1, Pallas kernels, local(): pl.pallas_call(pack_kernel, out_shape=(like(image), jax.ShapeDtypeStruct(...  1.19 us
    pallas_call x1, Pallas kernels, local(): pl.pallas_call(send_kernel, out_shape=(own_shape, message, message, jax.S...  0.75 us
  transfers between devices with their start and end apart: 4, of which 2 were waited for; matrix products, arithmetic and copies ran while one was open for 0% of the time, Pallas kernels for 27%

profile of v6, /device:TPU:11, one launch (start us, length us, event | category | flops | bytes accessed | tf_op | source)
XLA Modules:
  0.0 17.4 jit_solution(12318801701810613878)
XLA Ops:
  0.6 1.2 %pack.1 = (f32[64,2048]{1,0:T(8,128)S(1)}, f32[64,128]{1,0:T(8,128)S(1)}, bf16[832,256]{1,0:T(8,128)(2,1)S(1)}) custom-call(f32[64,2048]{1,0:T(8,128)} %x_hbm.1, bf16[832,256]{1,0:T(8,128)(2,1)} %constant.4.clone.early_hbm), custom_call_target="tpu_custom_call" | custom-call | tf_op jit(solution)/shard_map/pack/pallas_call | solution.py:562
  1.8 0.0 copy-start
  1.8 0.7 %collective-permute-start = (f32[64,128]{1,0:T(8,128)S(1)}, f32[64,128]{1,0:T(8,128)S(1)}, u32[]{:S(2)}, u32[]{:S(2)}) collective-permute-start(f32[64,128]{1,0:T(8,128)S(1)} %get-tuple-element.24), channel_id=1, source_target_pairs={{0,1},{1,0},{2,3},{3,2},{4,5},{5,4},{6,7},{7,6},{8,9},{9,8},{10,11... | collective-permute-start | bytes 98312 | tf_op jit(solution)/shard_map/ppermute | solution.py:571
  2.6 0.8 %send.1 = (bf16[128,2176]{1,0:T(8,128)(2,1)S(1)}, bf16[24,2176]{1,0:T(8,128)(2,1)S(1)}, bf16[24,2176]{1,0:T(8,128)(2,1)S(1)}, f32[64,1152]{1,0:T(8,128)S(1)}) custom-call(f32[64,2048]{1,0:T(8,128)S(1)} %get-tuple-element.21.x_ref, bf16[832,256]{1,0:T(8,128)(2,1)S(1)} %get-tuple-element.22.early_ref), custom_call_target="tpu_custom_call" | custom-call | flops 1000000000 | bytes 1000000 | tf_op jit(solution)/shard_map/send/pallas_call | solution.py:572
  3.3 0.1 collective-permute-done.side_ref
  3.5 1.3 %collective-permute-start.1 = (bf16[24,2176]{1,0:T(8,128)(2,1)S(1)}, bf16[24,2176]{1,0:T(8,128)(2,1)S(1)}, u32[]{:S(2)}, u32[]{:S(2)}) collective-permute-start(bf16[24,2176]{1,0:T(8,128)(2,1)S(1)} %get-tuple-element.28), channel_id=1, source_target_pairs={{0,2},{4,6},{8,10},{12,14},{2,0},{6,4},{10,8},{14,12},{1,3},{5,7},... | collective-permute-start | bytes 313352 | tf_op jit(solution)/shard_map/ppermute | solution.py:597
  4.8 2.0 %collective-permute-start.2 = (bf16[24,2176]{1,0:T(8,128)(2,1)S(1)}, bf16[24,2176]{1,0:T(8,128)(2,1)S(1)}, u32[]{:S(2)}, u32[]{:S(2)}) collective-permute-start(bf16[24,2176]{1,0:T(8,128)(2,1)S(1)} %get-tuple-element.29), channel_id=1, source_target_pairs={{2,4},{6,8},{10,12},{4,2},{8,6},{12,10},{3,5},{7,9},{11,13},{5,3},... | collective-permute-start | bytes 313352 | tf_op jit(solution)/shard_map/ppermute | solution.py:597
  6.8 0.0 copy-done
  6.8 2.9 %inner.1 = (bf16[4,64,2048]{2,1,0:T(8,128)(2,1)S(1)}, bf16[2,64,2048]{2,1,0:T(8,128)(2,1)S(1)}, f32[4,64,2304]{2,1,0:T(8,128)S(1)}) custom-call(bf16[128,2176]{1,0:T(8,128)(2,1)S(1)} %get-tuple-element.30.own_ref, bf16[4560,256]{1,0:T(8,128)(2,1)S(1)} %copy-done), custom_call_target="tpu_custom_call" | custom-call | flops 2000000000 | bytes 10000000 | tf_op jit(solution)/shard_map/inner/pallas_call | solution.py:621
  9.7 0.0 collective-permute-done.1.even_ref
  9.7 1.7 %collective-permute-done.2.odd_ref = bf16[24,2176]{1,0:T(8,128)(2,1)S(1)} collective-permute-done((bf16[24,2176]{1,0:T(8,128)(2,1)S(1)}, bf16[24,2176]{1,0:T(8,128)(2,1)S(1)}, u32[]{:S(2)}, u32[]{:S(2)}) %collective-permute-start.2) | collective-permute-done | bytes 104480 | tf_op jit(solution)/shard_map/ppermute | solution.py:597
  11.4 0.1 base.1
  11.5 1.6 %collective-permute-start.3 = (f32[48,1152]{1,0:T(8,128)S(1)}, f32[48,1152]{1,0:T(8,128)S(1)}, u32[]{:S(2)}, u32[]{:S(2)}) collective-permute-start(f32[48,1152]{1,0:T(8,128)S(1)} %get-tuple-element.33), channel_id=1, source_target_pairs={{0,1},{1,0},{2,3},{3,2},{4,5},{5,4},{6,7},{7,6},{8,9},{9,8},{10,11... | collective-permute-start | bytes 663560 | tf_op jit(solution)/shard_map/ppermute | solution.py:644
  13.1 1.8 %outer.1 = (bf16[4,64,2048]{2,1,0:T(8,128)(2,1)S(1)}, bf16[2,64,2048]{2,1,0:T(8,128)(2,1)S(1)}) custom-call(bf16[24,2176]{1,0:T(8,128)(2,1)S(1)} %collective-permute-done.1.even_ref, bf16[24,2176]{1,0:T(8,128)(2,1)S(1)} %collective-permute-done.2.odd_ref, bf16[4560,256]{1,0:T(8,128)(2,1)S(1)} %copy-done, ...), custom_call_target="tpu_custom_call", output_to_operand_aliasing={{0}: (4, {}), {1}: (5, {})} | custom-call | flops 1000000000 | bytes 1000000 | tf_op jit(solution)/shard_map/outer/pallas_call | solution.py:645
  14.9 0.0 collective-permute-done.3.other_ref
  14.9 2.5 %coarse.1 = (bf16[4,64,2048]{2,1,0:T(8,128)(2,1)}, bf16[2,64,2048]{2,1,0:T(8,128)(2,1)}, bf16[4,16,2048]{2,1,0:T(8,128)(2,1)}, bf16[2,16,2048]{2,1,0:T(8,128)(2,1)}) custom-call(f32[48,1152]{1,0:T(8,128)S(1)} %get-tuple-element.32.keep_ref, f32[48,1152]{1,0:T(8,128)S(1)} %collective-permute-done.3.other_ref, ...), custom_call_target="tpu_custom_call" | custom-call | tf_op jit(solution)/shard_map/coarse/pallas_call | solution.py:657
  (1 shorter events, 0.0 us)
Async XLA Ops:
  1.8 5.0 %copy-start = (bf16[4560,256]{1,0:T(8,128)(2,1)S(1)}, bf16[4560,256]{1,0:T(8,128)(2,1)}, u32[]{:S(2)}) copy-start(bf16[4560,256]{1,0:T(8,128)(2,1)} %constant.5.clone.late_ref) | copy-start | bytes 7004164
  1.8 1.6 %collective-permute-start = (f32[64,128]{1,0:T(8,128)S(1)}, f32[64,128]{1,0:T(8,128)S(1)}, u32[]{:S(2)}, u32[]{:S(2)}) collective-permute-start(f32[64,128]{1,0:T(8,128)S(1)} %get-tuple-element.24), channel_id=1, source_target_pairs={{0,1},{1,0},{2,3},{3,2},{4,5},{5,4},{6,7},{7,6},{8,9},{9,8},{10,11... | collective-permute-start | bytes 98312 | tf_op jit(solution)/shard_map/ppermute | solution.py:571
  3.5 6.3 %collective-permute-start.1 = (bf16[24,2176]{1,0:T(8,128)(2,1)S(1)}, bf16[24,2176]{1,0:T(8,128)(2,1)S(1)}, u32[]{:S(2)}, u32[]{:S(2)}) collective-permute-start(bf16[24,2176]{1,0:T(8,128)(2,1)S(1)} %get-tuple-element.28), channel_id=1, source_target_pairs={{0,2},{4,6},{8,10},{12,14},{2,0},{6,4},{10,8},{14,12},{1,3},{5,7},... | collective-permute-start | bytes 313352 | tf_op jit(solution)/shard_map/ppermute | solution.py:597
  4.8 6.6 %collective-permute-start.2 = (bf16[24,2176]{1,0:T(8,128)(2,1)S(1)}, bf16[24,2176]{1,0:T(8,128)(2,1)S(1)}, u32[]{:S(2)}, u32[]{:S(2)}) collective-permute-start(bf16[24,2176]{1,0:T(8,128)(2,1)S(1)} %get-tuple-element.29), channel_id=1, source_target_pairs={{2,4},{6,8},{10,12},{4,2},{8,6},{12,10},{3,5},{7,9},{11,13},{5,3},... | collective-permute-start | bytes 313352 | tf_op jit(solution)/shard_map/ppermute | solution.py:597
  11.5 3.3 %collective-permute-start.3 = (f32[48,1152]{1,0:T(8,128)S(1)}, f32[48,1152]{1,0:T(8,128)S(1)}, u32[]{:S(2)}, u32[]{:S(2)}) collective-permute-start(f32[48,1152]{1,0:T(8,128)S(1)} %get-tuple-element.33), channel_id=1, source_target_pairs={{0,1},{1,0},{2,3},{3,2},{4,5},{5,4},{6,7},{7,6},{8,9},{9,8},{10,11... | collective-permute-start | bytes 663560 | tf_op jit(solution)/shard_map/ppermute | solution.py:644

commit v7 on v6

--- a/solution.py
+++ b/solution.py
@@ -116,16 +116,12 @@
     return lax.axis_index("row"), lax.axis_index("col")
 
 
-def pack_kernel(x_hbm, early_hbm, x_ref, side_ref, early_ref, sems):
-    copy = pltpu.make_async_copy(x_hbm, x_ref, sems.at[0])
-    constants = pltpu.make_async_copy(early_hbm, early_ref, sems.at[1])
+def border_kernel(x_hbm, side_ref, sem):
+    _, col = mesh_place()
+    start = pl.multiple_of(jnp.where(col == 0, x_hbm.shape[1] - LANES, 0), LANES)
+    copy = pltpu.make_async_copy(x_hbm.at[:, pl.ds(start, LANES)], side_ref, sem)
     copy.start()
-    constants.start()
-    _, col = mesh_place()
-    cols = x_ref.shape[1]
     copy.wait()
-    side_ref[...] = jnp.where(col == 0, x_ref[:, cols - LANES :], x_ref[:, :LANES])
-    constants.wait()
 
 
 def build_message(own_ref, part, rows, to):
@@ -553,21 +549,22 @@
     cw = coarse_constants(strip, strip_rows)
     bands = [column_weights(s, 1) for s in SIGMAS]
     wc, wl, we = (np.stack([b[i] for b in bands]) for i in range(3))
-    early = far(joined([bm, *column_weights(SIGMAS[-1], 2)]))
+    early = jnp.asarray(joined([bm, *column_weights(SIGMAS[-1], 2)]))
     late = jnp.asarray(joined([wc, wl, we, lh, lt, cw]))
     base_rows = bm.shape[0]
     own_shape = jax.ShapeDtypeStruct((2 * rows, wide), BF16)
     message = jax.ShapeDtypeStruct((MESSAGE, wide), BF16)
 
-    tile, side, early = pl.pallas_call(
-        pack_kernel,
-        out_shape=(like(image), jax.ShapeDtypeStruct((rows, LANES), F32), like(early)),
-        in_specs=far_specs(2),
-        out_specs=tuple(vmem_specs(3)),
-        scratch_shapes=[pltpu.SemaphoreType.DMA((2,))],
-        compiler_params=limit(4),
-        name="pack",
-    )(far(image), early)
+    side = pl.pallas_call(
+        border_kernel,
+        out_shape=jax.ShapeDtypeStruct((rows, LANES), F32),
+        in_specs=far_specs(1),
+        out_specs=vmem_specs(1)[0],
+        scratch_shapes=[pltpu.SemaphoreType.DMA],
+        compiler_params=limit(1),
+        cost_estimate=pl.CostEstimate(flops=2 * 10**9, bytes_accessed=10**7, transcendentals=0),
+        name="border",
+    )(far(image))
     side = lax.ppermute(side, "col", [(0, 1), (1, 0)])
     own, to_even, to_odd, base = pl.pallas_call(
         send_kernel,
@@ -581,7 +578,7 @@
         compiler_params=limit(6),
         cost_estimate=pl.CostEstimate(flops=10**9, bytes_accessed=10**6, transcendentals=0),
         name="send",
-    )(tile, early)
+    )(image, early)
     own, to_even, to_odd = pl.pallas_call(
         side_kernel,
         out_shape=(own_shape, message, message),

time: 17.5 us -> 17.2 us (0.983)
  Pallas kernels: 9.29 us -> 8.95 us
    pallas_call x1, Pallas kernels: 1.19 us -> 0.85 us  [local(): pl.pallas_call(border_kernel, out_shape=jax.ShapeDtypeStruct((rows, LANES...]
where the time goes in v7:
time: 17.2 us; the launch traced here: 17.1 us
  Pallas kernels  8.95 us (52%)
  starting transfers between devices  5.61 us (33%)
  waiting for transfers between devices  1.79 us (10%)
  between operations  0.72 us (4%)
    ppermute x2, starting transfers between devices, swap(): return lax.ppermute(value, 'row', pairs + [(j, i) for i, j in pairs])  3.31 us
    pallas_call x1, Pallas kernels, local(): pl.pallas_call(inner_kernel, out_shape=(*fine_shapes, jax.ShapeDtypeStruc...  2.91 us
    pallas_call x1, Pallas kernels, local(): pl.pallas_call(functools.partial(coarse_kernel, row_count - 1), out_shape...  2.52 us
    pallas_call x1, Pallas kernels, local(): pl.pallas_call(functools.partial(outer_kernel, row_count - 1), out_shape=...  1.76 us
    ppermute x2, waiting for transfers between devices, swap(): return lax.ppermute(value, 'row', pairs + [(j, i) for i, j in pairs])  1.68 us
    ppermute x1, starting transfers between devices, local(): other = lax.ppermute(send, 'col', [(0, 1), (1, 0)])  1.55 us
    pallas_call x1, Pallas kernels, local(): pl.pallas_call(border_kernel, out_shape=jax.ShapeDtypeStruct((rows, LANES...  0.85 us
    pallas_call x1, Pallas kernels, local(): pl.pallas_call(send_kernel, out_shape=(own_shape, message, message, jax.S...  0.75 us
  transfers between devices with their start and end apart: 4, of which 2 were waited for; matrix products, arithmetic and copies ran while one was open for 0% of the time, Pallas kernels for 27%

profile of v7, /device:TPU:11, one launch (start us, length us, event | category | flops | bytes accessed | tf_op | source)
XLA Modules:
  0.0 17.1 jit_solution(3874129480763621908)
XLA Ops:
  0.6 0.0 copy-start.2
  0.6 0.0 copy-start.1
  0.7 0.9 %border.1 = f32[64,128]{1,0:T(8,128)S(1)} custom-call(f32[64,2048]{1,0:T(8,128)} %x_hbm.1), custom_call_target="tpu_custom_call" | custom-call | flops 2000000000 | bytes 10000000 | tf_op jit(solution)/shard_map/border/pallas_call | solution.py:558
  1.5 0.0 copy-start
  1.5 0.7 %collective-permute-start = (f32[64,128]{1,0:T(8,128)S(1)}, f32[64,128]{1,0:T(8,128)S(1)}, u32[]{:S(2)}, u32[]{:S(2)}) collective-permute-start(f32[64,128]{1,0:T(8,128)S(1)} %border.1), channel_id=1, source_target_pairs={{0,1},{1,0},{2,3},{3,2},{4,5},{5,4},{6,7},{7,6},{8,9},{9,8},{10,11... | collective-permute-start | bytes 98312 | tf_op jit(solution)/shard_map/ppermute | solution.py:568
  2.3 0.0 copy-done.2
  2.3 0.0 copy-done.1
  2.3 0.8 %send.1 = (bf16[128,2176]{1,0:T(8,128)(2,1)S(1)}, bf16[24,2176]{1,0:T(8,128)(2,1)S(1)}, bf16[24,2176]{1,0:T(8,128)(2,1)S(1)}, f32[64,1152]{1,0:T(8,128)S(1)}) custom-call(f32[64,2048]{1,0:T(8,128)S(1)} %copy-done.1, bf16[832,256]{1,0:T(8,128)(2,1)S(1)} %copy-done.2), custom_call_target="tpu_custom_call" | custom-call | flops 1000000000 | bytes 1000000 | tf_op jit(solution)/shard_map/send/pallas_call | solution.py:569
  3.0 0.1 collective-permute-done.side_ref
  3.2 1.3 %collective-permute-start.1 = (bf16[24,2176]{1,0:T(8,128)(2,1)S(1)}, bf16[24,2176]{1,0:T(8,128)(2,1)S(1)}, u32[]{:S(2)}, u32[]{:S(2)}) collective-permute-start(bf16[24,2176]{1,0:T(8,128)(2,1)S(1)} %get-tuple-element.22), channel_id=1, source_target_pairs={{0,2},{4,6},{8,10},{12,14},{2,0},{6,4},{10,8},{14,12},{1,3},{5,7},... | collective-permute-start | bytes 313352 | tf_op jit(solution)/shard_map/ppermute | solution.py:594
  4.5 2.0 %collective-permute-start.2 = (bf16[24,2176]{1,0:T(8,128)(2,1)S(1)}, bf16[24,2176]{1,0:T(8,128)(2,1)S(1)}, u32[]{:S(2)}, u32[]{:S(2)}) collective-permute-start(bf16[24,2176]{1,0:T(8,128)(2,1)S(1)} %get-tuple-element.23), channel_id=1, source_target_pairs={{2,4},{6,8},{10,12},{4,2},{8,6},{12,10},{3,5},{7,9},{11,13},{5,3},... | collective-permute-start | bytes 313352 | tf_op jit(solution)/shard_map/ppermute | solution.py:594
  6.5 0.0 copy-done
  6.5 2.9 %inner.1 = (bf16[4,64,2048]{2,1,0:T(8,128)(2,1)S(1)}, bf16[2,64,2048]{2,1,0:T(8,128)(2,1)S(1)}, f32[4,64,2304]{2,1,0:T(8,128)S(1)}) custom-call(bf16[128,2176]{1,0:T(8,128)(2,1)S(1)} %get-tuple-element.24.own_ref, bf16[4560,256]{1,0:T(8,128)(2,1)S(1)} %copy-done), custom_call_target="tpu_custom_call" | custom-call | flops 2000000000 | bytes 10000000 | tf_op jit(solution)/shard_map/inner/pallas_call | solution.py:618
  9.4 0.0 collective-permute-done.1.even_ref
  9.4 1.7 %collective-permute-done.2.odd_ref = bf16[24,2176]{1,0:T(8,128)(2,1)S(1)} collective-permute-done((bf16[24,2176]{1,0:T(8,128)(2,1)S(1)}, bf16[24,2176]{1,0:T(8,128)(2,1)S(1)}, u32[]{:S(2)}, u32[]{:S(2)}) %collective-permute-start.2) | collective-permute-done | bytes 104480 | tf_op jit(solution)/shard_map/ppermute | solution.py:594
  11.1 0.1 base.1
  11.2 1.6 %collective-permute-start.3 = (f32[48,1152]{1,0:T(8,128)S(1)}, f32[48,1152]{1,0:T(8,128)S(1)}, u32[]{:S(2)}, u32[]{:S(2)}) collective-permute-start(f32[48,1152]{1,0:T(8,128)S(1)} %get-tuple-element.27), channel_id=1, source_target_pairs={{0,1},{1,0},{2,3},{3,2},{4,5},{5,4},{6,7},{7,6},{8,9},{9,8},{10,11... | collective-permute-start | bytes 663560 | tf_op jit(solution)/shard_map/ppermute | solution.py:641
  12.8 1.8 %outer.1 = (bf16[4,64,2048]{2,1,0:T(8,128)(2,1)S(1)}, bf16[2,64,2048]{2,1,0:T(8,128)(2,1)S(1)}) custom-call(bf16[24,2176]{1,0:T(8,128)(2,1)S(1)} %collective-permute-done.1.even_ref, bf16[24,2176]{1,0:T(8,128)(2,1)S(1)} %collective-permute-done.2.odd_ref, bf16[4560,256]{1,0:T(8,128)(2,1)S(1)} %copy-done, ...), custom_call_target="tpu_custom_call", output_to_operand_aliasing={{0}: (4, {}), {1}: (5, {})} | custom-call | flops 1000000000 | bytes 1000000 | tf_op jit(solution)/shard_map/outer/pallas_call | solution.py:642
  14.6 0.0 collective-permute-done.3.other_ref
  14.6 2.5 %coarse.1 = (bf16[4,64,2048]{2,1,0:T(8,128)(2,1)}, bf16[2,64,2048]{2,1,0:T(8,128)(2,1)}, bf16[4,16,2048]{2,1,0:T(8,128)(2,1)}, bf16[2,16,2048]{2,1,0:T(8,128)(2,1)}) custom-call(f32[48,1152]{1,0:T(8,128)S(1)} %get-tuple-element.26.keep_ref, f32[48,1152]{1,0:T(8,128)S(1)} %collective-permute-done.3.other_ref, ...), custom_call_target="tpu_custom_call" | custom-call | tf_op jit(solution)/shard_map/coarse/pallas_call | solution.py:654
  (1 shorter events, 0.0 us)
Async XLA Ops:
  0.6 1.6 %copy-start.2 = (bf16[832,256]{1,0:T(8,128)(2,1)S(1)}, bf16[832,256]{1,0:T(8,128)(2,1)}, u32[]{:S(2)}) copy-start(bf16[832,256]{1,0:T(8,128)(2,1)} %constant.4.clone.early_ref) | copy-start | bytes 1277956
  0.6 1.6 %copy-start.1 = (f32[64,2048]{1,0:T(8,128)S(1)}, f32[64,2048]{1,0:T(8,128)}, u32[]{:S(2)}) copy-start(f32[64,2048]{1,0:T(8,128)} %x_hbm.1) | copy-start | bytes 1572868
  1.5 5.0 %copy-start = (bf16[4560,256]{1,0:T(8,128)(2,1)S(1)}, bf16[4560,256]{1,0:T(8,128)(2,1)}, u32[]{:S(2)}) copy-start(bf16[4560,256]{1,0:T(8,128)(2,1)} %constant.5.clone.late_ref) | copy-start | bytes 7004164
  1.5 1.6 %collective-permute-start = (f32[64,128]{1,0:T(8,128)S(1)}, f32[64,128]{1,0:T(8,128)S(1)}, u32[]{:S(2)}, u32[]{:S(2)}) collective-permute-start(f32[64,128]{1,0:T(8,128)S(1)} %border.1), channel_id=1, source_target_pairs={{0,1},{1,0},{2,3},{3,2},{4,5},{5,4},{6,7},{7,6},{8,9},{9,8},{10,11... | collective-permute-start | bytes 98312 | tf_op jit(solution)/shard_map/ppermute | solution.py:568
  3.2 6.3 %collective-permute-start.1 = (bf16[24,2176]{1,0:T(8,128)(2,1)S(1)}, bf16[24,2176]{1,0:T(8,128)(2,1)S(1)}, u32[]{:S(2)}, u32[]{:S(2)}) collective-permute-start(bf16[24,2176]{1,0:T(8,128)(2,1)S(1)} %get-tuple-element.22), channel_id=1, source_target_pairs={{0,2},{4,6},{8,10},{12,14},{2,0},{6,4},{10,8},{14,12},{1,3},{5,7},... | collective-permute-start | bytes 313352 | tf_op jit(solution)/shard_map/ppermute | solution.py:594
  4.5 6.6 %collective-permute-start.2 = (bf16[24,2176]{1,0:T(8,128)(2,1)S(1)}, bf16[24,2176]{1,0:T(8,128)(2,1)S(1)}, u32[]{:S(2)}, u32[]{:S(2)}) collective-permute-start(bf16[24,2176]{1,0:T(8,128)(2,1)S(1)} %get-tuple-element.23), channel_id=1, source_target_pairs={{2,4},{6,8},{10,12},{4,2},{8,6},{12,10},{3,5},{7,9},{11,13},{5,3},... | collective-permute-start | bytes 313352 | tf_op jit(solution)/shard_map/ppermute | solution.py:594
  11.2 3.3 %collective-permute-start.3 = (f32[48,1152]{1,0:T(8,128)S(1)}, f32[48,1152]{1,0:T(8,128)S(1)}, u32[]{:S(2)}, u32[]{:S(2)}) collective-permute-start(f32[48,1152]{1,0:T(8,128)S(1)} %get-tuple-element.27), channel_id=1, source_target_pairs={{0,1},{1,0},{2,3},{3,2},{4,5},{5,4},{6,7},{7,6},{8,9},{9,8},{10,11... | collective-permute-start | bytes 663560 | tf_op jit(solution)/shard_map/ppermute | solution.py:641

commit v8 on v7

--- a/solution.py
+++ b/solution.py
@@ -351,52 +351,56 @@
     filter_columns(vh, vl, w_refs, 4, cols, lev, emit, after_group, seam)
 
 
-def outer_kernel(last_row, even_ref, odd_ref, late_ref, rim_ref, dog_in, hess_in,
-                 dog_ref, hess_ref, vh, vl, lev, d1, d2):
+def outer_kernel(last_row, one_hop, message_ref, late_ref, rim_ref, dog_in, hess_in, dog_ref, hess_ref, *scratch):
+    row, _ = mesh_place()
+    from_above = (row % 2 == 1) if one_hop else (row % 2 == 0)
+    for above in (True, False):
+
+        @pl.when(from_above if above else jnp.logical_not(from_above))
+        def _():
+            outer_side(last_row, above, message_ref, late_ref, rim_ref, dog_ref, hess_ref, *scratch)
+
+
+def outer_side(last_row, above, message_ref, late_ref, rim_ref, dog_ref, hess_ref, vh, vl, lev, d1, d2):
     _, rows, cols = dog_ref.shape
     row, col = mesh_place()
     is_left = col == 0
-    even = row % 2 == 0
     diffs = {1: d1, 2: d2}
     rim_tall = RIM + 2 * PAD
+    skip = PAD - 1 if above else PAD + 1
+    first = 0 if above else rim_tall
+    outs = slice(0, RIM) if above else slice(rows - RIM, rows)
+    height = LEVELS * RIM
+    start = 3 * LEVELS * BLOCK + LEVELS * (rows + 2 * PAD) + (0 if above else 2 * height)
+    lt_high = late_ref[start : start + height, :MESSAGE]
+    lt_low = late_ref[start + height : start + 2 * height, :MESSAGE]
 
     def rows_of(part):
-        a, b = even_ref[:, part], odd_ref[:, part]
-        bot, top = jnp.where(even, a, b), jnp.where(even, b, a)
-        ends = jnp.concatenate([top[16:], bot[16:]], axis=0)
-        stack = jnp.concatenate([top[:16], bot[:16], ends], axis=0)
-        return mm(lt, jnp.concatenate([stack, stack], axis=0))
+        return mm(lt_high, message_ref[:, part]) + mm(lt_low, message_ref[:, part])
 
     def emit(k, at, d):
         to = slice(at, at + d.shape[1])
         zero = lambda count: jnp.zeros((count, d.shape[1]), F32)
-        top = rim_ref[k, :rim_tall, to] + jnp.concatenate(
-            [zero(PAD - 1), d[:RIM], zero(rim_tall - RIM - PAD + 1)], axis=0
-        )
-        bot = rim_ref[k, rim_tall:, to] + jnp.concatenate(
-            [zero(rim_tall - RIM - PAD + 1), d[RIM:], zero(PAD - 1)], axis=0
+        total = rim_ref[k, first : first + rim_tall, to] + jnp.concatenate(
+            [zero(skip), d, zero(rim_tall - RIM - skip)], axis=0
         )
         if 0 < at <= cols:
-            out = slice(at - LANES, at - LANES + BLOCK)
-            dog_ref[k, :RIM, out] = (20.0 * top[PAD : PAD + RIM]).astype(BF16)
-            dog_ref[k, rows - RIM :, out] = (20.0 * bot[PAD : PAD + RIM]).astype(BF16)
+            dog_ref[k, outs, at - LANES : at - LANES + BLOCK] = (20.0 * total[PAD : PAD + RIM]).astype(BF16)
         if k in diffs:
             d = diffs[k]
-            d[:PAD, to] = jnp.where(row == 0, 0.0, top[:PAD])
-            d[PAD:rim_tall, to] = top[PAD:]
-            d[rim_tall : 2 * rim_tall - PAD, to] = bot[: rim_tall - PAD]
-            d[2 * rim_tall - PAD :, to] = jnp.where(row == last_row, 0.0, bot[rim_tall - PAD :])
-
-    def after_group(m, first, count):
-        for top, to in ((0, slice(0, RIM)), (rim_tall, slice(rows - RIM, rows))):
-
-            def put(t, value):
-                hess_ref[m, to, t * LANES : (t + 1) * LANES] = value
-
-            hess_tiles(diffs[m + 1], top, RIM, first, count, 5000.0, put)
-
-    first = 3 * LEVELS * BLOCK + LEVELS * (rows + 2 * PAD)
-    lt = late_ref[first : first + LEVELS * 2 * RIM, : 4 * MESSAGE]
+            if above:
+                d[:PAD, to] = jnp.where(row == 0, 0.0, total[:PAD])
+                d[PAD:, to] = total[PAD:]
+            else:
+                d[: rim_tall - PAD, to] = total[: rim_tall - PAD]
+                d[rim_tall - PAD :, to] = jnp.where(row == last_row, 0.0, total[rim_tall - PAD :])
+
+    def after_group(m, tile, count):
+        def put(t, value):
+            hess_ref[m, outs, t * LANES : (t + 1) * LANES] = value
+
+        hess_tiles(diffs[m + 1], 0, RIM, tile, count, 5000.0, put)
+
     place_rows(vh, vl, rows_of, cols, is_left)
     w_refs = band_refs(late_ref)
     seam = seam_filter(vh, vl, w_refs, cols, lev, is_left, emit)
@@ -453,20 +457,20 @@
             diffs[k][PAD : PAD + rows, to] = d[PAD : PAD + rows]
             diffs[k][PAD + rows :, to] = jnp.where((row == last_row) & (col == 1), 0.0, d[PAD + rows :])
 
+    dog_copy = pltpu.make_async_copy(dog_ref, dog_hbm, sems.at[2])
+    hess_copies = [pltpu.make_async_copy(hess_ref.at[m], hess_hbm.at[m], sems.at[3 + m]) for m in range(2)]
+
     def after_group(m, first, count):
         def put(t, value):
             hess_ref[m, :, t * LANES : (t + 1) * LANES] = value
 
+        if m == 1:
+            dog_copy.start()
         hess_tiles(diffs[m + 1], 0, rows, first, count, 200000.0, put)
+        hess_copies[m].start()
 
     filter_columns(vh, vl, band_refs(late_ref), 8, cols, lev, emit, after_group, lambda s: None)
-    copies = [
-        pltpu.make_async_copy(dog_ref, dog_hbm, sems.at[2]),
-        pltpu.make_async_copy(hess_ref, hess_hbm, sems.at[3]),
-    ]
-    for copy in copies:
-        copy.start()
-    for copy in fine_copies + copies:
+    for copy in fine_copies + [dog_copy] + hess_copies:
         copy.wait()
 
 
@@ -479,12 +483,6 @@
     top[: NEAR + 1] = np.append(np.arange(-NEAR, 0), -1)
     bot = np.full(MESSAGE, nowhere)
     bot[: NEAR + 1] = rows + np.append(np.arange(NEAR), 0)
-    inputs = np.concatenate([top[:16], bot[:16], top[16:], bot[16:]])
-    again = inputs.copy()
-    again[[NEAR, 16 + NEAR]] = nowhere
-    far_inputs = np.concatenate([inputs, again])
-    far_low = np.arange(4 * MESSAGE) >= 2 * MESSAGE
-
     def matrix(sigma, centres, valid, inputs, use_low):
         high, low = two_parts(row_matrix(sigma, centres, inputs) * valid[:, None])
         return np.where(use_low[None, :], low.astype(np.float32), high.astype(np.float32)).astype(BF16)
@@ -492,8 +490,13 @@
     centres = np.arange(-PAD, rows + PAD)
     valid = ((centres >= -1) & (centres <= rows)).astype(np.float32)
     level = [matrix(s, centres, valid, own_inputs, own_low) for s in SIGMAS]
-    rim = np.concatenate([np.arange(-1, RIM - 1), np.arange(rows + 1 - RIM, rows + 1)])
-    halo = [matrix(s, rim, np.ones(rim.shape, np.float32), far_inputs, far_low) for s in SIGMAS]
+    halo = []
+    for inputs, rim in ((top, np.arange(-1, RIM - 1)), (bot, np.arange(rows + 1 - RIM, rows + 1))):
+        again = inputs.copy()
+        again[NEAR] = nowhere
+        for rows_in, use_low in ((inputs, False), (again, True)):
+            part = np.full(MESSAGE, use_low)
+            halo += [matrix(s, rim, np.ones(RIM, np.float32), rows_in, part) for s in SIGMAS]
     count = rows // 2 + 2 * (REACH + 1)
     index = np.arange(-(-count // 8) * 8)
     base = matrix(SIGMAS[-1], 2 * (index - REACH - 1), (index < count).astype(np.float32), own_inputs, own_low)
@@ -626,6 +629,21 @@
         name="inner",
     )(own, late)
 
+    def finish(one_hop, message, dog, hess):
+        return pl.pallas_call(
+            functools.partial(outer_kernel, row_count - 1, one_hop),
+            out_shape=fine_shapes,
+            in_specs=vmem_specs(5),
+            out_specs=tuple(vmem_specs(2)),
+            scratch_shapes=scratch(rim_tall, RIM, BLOCK),
+            input_output_aliases={3: 0, 4: 1},
+            compiler_params=limit(12),
+            cost_estimate=pl.CostEstimate(flops=10**9, bytes_accessed=10**6, transcendentals=0),
+            name="outer",
+        )(message, late, rim, dog, hess)
+
+    dog_fine, hess_fine = finish(True, even, dog_fine, hess_fine)
+
     keep, send = pl.pallas_call(
         functools.partial(base_kernel, row_count, rows // 2),
         out_shape=(
@@ -637,19 +655,9 @@
         scratch_shapes=[pltpu.VMEM((base_rows, LANES), F32)],
         compiler_params=limit(4),
         name="base",
-    )(base, even, odd, rim)
+    )(base, even, odd, hess_fine)
     other = lax.ppermute(send, "col", [(0, 1), (1, 0)])
-    dog_fine, hess_fine = pl.pallas_call(
-        functools.partial(outer_kernel, row_count - 1),
-        out_shape=fine_shapes,
-        in_specs=vmem_specs(6),
-        out_specs=tuple(vmem_specs(2)),
-        scratch_shapes=scratch(2 * rim_tall, 2 * RIM, BLOCK),
-        input_output_aliases={4: 0, 5: 1},
-        compiler_params=limit(14),
-        cost_estimate=pl.CostEstimate(flops=10**9, bytes_accessed=10**6, transcendentals=0),
-        name="outer",
-    )(even, odd, late, rim, dog_fine, hess_fine)
+    dog_fine, hess_fine = finish(False, odd, dog_fine, hess_fine)
 
     return pl.pallas_call(
         functools.partial(coarse_kernel, row_count - 1),
@@ -660,7 +668,7 @@
             pltpu.VMEM((4, strip, cols), BF16),
             pltpu.VMEM((2, strip, cols), BF16),
             *scratch(small, small, 0),
-            pltpu.SemaphoreType.DMA((4,)),
+            pltpu.SemaphoreType.DMA((5,)),
         ],
         compiler_params=limit(12),
         name="coarse",

time: 17.2 us -> 16.1 us (0.936)
  waiting for transfers between devices: 1.79 us -> 0.67 us
    ppermute x2, waiting for transfers between devices: 1.68 us -> 0.57 us  [swap(): return lax.ppermute(value, 'row', pairs + [(j, i) for i, j in pairs])]
    pallas_call x1 -> x2, Pallas kernels: 1.76 us -> 2.44 us  [finish(): pl.pallas_call(functools.partial(outer_kernel, row_count - 1, one_hop), o...]
    pallas_call x1, Pallas kernels: 2.52 us -> 1.94 us  [local(): pl.pallas_call(functools.partial(coarse_kernel, row_count - 1), out_shape...]
  transfers between devices with their start and end apart: 4 -> 4, of which waited for: 2 -> 2; matrix products, arithmetic and copies ran while one was open for 0% -> 0% of each run, Pallas kernels for 27% -> 33%
where the time goes in v8:
time: 16.1 us; the launch traced here: 15.9 us
  Pallas kernels  8.92 us (55%)
  starting transfers between devices  5.61 us (35%)
  between operations  0.73 us (5%)
  waiting for transfers between devices  0.67 us (4%)
    ppermute x2, starting transfers between devices, swap(): return lax.ppermute(value, 'row', pairs + [(j, i) for i, j in pairs])  3.31 us
    pallas_call x1, Pallas kernels, local(): pl.pallas_call(inner_kernel, out_shape=(*fine_shapes, jax.ShapeDtypeStruc...  2.78 us
    pallas_call x2, Pallas kernels, finish(): pl.pallas_call(functools.partial(outer_kernel, row_count - 1, one_hop), o...  2.44 us
    pallas_call x1, Pallas kernels, local(): pl.pallas_call(functools.partial(coarse_kernel, row_count - 1), out_shape...  1.94 us
    ppermute x1, starting transfers between devices, local(): other = lax.ppermute(send, 'col', [(0, 1), (1, 0)])  1.55 us
    pallas_call x1, Pallas kernels, local(): pl.pallas_call(border_kernel, out_shape=jax.ShapeDtypeStruct((rows, LANES...  0.85 us
    pallas_call x1, Pallas kernels, local(): pl.pallas_call(send_kernel, out_shape=(own_shape, message, message, jax.S...  0.76 us
    ppermute x1, starting transfers between devices, local(): side = lax.ppermute(side, 'col', [(0, 1), (1, 0)])  0.74 us
  transfers between devices with their start and end apart: 4, of which 2 were waited for; matrix products, arithmetic and copies ran while one was open for 0% of the time, Pallas kernels for 33%

profile of v8, /device:TPU:11, one launch (start us, length us, event | category | flops | bytes accessed | tf_op | source)
XLA Modules:
  0.0 15.9 jit_solution(13919894959618604824)
XLA Ops:
  0.6 0.0 copy-start.2
  0.6 0.0 copy-start.1
  0.7 0.9 %border.1 = f32[64,128]{1,0:T(8,128)S(1)} custom-call(f32[64,2048]{1,0:T(8,128)} %x_hbm.1), custom_call_target="tpu_custom_call" | custom-call | flops 2000000000 | bytes 10000000 | tf_op jit(solution)/shard_map/border/pallas_call | solution.py:561
  1.5 0.0 copy-start
  1.5 0.7 %collective-permute-start = (f32[64,128]{1,0:T(8,128)S(1)}, f32[64,128]{1,0:T(8,128)S(1)}, u32[]{:S(2)}, u32[]{:S(2)}) collective-permute-start(f32[64,128]{1,0:T(8,128)S(1)} %border.1), channel_id=1, source_target_pairs={{0,1},{1,0},{2,3},{3,2},{4,5},{5,4},{6,7},{7,6},{8,9},{9,8},{10,11... | collective-permute-start | bytes 98312 | tf_op jit(solution)/shard_map/ppermute | solution.py:571
  2.3 0.0 copy-done.2
  2.3 0.0 copy-done.1
  2.3 0.8 %send.1 = (bf16[128,2176]{1,0:T(8,128)(2,1)S(1)}, bf16[24,2176]{1,0:T(8,128)(2,1)S(1)}, bf16[24,2176]{1,0:T(8,128)(2,1)S(1)}, f32[64,1152]{1,0:T(8,128)S(1)}) custom-call(f32[64,2048]{1,0:T(8,128)S(1)} %copy-done.1, bf16[832,256]{1,0:T(8,128)(2,1)S(1)} %copy-done.2), custom_call_target="tpu_custom_call" | custom-call | flops 1000000000 | bytes 1000000 | tf_op jit(solution)/shard_map/send/pallas_call | solution.py:572
  3.0 0.1 collective-permute-done.side_ref
  3.2 1.3 %collective-permute-start.1 = (bf16[24,2176]{1,0:T(8,128)(2,1)S(1)}, bf16[24,2176]{1,0:T(8,128)(2,1)S(1)}, u32[]{:S(2)}, u32[]{:S(2)}) collective-permute-start(bf16[24,2176]{1,0:T(8,128)(2,1)S(1)} %get-tuple-element.24), channel_id=1, source_target_pairs={{0,2},{4,6},{8,10},{12,14},{2,0},{6,4},{10,8},{14,12},{1,3},{5,7},... | collective-permute-start | bytes 313352 | tf_op jit(solution)/shard_map/ppermute | solution.py:597
  4.5 2.0 %collective-permute-start.2 = (bf16[24,2176]{1,0:T(8,128)(2,1)S(1)}, bf16[24,2176]{1,0:T(8,128)(2,1)S(1)}, u32[]{:S(2)}, u32[]{:S(2)}) collective-permute-start(bf16[24,2176]{1,0:T(8,128)(2,1)S(1)} %get-tuple-element.25), channel_id=1, source_target_pairs={{2,4},{6,8},{10,12},{4,2},{8,6},{12,10},{3,5},{7,9},{11,13},{5,3},... | collective-permute-start | bytes 313352 | tf_op jit(solution)/shard_map/ppermute | solution.py:597
  6.5 0.0 copy-done
  6.5 2.8 %inner.1 = (bf16[4,64,2048]{2,1,0:T(8,128)(2,1)S(1)}, bf16[2,64,2048]{2,1,0:T(8,128)(2,1)S(1)}, f32[4,64,2304]{2,1,0:T(8,128)S(1)}) custom-call(bf16[128,2176]{1,0:T(8,128)(2,1)S(1)} %get-tuple-element.26.own_ref, bf16[4720,256]{1,0:T(8,128)(2,1)S(1)} %copy-done), custom_call_target="tpu_custom_call" | custom-call | flops 2000000000 | bytes 10000000 | tf_op jit(solution)/shard_map/inner/pallas_call | solution.py:621
  9.3 0.0 collective-permute-done.1.message_ref.even_ref
  9.3 1.2 %outer.2 = (bf16[4,64,2048]{2,1,0:T(8,128)(2,1)S(1)}, bf16[2,64,2048]{2,1,0:T(8,128)(2,1)S(1)}) custom-call(bf16[24,2176]{1,0:T(8,128)(2,1)S(1)} %collective-permute-done.1.message_ref.even_ref, bf16[4720,256]{1,0:T(8,128)(2,1)S(1)} %copy-done, f32[4,64,2304]{2,1,0:T(8,128)S(1)} %get-tuple-element.27.rim_ref, ...), custom_call_target="tpu_custom_call", output_to_operand_aliasing={{0}: (3, {}), {1}: (4, {})} | custom-call | flops 1000000000 | bytes 1000000 | tf_op jit(solution)/shard_map/outer/pallas_call | solution.py:633
  10.5 0.6 %collective-permute-done.2.odd_ref.message_ref = bf16[24,2176]{1,0:T(8,128)(2,1)S(1)} collective-permute-done((bf16[24,2176]{1,0:T(8,128)(2,1)S(1)}, bf16[24,2176]{1,0:T(8,128)(2,1)S(1)}, u32[]{:S(2)}, u32[]{:S(2)}) %collective-permute-start.2) | collective-permute-done | bytes 104480 | tf_op jit(solution)/shard_map/ppermute | solution.py:597
  11.1 0.1 base.1
  11.2 1.6 %collective-permute-start.3 = (f32[48,1152]{1,0:T(8,128)S(1)}, f32[48,1152]{1,0:T(8,128)S(1)}, u32[]{:S(2)}, u32[]{:S(2)}) collective-permute-start(f32[48,1152]{1,0:T(8,128)S(1)} %get-tuple-element.32), channel_id=1, source_target_pairs={{0,1},{1,0},{2,3},{3,2},{4,5},{5,4},{6,7},{7,6},{8,9},{9,8},{10,11... | collective-permute-start | bytes 663560 | tf_op jit(solution)/shard_map/ppermute | solution.py:659
  12.8 1.2 %outer.3 = (bf16[4,64,2048]{2,1,0:T(8,128)(2,1)S(1)}, bf16[2,64,2048]{2,1,0:T(8,128)(2,1)S(1)}) custom-call(bf16[24,2176]{1,0:T(8,128)(2,1)S(1)} %collective-permute-done.2.odd_ref.message_ref, bf16[4720,256]{1,0:T(8,128)(2,1)S(1)} %copy-done, f32[4,64,2304]{2,1,0:T(8,128)S(1)} %get-tuple-element.27.rim_ref, ...), custom_call_target="tpu_custom_call", output_to_operand_aliasing={{0}: (3, {}), {1}: (4, {})} | custom-call | flops 1000000000 | bytes 1000000 | tf_op jit(solution)/shard_map/outer/pallas_call | solution.py:633
  14.0 0.0 collective-permute-done.3.other_ref
  14.0 1.9 %coarse.1 = (bf16[4,64,2048]{2,1,0:T(8,128)(2,1)}, bf16[2,64,2048]{2,1,0:T(8,128)(2,1)}, bf16[4,16,2048]{2,1,0:T(8,128)(2,1)}, bf16[2,16,2048]{2,1,0:T(8,128)(2,1)}) custom-call(f32[48,1152]{1,0:T(8,128)S(1)} %get-tuple-element.31.keep_ref, f32[48,1152]{1,0:T(8,128)S(1)} %collective-permute-done.3.other_ref, ...), custom_call_target="tpu_custom_call" | custom-call | tf_op jit(solution)/shard_map/coarse/pallas_call | solution.py:662
  (1 shorter events, 0.0 us)
Async XLA Ops:
  0.6 1.6 %copy-start.2 = (bf16[832,256]{1,0:T(8,128)(2,1)S(1)}, bf16[832,256]{1,0:T(8,128)(2,1)}, u32[]{:S(2)}) copy-start(bf16[832,256]{1,0:T(8,128)(2,1)} %constant.4.clone.early_ref) | copy-start | bytes 1277956
  0.6 1.6 %copy-start.1 = (f32[64,2048]{1,0:T(8,128)S(1)}, f32[64,2048]{1,0:T(8,128)}, u32[]{:S(2)}) copy-start(f32[64,2048]{1,0:T(8,128)} %x_hbm.1) | copy-start | bytes 1572868
  1.5 5.0 %copy-start = (bf16[4720,256]{1,0:T(8,128)(2,1)S(1)}, bf16[4720,256]{1,0:T(8,128)(2,1)}, u32[]{:S(2)}) copy-start(bf16[4720,256]{1,0:T(8,128)(2,1)} %constant.5.clone.late_ref) | copy-start | bytes 7249924
  1.5 1.6 %collective-permute-start = (f32[64,128]{1,0:T(8,128)S(1)}, f32[64,128]{1,0:T(8,128)S(1)}, u32[]{:S(2)}, u32[]{:S(2)}) collective-permute-start(f32[64,128]{1,0:T(8,128)S(1)} %border.1), channel_id=1, source_target_pairs={{0,1},{1,0},{2,3},{3,2},{4,5},{5,4},{6,7},{7,6},{8,9},{9,8},{10,11... | collective-permute-start | bytes 98312 | tf_op jit(solution)/shard_map/ppermute | solution.py:571
  3.2 6.1 %collective-permute-start.1 = (bf16[24,2176]{1,0:T(8,128)(2,1)S(1)}, bf16[24,2176]{1,0:T(8,128)(2,1)S(1)}, u32[]{:S(2)}, u32[]{:S(2)}) collective-permute-start(bf16[24,2176]{1,0:T(8,128)(2,1)S(1)} %get-tuple-element.24), channel_id=1, source_target_pairs={{0,2},{4,6},{8,10},{12,14},{2,0},{6,4},{10,8},{14,12},{1,3},{5,7},... | collective-permute-start | bytes 313352 | tf_op jit(solution)/shard_map/ppermute | solution.py:597
  4.5 6.6 %collective-permute-start.2 = (bf16[24,2176]{1,0:T(8,128)(2,1)S(1)}, bf16[24,2176]{1,0:T(8,128)(2,1)S(1)}, u32[]{:S(2)}, u32[]{:S(2)}) collective-permute-start(bf16[24,2176]{1,0:T(8,128)(2,1)S(1)} %get-tuple-element.25), channel_id=1, source_target_pairs={{2,4},{6,8},{10,12},{4,2},{8,6},{12,10},{3,5},{7,9},{11,13},{5,3},... | collective-permute-start | bytes 313352 | tf_op jit(solution)/shard_map/ppermute | solution.py:597
  11.2 2.8 %collective-permute-start.3 = (f32[48,1152]{1,0:T(8,128)S(1)}, f32[48,1152]{1,0:T(8,128)S(1)}, u32[]{:S(2)}, u32[]{:S(2)}) collective-permute-start(f32[48,1152]{1,0:T(8,128)S(1)} %get-tuple-element.32), channel_id=1, source_target_pairs={{0,1},{1,0},{2,3},{3,2},{4,5},{5,4},{6,7},{7,6},{8,9},{9,8},{10,11... | collective-permute-start | bytes 663560 | tf_op jit(solution)/shard_map/ppermute | solution.py:659

commit v9 on v8

--- a/solution.py
+++ b/solution.py
@@ -319,9 +319,8 @@
     _, col = mesh_place()
     is_left = col == 0
     diffs = {1: d1, 2: d2}
-    tall = rows + 2 * PAD
     mid_rows = rows - 2 * RIM
-    rim_tall = RIM + 2 * PAD
+    rim_tall = RIM + PAD
 
     def rows_of(part):
         own = own_ref[:, part]
@@ -330,9 +329,9 @@
     def emit(k, at, d):
         to = slice(at, at + d.shape[1])
         rim_ref[k, :rim_tall, to] = d[:rim_tall]
-        rim_ref[k, rim_tall:, to] = d[tall - rim_tall :]
+        rim_ref[k, rim_tall:, to] = d[rows - rim_tall :]
         if 0 < at <= cols:
-            mid = d[PAD + RIM : PAD + RIM + mid_rows]
+            mid = d[RIM : RIM + mid_rows]
             dog_ref[k, RIM : RIM + mid_rows, at - LANES : at - LANES + BLOCK] = (20.0 * mid).astype(BF16)
         if k in diffs:
             diffs[k][:, to] = d
@@ -341,49 +340,55 @@
         def put(t, value):
             hess_ref[m, RIM : RIM + mid_rows, t * LANES : (t + 1) * LANES] = value
 
-        hess_tiles(diffs[m + 1], RIM, mid_rows, first, count, 5000.0, put)
+        hess_tiles(diffs[m + 1], RIM - PAD, mid_rows, first, count, 5000.0, put)
 
     first = 3 * LEVELS * BLOCK
-    lh = late_ref[first : first + LEVELS * tall, : 3 * rows]
+    lh = late_ref[first : first + LEVELS * rows, : 3 * rows]
     place_rows(vh, vl, rows_of, cols, is_left)
     w_refs = band_refs(late_ref)
     seam = seam_filter(vh, vl, w_refs, cols, lev, is_left, emit)
     filter_columns(vh, vl, w_refs, 4, cols, lev, emit, after_group, seam)
 
 
-def outer_kernel(last_row, one_hop, message_ref, late_ref, rim_ref, dog_in, hess_in, dog_ref, hess_ref, *scratch):
+def outer_kernel(last_row, one_hop, message_ref, own_ref, late_ref, rim_ref, dog_in, hess_in, dog_ref, hess_ref, *scratch):
     row, _ = mesh_place()
     from_above = (row % 2 == 1) if one_hop else (row % 2 == 0)
     for above in (True, False):
 
         @pl.when(from_above if above else jnp.logical_not(from_above))
         def _():
-            outer_side(last_row, above, message_ref, late_ref, rim_ref, dog_ref, hess_ref, *scratch)
-
-
-def outer_side(last_row, above, message_ref, late_ref, rim_ref, dog_ref, hess_ref, vh, vl, lev, d1, d2):
+            outer_side(last_row, above, message_ref, own_ref, late_ref, rim_ref, dog_ref, hess_ref, *scratch)
+
+
+def outer_side(last_row, above, message_ref, own_ref, late_ref, rim_ref, dog_ref, hess_ref, vh, vl, lev, d1, d2):
     _, rows, cols = dog_ref.shape
     row, col = mesh_place()
     is_left = col == 0
     diffs = {1: d1, 2: d2}
     rim_tall = RIM + 2 * PAD
     skip = PAD - 1 if above else PAD + 1
-    first = 0 if above else rim_tall
     outs = slice(0, RIM) if above else slice(rows - RIM, rows)
     height = LEVELS * RIM
-    start = 3 * LEVELS * BLOCK + LEVELS * (rows + 2 * PAD) + (0 if above else 2 * height)
-    lt_high = late_ref[start : start + height, :MESSAGE]
+    start = 3 * LEVELS * BLOCK + LEVELS * rows + (0 if above else 2 * height)
+    lt_high = late_ref[start : start + height, : 3 * RIM + MESSAGE]
     lt_low = late_ref[start + height : start + 2 * height, :MESSAGE]
+    own_first = 0 if above else rows - RIM
 
     def rows_of(part):
-        return mm(lt_high, message_ref[:, part]) + mm(lt_low, message_ref[:, part])
+        message = message_ref[:, part]
+        high = own_ref[own_first : own_first + RIM, part]
+        low = own_ref[rows + own_first : rows + own_first + RIM, part]
+        return mm(lt_high, jnp.concatenate([high, low, high, message], axis=0)) + mm(lt_low, message)
 
     def emit(k, at, d):
         to = slice(at, at + d.shape[1])
         zero = lambda count: jnp.zeros((count, d.shape[1]), F32)
-        total = rim_ref[k, first : first + rim_tall, to] + jnp.concatenate(
-            [zero(skip), d, zero(rim_tall - RIM - skip)], axis=0
-        )
+        total = jnp.concatenate([zero(skip), d, zero(rim_tall - RIM - skip)], axis=0)
+        if above:
+            total = jnp.concatenate([total[:PAD], total[PAD:] + rim_ref[k, : rim_tall - PAD, to]], axis=0)
+        else:
+            own = total[: rim_tall - PAD] + rim_ref[k, rim_tall - PAD :, to]
+            total = jnp.concatenate([own, total[rim_tall - PAD :]], axis=0)
         if 0 < at <= cols:
             dog_ref[k, outs, at - LANES : at - LANES + BLOCK] = (20.0 * total[PAD : PAD + RIM]).astype(BF16)
         if k in diffs:
@@ -487,16 +492,25 @@
         high, low = two_parts(row_matrix(sigma, centres, inputs) * valid[:, None])
         return np.where(use_low[None, :], low.astype(np.float32), high.astype(np.float32)).astype(BF16)
 
-    centres = np.arange(-PAD, rows + PAD)
-    valid = ((centres >= -1) & (centres <= rows)).astype(np.float32)
-    level = [matrix(s, centres, valid, own_inputs, own_low) for s in SIGMAS]
+    level = [matrix(s, own, np.ones(rows, np.float32), own_inputs, own_low) for s in SIGMAS]
     halo = []
-    for inputs, rim in ((top, np.arange(-1, RIM - 1)), (bot, np.arange(rows + 1 - RIM, rows + 1))):
+    for inputs, rim, near_own, outer in (
+        (top, np.arange(-1, RIM - 1), own[:RIM], 0),
+        (bot, np.arange(rows + 1 - RIM, rows + 1), own[rows - RIM :], RIM - 1),
+    ):
+        ones = np.ones(RIM, np.float32)
+        alone = (np.arange(RIM) == outer).astype(np.float32)
+        triple = np.concatenate([near_own, near_own, near_own])
+        triple_low = np.arange(3 * RIM) >= 2 * RIM
         again = inputs.copy()
         again[NEAR] = nowhere
-        for rows_in, use_low in ((inputs, False), (again, True)):
-            part = np.full(MESSAGE, use_low)
-            halo += [matrix(s, rim, np.ones(RIM, np.float32), rows_in, part) for s in SIGMAS]
+        for s in SIGMAS:
+            beside = matrix(s, rim, alone, triple, triple_low).astype(np.float32)
+            beyond = matrix(s, rim, ones, inputs, np.zeros(MESSAGE, bool)).astype(np.float32)
+            halo.append(np.concatenate([beside, beyond], axis=1))
+        for s in SIGMAS:
+            low = matrix(s, rim, ones, again, np.ones(MESSAGE, bool)).astype(np.float32)
+            halo.append(np.pad(low, ((0, 0), (0, 3 * RIM))))
     count = rows // 2 + 2 * (REACH + 1)
     index = np.arange(-(-count // 8) * 8)
     base = matrix(SIGMAS[-1], 2 * (index - REACH - 1), (index < count).astype(np.float32), own_inputs, own_low)
@@ -546,7 +560,6 @@
     row_count = lax.axis_size("row")
     strip = rows // 4
     wide = cols + LANES
-    tall = rows + 2 * PAD
     small = strip + 2 * PAD
     lh, lt, bm, strip_rows = fine_constants(rows)
     cw = coarse_constants(strip, strip_rows)
@@ -620,10 +633,10 @@
     rim_tall = RIM + 2 * PAD
     dog_fine, hess_fine, rim = pl.pallas_call(
         inner_kernel,
-        out_shape=(*fine_shapes, jax.ShapeDtypeStruct((4, 2 * rim_tall, cols + 2 * LANES), F32)),
+        out_shape=(*fine_shapes, jax.ShapeDtypeStruct((4, 2 * (RIM + PAD), cols + 2 * LANES), F32)),
         in_specs=vmem_specs(2),
         out_specs=tuple(vmem_specs(3)),
-        scratch_shapes=scratch(tall, tall, BLOCK),
+        scratch_shapes=scratch(rows, rows, BLOCK),
         compiler_params=limit(18),
         cost_estimate=pl.CostEstimate(flops=2 * 10**9, bytes_accessed=10**7, transcendentals=0),
         name="inner",
@@ -633,14 +646,14 @@
         return pl.pallas_call(
             functools.partial(outer_kernel, row_count - 1, one_hop),
             out_shape=fine_shapes,
-            in_specs=vmem_specs(5),
+            in_specs=vmem_specs(6),
             out_specs=tuple(vmem_specs(2)),
             scratch_shapes=scratch(rim_tall, RIM, BLOCK),
-            input_output_aliases={3: 0, 4: 1},
+            input_output_aliases={4: 0, 5: 1},
             compiler_params=limit(12),
             cost_estimate=pl.CostEstimate(flops=10**9, bytes_accessed=10**6, transcendentals=0),
             name="outer",
-        )(message, late, rim, dog, hess)
+        )(message, own, late, rim, dog, hess)
 
     dog_fine, hess_fine = finish(True, even, dog_fine, hess_fine)
 

time: 16.1 us -> 16.1 us (level)
  Pallas kernels: 8.92 us -> 8.35 us
  waiting for transfers between devices: 0.67 us -> 1.23 us
    ppermute x2, waiting for transfers between devices: 0.57 us -> 1.11 us  [swap(): return lax.ppermute(value, 'row', pairs + [(j, i) for i, j in pairs])]
    pallas_call x1, Pallas kernels: 2.78 us -> 2.29 us  [local(): pl.pallas_call(inner_kernel, out_shape=(*fine_shapes, jax.ShapeDtypeStruc...]
  transfers between devices with their start and end apart: 4 -> 4, of which waited for: 2 -> 2; matrix products, arithmetic and copies ran while one was open for 0% -> 0% of each run, Pallas kernels for 33% -> 29%
where the time goes in v9:
time: 16.1 us; the launch traced here: 15.9 us
  Pallas kernels  8.35 us (52%)
  starting transfers between devices  5.61 us (35%)
  waiting for transfers between devices  1.23 us (8%)
  between operations  0.73 us (5%)
    ppermute x2, starting transfers between devices, swap(): return lax.ppermute(value, 'row', pairs + [(j, i) for i, j in pairs])  3.31 us
    pallas_call x2, Pallas kernels, finish(): pl.pallas_call(functools.partial(outer_kernel, row_count - 1, one_hop), o...  2.36 us
    pallas_call x1, Pallas kernels, local(): pl.pallas_call(inner_kernel, out_shape=(*fine_shapes, jax.ShapeDtypeStruc...  2.29 us
    pallas_call x1, Pallas kernels, local(): pl.pallas_call(functools.partial(coarse_kernel, row_count - 1), out_shape...  1.95 us
    ppermute x1, starting transfers between devices, local(): other = lax.ppermute(send, 'col', [(0, 1), (1, 0)])  1.55 us
    ppermute x2, waiting for transfers between devices, swap(): return lax.ppermute(value, 'row', pairs + [(j, i) for i, j in pairs])  1.11 us
    pallas_call x1, Pallas kernels, local(): pl.pallas_call(border_kernel, out_shape=jax.ShapeDtypeStruct((rows, LANES...  0.85 us
    ppermute x1, starting transfers between devices, local(): side = lax.ppermute(side, 'col', [(0, 1), (1, 0)])  0.74 us
  transfers between devices with their start and end apart: 4, of which 2 were waited for; matrix products, arithmetic and copies ran while one was open for 0% of the time, Pallas kernels for 29%

profile of v9, /device:TPU:11, one launch (start us, length us, event | category | flops | bytes accessed | tf_op | source)
XLA Modules:
  0.0 15.9 jit_solution(12166290426575948137)
XLA Ops:
  0.6 0.0 copy-start.2
  0.6 0.0 copy-start.1
  0.7 0.9 %border.1 = f32[64,128]{1,0:T(8,128)S(1)} custom-call(f32[64,2048]{1,0:T(8,128)} %x_hbm.1), custom_call_target="tpu_custom_call" | custom-call | flops 2000000000 | bytes 10000000 | tf_op jit(solution)/shard_map/border/pallas_call | solution.py:574
  1.5 0.0 copy-start
  1.5 0.7 %collective-permute-start = (f32[64,128]{1,0:T(8,128)S(1)}, f32[64,128]{1,0:T(8,128)S(1)}, u32[]{:S(2)}, u32[]{:S(2)}) collective-permute-start(f32[64,128]{1,0:T(8,128)S(1)} %border.1), channel_id=1, source_target_pairs={{0,1},{1,0},{2,3},{3,2},{4,5},{5,4},{6,7},{7,6},{8,9},{9,8},{10,11... | collective-permute-start | bytes 98312 | tf_op jit(solution)/shard_map/ppermute | solution.py:584
  2.3 0.0 copy-done.2
  2.3 0.0 copy-done.1
  2.3 0.7 %send.1 = (bf16[128,2176]{1,0:T(8,128)(2,1)S(1)}, bf16[24,2176]{1,0:T(8,128)(2,1)S(1)}, bf16[24,2176]{1,0:T(8,128)(2,1)S(1)}, f32[64,1152]{1,0:T(8,128)S(1)}) custom-call(f32[64,2048]{1,0:T(8,128)S(1)} %copy-done.1, bf16[832,256]{1,0:T(8,128)(2,1)S(1)} %copy-done.2), custom_call_target="tpu_custom_call" | custom-call | flops 1000000000 | bytes 1000000 | tf_op jit(solution)/shard_map/send/pallas_call | solution.py:585
  3.0 0.1 collective-permute-done.side_ref
  3.2 1.3 %collective-permute-start.1 = (bf16[24,2176]{1,0:T(8,128)(2,1)S(1)}, bf16[24,2176]{1,0:T(8,128)(2,1)S(1)}, u32[]{:S(2)}, u32[]{:S(2)}) collective-permute-start(bf16[24,2176]{1,0:T(8,128)(2,1)S(1)} %get-tuple-element.24), channel_id=1, source_target_pairs={{0,2},{4,6},{8,10},{12,14},{2,0},{6,4},{10,8},{14,12},{1,3},{5,7},... | collective-permute-start | bytes 313352 | tf_op jit(solution)/shard_map/ppermute | solution.py:610
  4.5 2.0 %collective-permute-start.2 = (bf16[24,2176]{1,0:T(8,128)(2,1)S(1)}, bf16[24,2176]{1,0:T(8,128)(2,1)S(1)}, u32[]{:S(2)}, u32[]{:S(2)}) collective-permute-start(bf16[24,2176]{1,0:T(8,128)(2,1)S(1)} %get-tuple-element.25), channel_id=1, source_target_pairs={{2,4},{6,8},{10,12},{4,2},{8,6},{12,10},{3,5},{7,9},{11,13},{5,3},... | collective-permute-start | bytes 313352 | tf_op jit(solution)/shard_map/ppermute | solution.py:610
  6.5 0.0 copy-done
  6.5 2.3 %inner.1 = (bf16[4,64,2048]{2,1,0:T(8,128)(2,1)S(1)}, bf16[2,64,2048]{2,1,0:T(8,128)(2,1)S(1)}, f32[4,48,2304]{2,1,0:T(8,128)S(1)}) custom-call(bf16[128,2176]{1,0:T(8,128)(2,1)S(1)} %get-tuple-element.26.own_ref, bf16[4640,256]{1,0:T(8,128)(2,1)S(1)} %copy-done), custom_call_target="tpu_custom_call" | custom-call | flops 2000000000 | bytes 10000000 | tf_op jit(solution)/shard_map/inner/pallas_call | solution.py:634
  8.8 0.0 collective-permute-done.1.message_ref.even_ref
  8.8 1.2 %outer.2 = (bf16[4,64,2048]{2,1,0:T(8,128)(2,1)S(1)}, bf16[2,64,2048]{2,1,0:T(8,128)(2,1)S(1)}) custom-call(bf16[24,2176]{1,0:T(8,128)(2,1)S(1)} %collective-permute-done.1.message_ref.even_ref, bf16[128,2176]{1,0:T(8,128)(2,1)S(1)} %get-tuple-element.26.own_ref, bf16[4640,256]{1,0:T(8,128)(2,1)S(1)} %copy-done, ...), custom_call_target="tpu_custom_call", output_to_operand_aliasing={{0}: (4, {}), {1}: (5, {})} | custom-call | flops 1000000000 | bytes 1000000 | tf_op jit(solution)/shard_map/outer/pallas_call | solution.py:646
  10.0 1.1 %collective-permute-done.2.odd_ref.message_ref = bf16[24,2176]{1,0:T(8,128)(2,1)S(1)} collective-permute-done((bf16[24,2176]{1,0:T(8,128)(2,1)S(1)}, bf16[24,2176]{1,0:T(8,128)(2,1)S(1)}, u32[]{:S(2)}, u32[]{:S(2)}) %collective-permute-start.2) | collective-permute-done | bytes 104480 | tf_op jit(solution)/shard_map/ppermute | solution.py:610
  11.1 0.1 base.1
  11.2 1.6 %collective-permute-start.3 = (f32[48,1152]{1,0:T(8,128)S(1)}, f32[48,1152]{1,0:T(8,128)S(1)}, u32[]{:S(2)}, u32[]{:S(2)}) collective-permute-start(f32[48,1152]{1,0:T(8,128)S(1)} %get-tuple-element.32), channel_id=1, source_target_pairs={{0,1},{1,0},{2,3},{3,2},{4,5},{5,4},{6,7},{7,6},{8,9},{9,8},{10,11... | collective-permute-start | bytes 663560 | tf_op jit(solution)/shard_map/ppermute | solution.py:672
  12.8 1.2 %outer.3 = (bf16[4,64,2048]{2,1,0:T(8,128)(2,1)S(1)}, bf16[2,64,2048]{2,1,0:T(8,128)(2,1)S(1)}) custom-call(bf16[24,2176]{1,0:T(8,128)(2,1)S(1)} %collective-permute-done.2.odd_ref.message_ref, bf16[128,2176]{1,0:T(8,128)(2,1)S(1)} %get-tuple-element.26.own_ref, bf16[4640,256]{1,0:T(8,128)(2,1)S(1)} %copy-done, ...), custom_call_target="tpu_custom_call", output_to_operand_aliasing={{0}: (4, {}), {1}: (5, {})} | custom-call | flops 1000000000 | bytes 1000000 | tf_op jit(solution)/shard_map/outer/pallas_call | solution.py:646
  14.0 0.0 collective-permute-done.3.other_ref
  14.0 1.9 %coarse.1 = (bf16[4,64,2048]{2,1,0:T(8,128)(2,1)}, bf16[2,64,2048]{2,1,0:T(8,128)(2,1)}, bf16[4,16,2048]{2,1,0:T(8,128)(2,1)}, bf16[2,16,2048]{2,1,0:T(8,128)(2,1)}) custom-call(f32[48,1152]{1,0:T(8,128)S(1)} %get-tuple-element.31.keep_ref, f32[48,1152]{1,0:T(8,128)S(1)} %collective-permute-done.3.other_ref, ...), custom_call_target="tpu_custom_call" | custom-call | tf_op jit(solution)/shard_map/coarse/pallas_call | solution.py:675
  (1 shorter events, 0.0 us)
Async XLA Ops:
  0.6 1.6 %copy-start.2 = (bf16[832,256]{1,0:T(8,128)(2,1)S(1)}, bf16[832,256]{1,0:T(8,128)(2,1)}, u32[]{:S(2)}) copy-start(bf16[832,256]{1,0:T(8,128)(2,1)} %constant.4.clone.early_ref) | copy-start | bytes 1277956
  0.6 1.6 %copy-start.1 = (f32[64,2048]{1,0:T(8,128)S(1)}, f32[64,2048]{1,0:T(8,128)}, u32[]{:S(2)}) copy-start(f32[64,2048]{1,0:T(8,128)} %x_hbm.1) | copy-start | bytes 1572868
  1.5 5.0 %copy-start = (bf16[4640,256]{1,0:T(8,128)(2,1)S(1)}, bf16[4640,256]{1,0:T(8,128)(2,1)}, u32[]{:S(2)}) copy-start(bf16[4640,256]{1,0:T(8,128)(2,1)} %constant.5.clone.late_ref) | copy-start | bytes 7127044
  1.5 1.6 %collective-permute-start = (f32[64,128]{1,0:T(8,128)S(1)}, f32[64,128]{1,0:T(8,128)S(1)}, u32[]{:S(2)}, u32[]{:S(2)}) collective-permute-start(f32[64,128]{1,0:T(8,128)S(1)} %border.1), channel_id=1, source_target_pairs={{0,1},{1,0},{2,3},{3,2},{4,5},{5,4},{6,7},{7,6},{8,9},{9,8},{10,11... | collective-permute-start | bytes 98312 | tf_op jit(solution)/shard_map/ppermute | solution.py:584
  3.2 5.6 %collective-permute-start.1 = (bf16[24,2176]{1,0:T(8,128)(2,1)S(1)}, bf16[24,2176]{1,0:T(8,128)(2,1)S(1)}, u32[]{:S(2)}, u32[]{:S(2)}) collective-permute-start(bf16[24,2176]{1,0:T(8,128)(2,1)S(1)} %get-tuple-element.24), channel_id=1, source_target_pairs={{0,2},{4,6},{8,10},{12,14},{2,0},{6,4},{10,8},{14,12},{1,3},{5,7},... | collective-permute-start | bytes 313352 | tf_op jit(solution)/shard_map/ppermute | solution.py:610
  4.5 6.6 %collective-permute-start.2 = (bf16[24,2176]{1,0:T(8,128)(2,1)S(1)}, bf16[24,2176]{1,0:T(8,128)(2,1)S(1)}, u32[]{:S(2)}, u32[]{:S(2)}) collective-permute-start(bf16[24,2176]{1,0:T(8,128)(2,1)S(1)} %get-tuple-element.25), channel_id=1, source_target_pairs={{2,4},{6,8},{10,12},{4,2},{8,6},{12,10},{3,5},{7,9},{11,13},{5,3},... | collective-permute-start | bytes 313352 | tf_op jit(solution)/shard_map/ppermute | solution.py:610
  11.2 2.7 %collective-permute-start.3 = (f32[48,1152]{1,0:T(8,128)S(1)}, f32[48,1152]{1,0:T(8,128)S(1)}, u32[]{:S(2)}, u32[]{:S(2)}) collective-permute-start(f32[48,1152]{1,0:T(8,128)S(1)} %get-tuple-element.32), channel_id=1, source_target_pairs={{0,1},{1,0},{2,3},{3,2},{4,5},{5,4},{6,7},{7,6},{8,9},{9,8},{10,11... | collective-permute-start | bytes 663560 | tf_op jit(solution)/shard_map/ppermute | solution.py:672

commit v10 on v9

--- a/solution.py
+++ b/solution.py
@@ -7,6 +7,7 @@
 from jax.experimental import pallas as pl
 from jax.experimental.pallas import tpu as pltpu
 from jax.sharding import PartitionSpec as P
+
 
 SIGMAS = [1.6 * 2.0 ** (k / 4.0) for k in range(5)]
 LEVELS = len(SIGMAS)
@@ -212,7 +213,7 @@
         ref[:, cols:] = jnp.where(index > NEAR, kept, jnp.where(even, a, b)).astype(BF16)
 
 
-def base_kernel(row_count, tile_base, base_ref, even_ref, odd_ref, _, keep_ref, send_ref, sum_ref):
+def base_kernel(row_count, tile_base, base_ref, even_ref, _, keep_ref, send_ref, sum_ref):
     row, col = mesh_place()
     base_rows, wide = base_ref.shape
     half = wide - LANES
@@ -221,32 +222,28 @@
     even = row % 2 == 0
     is_left = col == 0
     index = lax.broadcasted_iota(jnp.int32, (base_rows, LANES), 0)
-    lane = lax.broadcasted_iota(jnp.int32, (PART, LANES), 1)
-    outside = (lane >= LANES // 4) & (lane < 3 * LANES // 4)
     place = row * tile_base - REACH - 1 + index
     inside = (place >= 0) & (place < row_count * tile_base)
     first_bot = tile_base + REACH + 1 - 6
-
-    def parts(ref_a, ref_b, at):
-        def rows_of(lanes):
-            a, b = ref_a[:, lanes].astype(F32), ref_b[:, lanes].astype(F32)
-            return jnp.where(even, a, b)[NEAR + 1 :]
-
-        if at < half:
-            both = [rows_of(slice(at, at + LANES)), rows_of(slice(half + at, half + at + LANES))]
-        else:
-            value = rows_of(slice(2 * half, 2 * half + LANES))
-            both = [jnp.where(outside, 0.0, v) for v in (value, pltpu.roll(value, LANES // 2, 1))]
-        return jnp.concatenate([both[0], both[1][: SPAN - PART]], axis=0)
-
     for at in range(0, wide, LANES):
         to = slice(at, at + LANES)
+        if at < half:
+            both = [even_ref[:, lanes].astype(F32) for lanes in (to, slice(half + at, half + at + LANES))]
+        else:
+            both = unpack_extra(even_ref[:, 2 * half :].astype(F32))
+        part = jnp.concatenate([both[0][NEAR + 1 :], both[1][NEAR + 1 : NEAR + 1 + SPAN - PART]], axis=0)
         sum_ref[...] = base_ref[:, to]
-        sum_ref[:SPAN, :] += parts(odd_ref, even_ref, at)
-        sum_ref[first_bot : first_bot + SPAN, :] += parts(even_ref, odd_ref, at)
+        sum_ref[:SPAN, :] += jnp.where(even, 0.0, part)
+        sum_ref[first_bot : first_bot + SPAN, :] += jnp.where(even, part, 0.0)
         total = jnp.where(inside, sum_ref[...], 0.0)
         keep_ref[:, to] = jnp.where(is_left, total[:count], total[shift : shift + count])
         send_ref[:, to] = jnp.where(is_left, total[shift : shift + count], total[:count])
+
+
+def unpack_extra(value):
+    lane = lax.broadcasted_iota(jnp.int32, value.shape, 1)
+    outside = (lane >= LANES // 4) & (lane < 3 * LANES // 4)
+    return [jnp.where(outside, 0.0, v) for v in (value, pltpu.roll(value, LANES // 2, 1))]
 
 
 def filter_columns(vh, vl, w_refs, group, cols, lev, emit, after_group, after_level):
@@ -412,7 +409,7 @@
     filter_columns(vh, vl, w_refs, 8, cols, lev, emit, after_group, seam)
 
 
-def coarse_kernel(last_row, keep_ref, other_ref, fine_dog_ref, fine_hess_ref, late_ref,
+def coarse_kernel(last_row, keep_ref, other_ref, odd_ref, odd_other_ref, fine_dog_ref, fine_hess_ref, late_ref,
                   fine_dog_hbm, fine_hess_hbm, dog_hbm, hess_hbm,
                   dog_ref, hess_ref, vh, vl, lev, d1, d2, sems):
     fine_copies = [
@@ -438,18 +435,30 @@
         d[:, LANES + cols :] = zero
 
     strip_rows = keep_ref.shape[0]
-    lh = late_ref[late_ref.shape[0] - LEVELS * tall :, : 3 * strip_rows]
+    height = LEVELS * tall
+    variant = 2 * (row % 2) + col
+    start = pl.multiple_of(late_ref.shape[0] - 4 * height + variant * height, 16)
+    lh = late_ref[pl.ds(start, height), : 3 * strip_rows + 4 * MESSAGE]
+    lp = lh[:, 3 * strip_rows :]
     for at in range(0, cols, BLOCK):
         source = slice(at % half, at % half + BLOCK)
+        second = slice(half + at % half, half + at % half + BLOCK)
         first = is_left if at < half else jnp.logical_not(is_left)
         value = jnp.where(first, keep_ref[:, source], other_ref[:, source])
-        if at in (half - BLOCK, half):
-            extra = jnp.where(first, other_ref[:, half:], keep_ref[:, half:])
-            none = jnp.zeros(extra.shape, F32)
-            value = value + jnp.concatenate([none, extra] if at < half else [extra, none], axis=1)
+        message = [jnp.where(first, odd_ref[:, lanes], odd_other_ref[:, lanes]) for lanes in (source, second)]
+        at_seam = at in (half - BLOCK, half)
+        if at_seam:
+            join = lambda v: jnp.concatenate(
+                [jnp.zeros(v.shape, v.dtype), v] if at < half else [v, jnp.zeros(v.shape, v.dtype)], axis=1
+            )
+            value = value + join(jnp.where(first, other_ref[:, half:], keep_ref[:, half:]))
+            extra = jnp.where(first, odd_other_ref[:, cols:], odd_ref[:, cols:]).astype(F32)
+            extra = [v.astype(BF16) for v in unpack_extra(extra)]
         high, low = split(value)
-        stack = jnp.concatenate([high, low, high], axis=0)
+        stack = jnp.concatenate([high, low, high, *message, *message], axis=0)
         value = mm(lh, stack)
+        if at_seam:
+            value = value + join(mm(lp, jnp.concatenate([*extra, *extra], axis=0)))
         to = slice(LANES + at, LANES + at + BLOCK)
         for s in range(LEVELS):
             vh[s, :, to], vl[s, :, to] = split(value[s * tall : (s + 1) * tall])
@@ -488,6 +497,7 @@
     top[: NEAR + 1] = np.append(np.arange(-NEAR, 0), -1)
     bot = np.full(MESSAGE, nowhere)
     bot[: NEAR + 1] = rows + np.append(np.arange(NEAR), 0)
+
     def matrix(sigma, centres, valid, inputs, use_low):
         high, low = two_parts(row_matrix(sigma, centres, inputs) * valid[:, None])
         return np.where(use_low[None, :], low.astype(np.float32), high.astype(np.float32)).astype(BF16)
@@ -522,11 +532,18 @@
     inputs = np.arange(padded) - REACH - 1
     centres = np.arange(-PAD, strip + PAD)
     valid = ((centres >= -1) & (centres <= strip)).astype(np.float32)
-    parts = []
-    for s in SIGMAS:
-        high, low = two_parts(row_matrix(s, centres, inputs) * valid[:, None])
-        parts.append(np.concatenate([high, high, low], axis=1))
-    return np.concatenate(parts)
+    variants = []
+    for parity in range(2):
+        for core in range(2):
+            first = (2 * strip + REACH + 1 - 6) * parity - strip * core - REACH - 1
+            message = np.full(2 * MESSAGE, -1000)
+            message[NEAR + 1 : MESSAGE] = first + np.arange(PART)
+            message[MESSAGE + NEAR + 1 : 2 * MESSAGE - 1] = first + np.arange(PART, SPAN)
+            for s in SIGMAS:
+                high, low = two_parts(row_matrix(s, centres, inputs) * valid[:, None])
+                more_high, more_low = two_parts(row_matrix(s, centres, message) * valid[:, None])
+                variants.append(np.concatenate([high, high, low, more_high, more_low], axis=1))
+    return np.concatenate(variants)
 
 
 def joined(matrices, columns=BLOCK):
@@ -545,10 +562,6 @@
 
 def limit(mib):
     return pltpu.CompilerParams(vmem_limit_bytes=mib * 2**20)
-
-
-def like(value):
-    return jax.ShapeDtypeStruct(value.shape, value.dtype)
 
 
 def far(value):
@@ -609,7 +622,8 @@
         pairs = [(i, i + 1) for i in range(first, row_count - 1, 2)]
         return lax.ppermute(value, "row", pairs + [(j, i) for i, j in pairs])
 
-    even, odd = swap(to_even, 0), swap(to_odd, 1)
+    even = swap(to_even, 0)
+    odd = swap(to_odd, 1)
 
     fine_shapes = (
         jax.ShapeDtypeStruct((4, rows, cols), BF16),
@@ -663,19 +677,20 @@
             jax.ShapeDtypeStruct((strip_rows, cols // 2 + LANES), F32),
             jax.ShapeDtypeStruct((strip_rows, cols // 2 + LANES), F32),
         ),
-        in_specs=vmem_specs(3) + [pl.BlockSpec(memory_space=pl.ANY)],
+        in_specs=vmem_specs(2) + [pl.BlockSpec(memory_space=pl.ANY)],
         out_specs=tuple(vmem_specs(2)),
         scratch_shapes=[pltpu.VMEM((base_rows, LANES), F32)],
         compiler_params=limit(4),
         name="base",
-    )(base, even, odd, hess_fine)
+    )(base, even, rim)
     other = lax.ppermute(send, "col", [(0, 1), (1, 0)])
+    odd_other = lax.ppermute(odd, "col", [(0, 1), (1, 0)])
     dog_fine, hess_fine = finish(False, odd, dog_fine, hess_fine)
 
     return pl.pallas_call(
         functools.partial(coarse_kernel, row_count - 1),
         out_shape=fine_shapes + coarse_shapes,
-        in_specs=vmem_specs(5),
+        in_specs=vmem_specs(7),
         out_specs=tuple(far_specs(4)),
         scratch_shapes=[
             pltpu.VMEM((4, strip, cols), BF16),
@@ -685,7 +700,7 @@
         ],
         compiler_params=limit(12),
         name="coarse",
-    )(keep, other, dog_fine, hess_fine, late)
+    )(keep, other, odd, odd_other, dog_fine, hess_fine, late)
 
 
 def solution(mesh):

time: 16.1 us -> 17.1 us (1.062)
  starting transfers between devices: 5.61 us -> 6.51 us
    ppermute x0 -> x1, starting transfers between devices: none -> 1.49 us  [local(): odd_other = lax.ppermute(odd, 'col', [(0, 1), (1, 0)])]
    ppermute x1, starting transfers between devices: 1.55 us -> 0.97 us  [local(): other = lax.ppermute(send, 'col', [(0, 1), (1, 0)])]
  transfers between devices with their start and end apart: 4 -> 5, of which waited for: 2 -> 2; matrix products, arithmetic and copies ran while one was open for 0% -> 0% of each run, Pallas kernels for 29% -> 28%
where the time goes in v10:
time: 17.1 us; the launch traced here: 17 us
  Pallas kernels  8.39 us (49%)
  starting transfers between devices  6.51 us (38%)
  waiting for transfers between devices  1.31 us (8%)
  between operations  0.74 us (4%)
    ppermute x2, starting transfers between devices, swap(): return lax.ppermute(value, 'row', pairs + [(j, i) for i, j in pairs])  3.31 us
    pallas_call x2, Pallas kernels, finish(): pl.pallas_call(functools.partial(outer_kernel, row_count - 1, one_hop), o...  2.35 us
    pallas_call x1, Pallas kernels, local(): pl.pallas_call(inner_kernel, out_shape=(*fine_shapes, jax.ShapeDtypeStruc...  2.29 us
    pallas_call x1, Pallas kernels, local(): pl.pallas_call(functools.partial(coarse_kernel, row_count - 1), out_shape...  2.01 us
    ppermute x1, starting transfers between devices, local(): odd_other = lax.ppermute(odd, 'col', [(0, 1), (1, 0)])  1.49 us
    ppermute x2, waiting for transfers between devices, swap(): return lax.ppermute(value, 'row', pairs + [(j, i) for i, j in pairs])  1.19 us
    ppermute x1, starting transfers between devices, local(): other = lax.ppermute(send, 'col', [(0, 1), (1, 0)])  0.97 us
    pallas_call x1, Pallas kernels, local(): pl.pallas_call(border_kernel, out_shape=jax.ShapeDtypeStruct((rows, LANES...  0.85 us
  transfers between devices with their start and end apart: 5, of which 2 were waited for; matrix products, arithmetic and copies ran while one was open for 0% of the time, Pallas kernels for 28%

profile of v10, /device:TPU:11, one launch (start us, length us, event | category | flops | bytes accessed | tf_op | source)
XLA Modules:
  0.0 17.0 jit_solution(2241189077554775385)
XLA Ops:
  0.6 0.0 copy-start.2
  0.6 0.0 copy-start.1
  0.7 0.9 %border.1 = f32[64,128]{1,0:T(8,128)S(1)} custom-call(f32[64,2048]{1,0:T(8,128)} %x_hbm.1), custom_call_target="tpu_custom_call" | custom-call | flops 2000000000 | bytes 10000000 | tf_op jit(solution)/shard_map/border/pallas_call | solution.py:587
  1.5 0.0 copy-start
  1.5 0.7 %collective-permute-start = (f32[64,128]{1,0:T(8,128)S(1)}, f32[64,128]{1,0:T(8,128)S(1)}, u32[]{:S(2)}, u32[]{:S(2)}) collective-permute-start(f32[64,128]{1,0:T(8,128)S(1)} %border.1), channel_id=1, source_target_pairs={{0,1},{1,0},{2,3},{3,2},{4,5},{5,4},{6,7},{7,6},{8,9},{9,8},{10,11... | collective-permute-start | bytes 98312 | tf_op jit(solution)/shard_map/ppermute | solution.py:597
  2.3 0.0 copy-done.2
  2.3 0.0 copy-done.1
  2.3 0.7 %send.1 = (bf16[128,2176]{1,0:T(8,128)(2,1)S(1)}, bf16[24,2176]{1,0:T(8,128)(2,1)S(1)}, bf16[24,2176]{1,0:T(8,128)(2,1)S(1)}, f32[64,1152]{1,0:T(8,128)S(1)}) custom-call(f32[64,2048]{1,0:T(8,128)S(1)} %copy-done.1, bf16[832,256]{1,0:T(8,128)(2,1)S(1)} %copy-done.2), custom_call_target="tpu_custom_call" | custom-call | flops 1000000000 | bytes 1000000 | tf_op jit(solution)/shard_map/send/pallas_call | solution.py:598
  3.0 0.1 collective-permute-done.side_ref
  3.2 1.3 %collective-permute-start.1 = (bf16[24,2176]{1,0:T(8,128)(2,1)S(1)}, bf16[24,2176]{1,0:T(8,128)(2,1)S(1)}, u32[]{:S(2)}, u32[]{:S(2)}) collective-permute-start(bf16[24,2176]{1,0:T(8,128)(2,1)S(1)} %get-tuple-element.24), channel_id=1, source_target_pairs={{0,2},{4,6},{8,10},{12,14},{2,0},{6,4},{10,8},{14,12},{1,3},{5,7},... | collective-permute-start | bytes 313352 | tf_op jit(solution)/shard_map/ppermute | solution.py:623
  4.5 2.0 %collective-permute-start.3 = (bf16[24,2176]{1,0:T(8,128)(2,1)S(1)}, bf16[24,2176]{1,0:T(8,128)(2,1)S(1)}, u32[]{:S(2)}, u32[]{:S(2)}) collective-permute-start(bf16[24,2176]{1,0:T(8,128)(2,1)S(1)} %get-tuple-element.29), channel_id=1, source_target_pairs={{2,4},{6,8},{10,12},{4,2},{8,6},{12,10},{3,5},{7,9},{11,13},{5,3},... | collective-permute-start | bytes 313352 | tf_op jit(solution)/shard_map/ppermute | solution.py:623
  6.5 0.0 copy-done
  6.5 2.3 %inner.1 = (bf16[4,64,2048]{2,1,0:T(8,128)(2,1)S(1)}, bf16[2,64,2048]{2,1,0:T(8,128)(2,1)S(1)}, f32[4,48,2304]{2,1,0:T(8,128)S(1)}) custom-call(bf16[128,2176]{1,0:T(8,128)(2,1)S(1)} %get-tuple-element.25.own_ref, bf16[5120,256]{1,0:T(8,128)(2,1)S(1)} %copy-done), custom_call_target="tpu_custom_call" | custom-call | flops 2000000000 | bytes 10000000 | tf_op jit(solution)/shard_map/inner/pallas_call | solution.py:648
  8.8 0.0 collective-permute-done.1.even_ref.message_ref
  8.8 0.1 base.1
  8.9 1.0 %collective-permute-start.2 = (f32[48,1152]{1,0:T(8,128)S(1)}, f32[48,1152]{1,0:T(8,128)S(1)}, u32[]{:S(2)}, u32[]{:S(2)}) collective-permute-start(f32[48,1152]{1,0:T(8,128)S(1)} %get-tuple-element.28), channel_id=1, source_target_pairs={{0,1},{1,0},{2,3},{3,2},{4,5},{5,4},{6,7},{7,6},{8,9},{9,8},{10,11... | collective-permute-start | bytes 663560 | tf_op jit(solution)/shard_map/ppermute | solution.py:686
  9.9 1.2 %collective-permute-done.3.message_ref.odd_ref = bf16[24,2176]{1,0:T(8,128)(2,1)S(1)} collective-permute-done((bf16[24,2176]{1,0:T(8,128)(2,1)S(1)}, bf16[24,2176]{1,0:T(8,128)(2,1)S(1)}, u32[]{:S(2)}, u32[]{:S(2)}) %collective-permute-start.3) | collective-permute-done | bytes 104480 | tf_op jit(solution)/shard_map/ppermute | solution.py:623
  11.1 1.5 %collective-permute-start.4 = (bf16[24,2176]{1,0:T(8,128)(2,1)S(1)}, bf16[24,2176]{1,0:T(8,128)(2,1)S(1)}, u32[]{:S(2)}, u32[]{:S(2)}) collective-permute-start(bf16[24,2176]{1,0:T(8,128)(2,1)S(1)} %collective-permute-done.3.message_ref.odd_ref), channel_id=1, source_target_pairs={{0,1},{1,0},{2,3},{3,2},{4,5},{5,4},{6,7},{7,6},{8,9},{9,8},{10,11... | collective-permute-start | bytes 313352 | tf_op jit(solution)/shard_map/ppermute | solution.py:687
  12.6 1.2 %outer.2 = (bf16[4,64,2048]{2,1,0:T(8,128)(2,1)S(1)}, bf16[2,64,2048]{2,1,0:T(8,128)(2,1)S(1)}) custom-call(bf16[24,2176]{1,0:T(8,128)(2,1)S(1)} %collective-permute-done.1.even_ref.message_ref, bf16[128,2176]{1,0:T(8,128)(2,1)S(1)} %get-tuple-element.25.own_ref, bf16[5120,256]{1,0:T(8,128)(2,1)S(1)} %copy-done, ...), custom_call_target="tpu_custom_call", output_to_operand_aliasing={{0}: (4, {}), {1}: (5, {})} | custom-call | flops 1000000000 | bytes 1000000 | tf_op jit(solution)/shard_map/outer/pallas_call | solution.py:660
  13.7 1.2 %outer.3 = (bf16[4,64,2048]{2,1,0:T(8,128)(2,1)S(1)}, bf16[2,64,2048]{2,1,0:T(8,128)(2,1)S(1)}) custom-call(bf16[24,2176]{1,0:T(8,128)(2,1)S(1)} %collective-permute-done.3.message_ref.odd_ref, bf16[128,2176]{1,0:T(8,128)(2,1)S(1)} %get-tuple-element.25.own_ref, bf16[5120,256]{1,0:T(8,128)(2,1)S(1)} %copy-done, ...), custom_call_target="tpu_custom_call", output_to_operand_aliasing={{0}: (4, {}), {1}: (5, {})} | custom-call | flops 1000000000 | bytes 1000000 | tf_op jit(solution)/shard_map/outer/pallas_call | solution.py:660
  14.9 0.0 collective-permute-done.4.odd_other_ref
  15.0 0.0 collective-permute-done.2.other_ref
  15.0 2.0 %coarse.1 = (bf16[4,64,2048]{2,1,0:T(8,128)(2,1)}, bf16[2,64,2048]{2,1,0:T(8,128)(2,1)}, bf16[4,16,2048]{2,1,0:T(8,128)(2,1)}, bf16[2,16,2048]{2,1,0:T(8,128)(2,1)}) custom-call(f32[48,1152]{1,0:T(8,128)S(1)} %get-tuple-element.27.keep_ref, f32[48,1152]{1,0:T(8,128)S(1)} %collective-permute-done.2.other_ref, ...), custom_call_target="tpu_custom_call" | custom-call | tf_op jit(solution)/shard_map/coarse/pallas_call | solution.py:690
  (1 shorter events, 0.0 us)
Async XLA Ops:
  0.6 1.6 %copy-start.2 = (bf16[832,256]{1,0:T(8,128)(2,1)S(1)}, bf16[832,256]{1,0:T(8,128)(2,1)}, u32[]{:S(2)}) copy-start(bf16[832,256]{1,0:T(8,128)(2,1)} %constant.4.clone.early_ref) | copy-start | bytes 1277956
  0.6 1.6 %copy-start.1 = (f32[64,2048]{1,0:T(8,128)S(1)}, f32[64,2048]{1,0:T(8,128)}, u32[]{:S(2)}) copy-start(f32[64,2048]{1,0:T(8,128)} %x_hbm.1) | copy-start | bytes 1572868
  1.5 5.0 %copy-start = (bf16[5120,256]{1,0:T(8,128)(2,1)S(1)}, bf16[5120,256]{1,0:T(8,128)(2,1)}, u32[]{:S(2)}) copy-start(bf16[5120,256]{1,0:T(8,128)(2,1)} %constant.5.clone.late_ref) | copy-start | bytes 7864324
  1.5 1.6 %collective-permute-start = (f32[64,128]{1,0:T(8,128)S(1)}, f32[64,128]{1,0:T(8,128)S(1)}, u32[]{:S(2)}, u32[]{:S(2)}) collective-permute-start(f32[64,128]{1,0:T(8,128)S(1)} %border.1), channel_id=1, source_target_pairs={{0,1},{1,0},{2,3},{3,2},{4,5},{5,4},{6,7},{7,6},{8,9},{9,8},{10,11... | collective-permute-start | bytes 98312 | tf_op jit(solution)/shard_map/ppermute | solution.py:597
  3.2 5.6 %collective-permute-start.1 = (bf16[24,2176]{1,0:T(8,128)(2,1)S(1)}, bf16[24,2176]{1,0:T(8,128)(2,1)S(1)}, u32[]{:S(2)}, u32[]{:S(2)}) collective-permute-start(bf16[24,2176]{1,0:T(8,128)(2,1)S(1)} %get-tuple-element.24), channel_id=1, source_target_pairs={{0,2},{4,6},{8,10},{12,14},{2,0},{6,4},{10,8},{14,12},{1,3},{5,7},... | collective-permute-start | bytes 313352 | tf_op jit(solution)/shard_map/ppermute | solution.py:623
  4.5 6.6 %collective-permute-start.3 = (bf16[24,2176]{1,0:T(8,128)(2,1)S(1)}, bf16[24,2176]{1,0:T(8,128)(2,1)S(1)}, u32[]{:S(2)}, u32[]{:S(2)}) collective-permute-start(bf16[24,2176]{1,0:T(8,128)(2,1)S(1)} %get-tuple-element.29), channel_id=1, source_target_pairs={{2,4},{6,8},{10,12},{4,2},{8,6},{12,10},{3,5},{7,9},{11,13},{5,3},... | collective-permute-start | bytes 313352 | tf_op jit(solution)/shard_map/ppermute | solution.py:623
  8.9 6.0 %collective-permute-start.2 = (f32[48,1152]{1,0:T(8,128)S(1)}, f32[48,1152]{1,0:T(8,128)S(1)}, u32[]{:S(2)}, u32[]{:S(2)}) collective-permute-start(f32[48,1152]{1,0:T(8,128)S(1)} %get-tuple-element.28), channel_id=1, source_target_pairs={{0,1},{1,0},{2,3},{3,2},{4,5},{5,4},{6,7},{7,6},{8,9},{9,8},{10,11... | collective-permute-start | bytes 663560 | tf_op jit(solution)/shard_map/ppermute | solution.py:686
  11.1 3.9 %collective-permute-start.4 = (bf16[24,2176]{1,0:T(8,128)(2,1)S(1)}, bf16[24,2176]{1,0:T(8,128)(2,1)S(1)}, u32[]{:S(2)}, u32[]{:S(2)}) collective-permute-start(bf16[24,2176]{1,0:T(8,128)(2,1)S(1)} %collective-permute-done.3.message_ref.odd_ref), channel_id=1, source_target_pairs={{0,1},{1,0},{2,3},{3,2},{4,5},{5,4},{6,7},{7,6},{8,9},{9,8},{10,11... | collective-permute-start | bytes 313352 | tf_op jit(solution)/shard_map/ppermute | solution.py:687

commit v11 on v10

--- a/solution.py
+++ b/solution.py
@@ -11,6 +11,7 @@
 
 SIGMAS = [1.6 * 2.0 ** (k / 4.0) for k in range(5)]
 LEVELS = len(SIGMAS)
+ORDER = (1, 2, 3, 0, 4)
 REACH = 12
 LANES = 128
 BLOCK = 256
@@ -249,7 +250,7 @@
 def filter_columns(vh, vl, w_refs, group, cols, lev, emit, after_group, after_level):
     wc_ref, wl_ref, we_ref = w_refs
     tall = vh.shape[1]
-    for s in range(LEVELS):
+    for s in ORDER:
         band = slice(s * BLOCK, (s + 1) * BLOCK)
         for g in range(0, cols // BLOCK, group):
             ats = [LANES + BLOCK * (g + i) for i in range(group)]
@@ -261,12 +262,15 @@
             )
             for i, at in enumerate(ats):
                 new = value[i * tall : (i + 1) * tall]
-                if s > 0:
-                    emit(s - 1, at, new - lev[:, at : at + BLOCK])
-                if s + 1 < LEVELS:
-                    lev[:, at : at + BLOCK] = new
-            if s >= 3:
-                after_group(s - 3, g * BLOCK // LANES, group * BLOCK // LANES)
+                to = slice(at, at + BLOCK)
+                if s == 0:
+                    emit(0, at, lev[0, :, to] - new)
+                elif s > 1:
+                    emit(s - 1, at, new - lev[0 if s == 2 else 1, :, to])
+                if s in (1, 2, 3):
+                    lev[0 if s == 1 else 1, :, to] = new
+            if s in (0, 3):
+                after_group(0 if s == 3 else 1, g * BLOCK // LANES, group * BLOCK // LANES)
         after_level(s)
 
 
@@ -297,11 +301,11 @@
         band = slice(s * BLOCK, (s + 1) * BLOCK)
         new = mm(high, wc_ref[band]) + mm(low, wc_ref[band]) + mm(high, wl_ref[band])
         if s > 1:
-            d = new - lev[:, cols + 2 * LANES :]
+            d = new - lev[0, :, cols + 2 * LANES :]
             emit(s - 1, 0, jnp.where(is_left, 0.0, d[:, :LANES]))
             emit(s - 1, cols + LANES, jnp.where(is_left, d[:, LANES:], 0.0))
         if s < 3:
-            lev[:, cols + 2 * LANES :] = new
+            lev[0, :, cols + 2 * LANES :] = new
 
     return seam
 
@@ -471,20 +475,25 @@
             diffs[k][PAD : PAD + rows, to] = d[PAD : PAD + rows]
             diffs[k][PAD + rows :, to] = jnp.where((row == last_row) & (col == 1), 0.0, d[PAD + rows :])
 
-    dog_copy = pltpu.make_async_copy(dog_ref, dog_hbm, sems.at[2])
-    hess_copies = [pltpu.make_async_copy(hess_ref.at[m], hess_hbm.at[m], sems.at[3 + m]) for m in range(2)]
+    dog_copies = [pltpu.make_async_copy(dog_ref.at[k], dog_hbm.at[k], sems.at[4 + k]) for k in range(4)]
+    hess_copies = [pltpu.make_async_copy(hess_ref.at[m], hess_hbm.at[m], sems.at[2 + m]) for m in range(2)]
 
     def after_group(m, first, count):
         def put(t, value):
             hess_ref[m, :, t * LANES : (t + 1) * LANES] = value
 
-        if m == 1:
-            dog_copy.start()
         hess_tiles(diffs[m + 1], 0, rows, first, count, 200000.0, put)
-        hess_copies[m].start()
-
-    filter_columns(vh, vl, band_refs(late_ref), 8, cols, lev, emit, after_group, lambda s: None)
-    for copy in fine_copies + [dog_copy] + hess_copies:
+
+    def after_level(s):
+        if s == 0:
+            for copy in (dog_copies[1], dog_copies[2], hess_copies[0]):
+                copy.start()
+        if s == 4:
+            for copy in (hess_copies[1], dog_copies[0], dog_copies[3]):
+                copy.start()
+
+    filter_columns(vh, vl, band_refs(late_ref), 8, cols, lev, emit, after_group, after_level)
+    for copy in fine_copies + dog_copies + hess_copies:
         copy.wait()
 
 
@@ -639,7 +648,7 @@
         return [
             pltpu.VMEM((LEVELS, height, padded_cols), BF16),
             pltpu.VMEM((LEVELS, height, padded_cols), BF16),
-            pltpu.VMEM((height, padded_cols + seam), F32),
+            pltpu.VMEM((2, height, padded_cols + seam), F32),
             pltpu.VMEM((count, padded_cols), F32),
             pltpu.VMEM((count, padded_cols), F32),
         ]
@@ -696,7 +705,7 @@
             pltpu.VMEM((4, strip, cols), BF16),
             pltpu.VMEM((2, strip, cols), BF16),
             *scratch(small, small, 0),
-            pltpu.SemaphoreType.DMA((5,)),
+            pltpu.SemaphoreType.DMA((8,)),
         ],
         compiler_params=limit(12),
         name="coarse",

time: 17.1 us -> 17.5 us (1.023)
  Pallas kernels: 8.39 us -> 8.75 us
    pallas_call x1, Pallas kernels: 2.01 us -> 2.48 us  [local(): pl.pallas_call(functools.partial(coarse_kernel, row_count - 1), out_shape...]
  transfers between devices with their start and end apart: 5 -> 5, of which waited for: 2 -> 2; matrix products, arithmetic and copies ran while one was open for 0% -> 0% of each run, Pallas kernels for 28% -> 27%
where the time goes in v11:
time: 17.5 us; the launch traced here: 17.3 us
  Pallas kernels  8.75 us (50%)
  starting transfers between devices  6.51 us (37%)
  waiting for transfers between devices  1.31 us (7%)
  between operations  0.74 us (4%)
    ppermute x2, starting transfers between devices, swap(): return lax.ppermute(value, 'row', pairs + [(j, i) for i, j in pairs])  3.31 us
    pallas_call x1, Pallas kernels, local(): pl.pallas_call(functools.partial(coarse_kernel, row_count - 1), out_shape...  2.48 us
    pallas_call x1, Pallas kernels, local(): pl.pallas_call(inner_kernel, out_shape=(*fine_shapes, jax.ShapeDtypeStruc...  2.3 us
    pallas_call x2, Pallas kernels, finish(): pl.pallas_call(functools.partial(outer_kernel, row_count - 1, one_hop), o...  2.23 us
    ppermute x1, starting transfers between devices, local(): odd_other = lax.ppermute(odd, 'col', [(0, 1), (1, 0)])  1.49 us
    ppermute x2, waiting for transfers between devices, swap(): return lax.ppermute(value, 'row', pairs + [(j, i) for i, j in pairs])  1.19 us
    ppermute x1, starting transfers between devices, local(): other = lax.ppermute(send, 'col', [(0, 1), (1, 0)])  0.97 us
    pallas_call x1, Pallas kernels, local(): pl.pallas_call(border_kernel, out_shape=jax.ShapeDtypeStruct((rows, LANES...  0.85 us
  transfers between devices with their start and end apart: 5, of which 2 were waited for; matrix products, arithmetic and copies ran while one was open for 0% of the time, Pallas kernels for 27%

profile of v11, /device:TPU:11, one launch (start us, length us, event | category | flops | bytes accessed | tf_op | source)
XLA Modules:
  0.0 17.3 jit_solution(4032613410467781147)
XLA Ops:
  0.6 0.0 copy-start.2
  0.6 0.0 copy-start.1
  0.7 0.9 %border.1 = f32[64,128]{1,0:T(8,128)S(1)} custom-call(f32[64,2048]{1,0:T(8,128)} %x_hbm.1), custom_call_target="tpu_custom_call" | custom-call | flops 2000000000 | bytes 10000000 | tf_op jit(solution)/shard_map/border/pallas_call | solution.py:596
  1.5 0.0 copy-start
  1.5 0.7 %collective-permute-start = (f32[64,128]{1,0:T(8,128)S(1)}, f32[64,128]{1,0:T(8,128)S(1)}, u32[]{:S(2)}, u32[]{:S(2)}) collective-permute-start(f32[64,128]{1,0:T(8,128)S(1)} %border.1), channel_id=1, source_target_pairs={{0,1},{1,0},{2,3},{3,2},{4,5},{5,4},{6,7},{7,6},{8,9},{9,8},{10,11... | collective-permute-start | bytes 98312 | tf_op jit(solution)/shard_map/ppermute | solution.py:606
  2.3 0.0 copy-done.2
  2.3 0.0 copy-done.1
  2.3 0.7 %send.1 = (bf16[128,2176]{1,0:T(8,128)(2,1)S(1)}, bf16[24,2176]{1,0:T(8,128)(2,1)S(1)}, bf16[24,2176]{1,0:T(8,128)(2,1)S(1)}, f32[64,1152]{1,0:T(8,128)S(1)}) custom-call(f32[64,2048]{1,0:T(8,128)S(1)} %copy-done.1, bf16[832,256]{1,0:T(8,128)(2,1)S(1)} %copy-done.2), custom_call_target="tpu_custom_call" | custom-call | flops 1000000000 | bytes 1000000 | tf_op jit(solution)/shard_map/send/pallas_call | solution.py:607
  3.0 0.1 collective-permute-done.side_ref
  3.2 1.3 %collective-permute-start.1 = (bf16[24,2176]{1,0:T(8,128)(2,1)S(1)}, bf16[24,2176]{1,0:T(8,128)(2,1)S(1)}, u32[]{:S(2)}, u32[]{:S(2)}) collective-permute-start(bf16[24,2176]{1,0:T(8,128)(2,1)S(1)} %get-tuple-element.24), channel_id=1, source_target_pairs={{0,2},{4,6},{8,10},{12,14},{2,0},{6,4},{10,8},{14,12},{1,3},{5,7},... | collective-permute-start | bytes 313352 | tf_op jit(solution)/shard_map/ppermute | solution.py:632
  4.5 2.0 %collective-permute-start.3 = (bf16[24,2176]{1,0:T(8,128)(2,1)S(1)}, bf16[24,2176]{1,0:T(8,128)(2,1)S(1)}, u32[]{:S(2)}, u32[]{:S(2)}) collective-permute-start(bf16[24,2176]{1,0:T(8,128)(2,1)S(1)} %get-tuple-element.29), channel_id=1, source_target_pairs={{2,4},{6,8},{10,12},{4,2},{8,6},{12,10},{3,5},{7,9},{11,13},{5,3},... | collective-permute-start | bytes 313352 | tf_op jit(solution)/shard_map/ppermute | solution.py:632
  6.5 0.0 copy-done
  6.5 2.3 %inner.1 = (bf16[4,64,2048]{2,1,0:T(8,128)(2,1)S(1)}, bf16[2,64,2048]{2,1,0:T(8,128)(2,1)S(1)}, f32[4,48,2304]{2,1,0:T(8,128)S(1)}) custom-call(bf16[128,2176]{1,0:T(8,128)(2,1)S(1)} %get-tuple-element.25.own_ref, bf16[5120,256]{1,0:T(8,128)(2,1)S(1)} %copy-done), custom_call_target="tpu_custom_call" | custom-call | flops 2000000000 | bytes 10000000 | tf_op jit(solution)/shard_map/inner/pallas_call | solution.py:657
  8.8 0.0 collective-permute-done.1.even_ref.message_ref
  8.8 0.1 base.1
  8.9 1.0 %collective-permute-start.2 = (f32[48,1152]{1,0:T(8,128)S(1)}, f32[48,1152]{1,0:T(8,128)S(1)}, u32[]{:S(2)}, u32[]{:S(2)}) collective-permute-start(f32[48,1152]{1,0:T(8,128)S(1)} %get-tuple-element.28), channel_id=1, source_target_pairs={{0,1},{1,0},{2,3},{3,2},{4,5},{5,4},{6,7},{7,6},{8,9},{9,8},{10,11... | collective-permute-start | bytes 663560 | tf_op jit(solution)/shard_map/ppermute | solution.py:695
  9.9 1.2 %collective-permute-done.3.message_ref.odd_ref = bf16[24,2176]{1,0:T(8,128)(2,1)S(1)} collective-permute-done((bf16[24,2176]{1,0:T(8,128)(2,1)S(1)}, bf16[24,2176]{1,0:T(8,128)(2,1)S(1)}, u32[]{:S(2)}, u32[]{:S(2)}) %collective-permute-start.3) | collective-permute-done | bytes 104480 | tf_op jit(solution)/shard_map/ppermute | solution.py:632
  11.1 1.5 %collective-permute-start.4 = (bf16[24,2176]{1,0:T(8,128)(2,1)S(1)}, bf16[24,2176]{1,0:T(8,128)(2,1)S(1)}, u32[]{:S(2)}, u32[]{:S(2)}) collective-permute-start(bf16[24,2176]{1,0:T(8,128)(2,1)S(1)} %collective-permute-done.3.message_ref.odd_ref), channel_id=1, source_target_pairs={{0,1},{1,0},{2,3},{3,2},{4,5},{5,4},{6,7},{7,6},{8,9},{9,8},{10,11... | collective-permute-start | bytes 313352 | tf_op jit(solution)/shard_map/ppermute | solution.py:696
  12.6 1.1 %outer.2 = (bf16[4,64,2048]{2,1,0:T(8,128)(2,1)S(1)}, bf16[2,64,2048]{2,1,0:T(8,128)(2,1)S(1)}) custom-call(bf16[24,2176]{1,0:T(8,128)(2,1)S(1)} %collective-permute-done.1.even_ref.message_ref, bf16[128,2176]{1,0:T(8,128)(2,1)S(1)} %get-tuple-element.25.own_ref, bf16[5120,256]{1,0:T(8,128)(2,1)S(1)} %copy-done, ...), custom_call_target="tpu_custom_call", output_to_operand_aliasing={{0}: (4, {}), {1}: (5, {})} | custom-call | flops 1000000000 | bytes 1000000 | tf_op jit(solution)/shard_map/outer/pallas_call | solution.py:669
  13.7 1.1 %outer.3 = (bf16[4,64,2048]{2,1,0:T(8,128)(2,1)S(1)}, bf16[2,64,2048]{2,1,0:T(8,128)(2,1)S(1)}) custom-call(bf16[24,2176]{1,0:T(8,128)(2,1)S(1)} %collective-permute-done.3.message_ref.odd_ref, bf16[128,2176]{1,0:T(8,128)(2,1)S(1)} %get-tuple-element.25.own_ref, bf16[5120,256]{1,0:T(8,128)(2,1)S(1)} %copy-done, ...), custom_call_target="tpu_custom_call", output_to_operand_aliasing={{0}: (4, {}), {1}: (5, {})} | custom-call | flops 1000000000 | bytes 1000000 | tf_op jit(solution)/shard_map/outer/pallas_call | solution.py:669
  14.8 0.0 collective-permute-done.4.odd_other_ref
  14.8 0.0 collective-permute-done.2.other_ref
  14.8 2.5 %coarse.1 = (bf16[4,64,2048]{2,1,0:T(8,128)(2,1)}, bf16[2,64,2048]{2,1,0:T(8,128)(2,1)}, bf16[4,16,2048]{2,1,0:T(8,128)(2,1)}, bf16[2,16,2048]{2,1,0:T(8,128)(2,1)}) custom-call(f32[48,1152]{1,0:T(8,128)S(1)} %get-tuple-element.27.keep_ref, f32[48,1152]{1,0:T(8,128)S(1)} %collective-permute-done.2.other_ref, ...), custom_call_target="tpu_custom_call" | custom-call | tf_op jit(solution)/shard_map/coarse/pallas_call | solution.py:699
  (1 shorter events, 0.0 us)
Async XLA Ops:
  0.6 1.6 %copy-start.2 = (bf16[832,256]{1,0:T(8,128)(2,1)S(1)}, bf16[832,256]{1,0:T(8,128)(2,1)}, u32[]{:S(2)}) copy-start(bf16[832,256]{1,0:T(8,128)(2,1)} %constant.4.clone.early_ref) | copy-start | bytes 1277956
  0.6 1.6 %copy-start.1 = (f32[64,2048]{1,0:T(8,128)S(1)}, f32[64,2048]{1,0:T(8,128)}, u32[]{:S(2)}) copy-start(f32[64,2048]{1,0:T(8,128)} %x_hbm.1) | copy-start | bytes 1572868
  1.5 5.0 %copy-start = (bf16[5120,256]{1,0:T(8,128)(2,1)S(1)}, bf16[5120,256]{1,0:T(8,128)(2,1)}, u32[]{:S(2)}) copy-start(bf16[5120,256]{1,0:T(8,128)(2,1)} %constant.5.clone.late_ref) | copy-start | bytes 7864324
  1.5 1.6 %collective-permute-start = (f32[64,128]{1,0:T(8,128)S(1)}, f32[64,128]{1,0:T(8,128)S(1)}, u32[]{:S(2)}, u32[]{:S(2)}) collective-permute-start(f32[64,128]{1,0:T(8,128)S(1)} %border.1), channel_id=1, source_target_pairs={{0,1},{1,0},{2,3},{3,2},{4,5},{5,4},{6,7},{7,6},{8,9},{9,8},{10,11... | collective-permute-start | bytes 98312 | tf_op jit(solution)/shard_map/ppermute | solution.py:606
  3.2 5.6 %collective-permute-start.1 = (bf16[24,2176]{1,0:T(8,128)(2,1)S(1)}, bf16[24,2176]{1,0:T(8,128)(2,1)S(1)}, u32[]{:S(2)}, u32[]{:S(2)}) collective-permute-start(bf16[24,2176]{1,0:T(8,128)(2,1)S(1)} %get-tuple-element.24), channel_id=1, source_target_pairs={{0,2},{4,6},{8,10},{12,14},{2,0},{6,4},{10,8},{14,12},{1,3},{5,7},... | collective-permute-start | bytes 313352 | tf_op jit(solution)/shard_map/ppermute | solution.py:632
  4.5 6.6 %collective-permute-start.3 = (bf16[24,2176]{1,0:T(8,128)(2,1)S(1)}, bf16[24,2176]{1,0:T(8,128)(2,1)S(1)}, u32[]{:S(2)}, u32[]{:S(2)}) collective-permute-start(bf16[24,2176]{1,0:T(8,128)(2,1)S(1)} %get-tuple-element.29), channel_id=1, source_target_pairs={{2,4},{6,8},{10,12},{4,2},{8,6},{12,10},{3,5},{7,9},{11,13},{5,3},... | collective-permute-start | bytes 313352 | tf_op jit(solution)/shard_map/ppermute | solution.py:632
  8.9 5.9 %collective-permute-start.2 = (f32[48,1152]{1,0:T(8,128)S(1)}, f32[48,1152]{1,0:T(8,128)S(1)}, u32[]{:S(2)}, u32[]{:S(2)}) collective-permute-start(f32[48,1152]{1,0:T(8,128)S(1)} %get-tuple-element.28), channel_id=1, source_target_pairs={{0,1},{1,0},{2,3},{3,2},{4,5},{5,4},{6,7},{7,6},{8,9},{9,8},{10,11... | collective-permute-start | bytes 663560 | tf_op jit(solution)/shard_map/ppermute | solution.py:695
  11.1 3.7 %collective-permute-start.4 = (bf16[24,2176]{1,0:T(8,128)(2,1)S(1)}, bf16[24,2176]{1,0:T(8,128)(2,1)S(1)}, u32[]{:S(2)}, u32[]{:S(2)}) collective-permute-start(bf16[24,2176]{1,0:T(8,128)(2,1)S(1)} %collective-permute-done.3.message_ref.odd_ref), channel_id=1, source_target_pairs={{0,1},{1,0},{2,3},{3,2},{4,5},{5,4},{6,7},{7,6},{8,9},{9,8},{10,11... | collective-permute-start | bytes 313352 | tf_op jit(solution)/shard_map/ppermute | solution.py:696

commit v12 on v11

--- a/solution.py
+++ b/solution.py
@@ -84,8 +84,8 @@
     return edge_pair(high[:, left], high[:, right], low[:, left], low[:, right])
 
 
-def hess_tiles(d, top, rows, first_tile, count, gain, put):
-    tall = rows + 2 * PAD
+def hess_tiles(d, top, rows, first_tile, count, gain, put, pad=PAD, tall=None):
+    tall = tall or rows + 2 * pad
     lane = lax.broadcasted_iota(jnp.int32, (rows, LANES), 1)
     mid, slope, total = {}, {}, {}
     back, ahead = {}, {}
@@ -93,8 +93,8 @@
     def load(t):
         lanes = slice((first_tile + t + 1) * LANES, (first_tile + t + 2) * LANES)
         value = d[top : top + tall, lanes]
-        up, down = pltpu.roll(value, 1, 0)[PAD : PAD + rows], pltpu.roll(value, tall - 1, 0)[PAD : PAD + rows]
-        mid[t] = value[PAD : PAD + rows]
+        up, down = pltpu.roll(value, 1, 0)[pad : pad + rows], pltpu.roll(value, tall - 1, 0)[pad : pad + rows]
+        mid[t] = value[pad : pad + rows]
         slope[t], total[t] = down - up, up + down
         if t < count:
             back[t] = [pltpu.roll(v, 1, 1) for v in (mid[t], slope[t])]
@@ -247,16 +247,24 @@
     return [jnp.where(outside, 0.0, v) for v in (value, pltpu.roll(value, LANES // 2, 1))]
 
 
-def filter_columns(vh, vl, w_refs, group, cols, lev, emit, after_group, after_level):
+def plain_lhs(vh, vl):
+    def lhs(s, ats):
+        high = jnp.concatenate([vh[s, :, at : at + BLOCK] for at in ats], axis=0)
+        low = jnp.concatenate([vl[s, :, at : at + BLOCK] for at in ats], axis=0)
+        edge = jnp.concatenate([edge_columns(vh.at[s], vl.at[s], at, BLOCK) for at in ats], axis=0)
+        return high, low, edge
+
+    return lhs
+
+
+def filter_columns(lhs, w_refs, group, cols, lev, emit, after_group, after_level):
     wc_ref, wl_ref, we_ref = w_refs
-    tall = vh.shape[1]
+    tall = lev.shape[1]
     for s in ORDER:
         band = slice(s * BLOCK, (s + 1) * BLOCK)
         for g in range(0, cols // BLOCK, group):
             ats = [LANES + BLOCK * (g + i) for i in range(group)]
-            high = jnp.concatenate([vh[s, :, at : at + BLOCK] for at in ats], axis=0)
-            low = jnp.concatenate([vl[s, :, at : at + BLOCK] for at in ats], axis=0)
-            edge = jnp.concatenate([edge_columns(vh.at[s], vl.at[s], at, BLOCK) for at in ats], axis=0)
+            high, low, edge = lhs(s, ats)
             value = (
                 mm(high, wc_ref[band]) + mm(low, wc_ref[band]) + mm(high, wl_ref[band]) + mm(edge, we_ref[band])
             )
@@ -348,7 +356,7 @@
     place_rows(vh, vl, rows_of, cols, is_left)
     w_refs = band_refs(late_ref)
     seam = seam_filter(vh, vl, w_refs, cols, lev, is_left, emit)
-    filter_columns(vh, vl, w_refs, 4, cols, lev, emit, after_group, seam)
+    filter_columns(plain_lhs(vh, vl), w_refs, 4, cols, lev, emit, after_group, seam)
 
 
 def outer_kernel(last_row, one_hop, message_ref, own_ref, late_ref, rim_ref, dog_in, hess_in, dog_ref, hess_ref, *scratch):
@@ -410,12 +418,12 @@
     place_rows(vh, vl, rows_of, cols, is_left)
     w_refs = band_refs(late_ref)
     seam = seam_filter(vh, vl, w_refs, cols, lev, is_left, emit)
-    filter_columns(vh, vl, w_refs, 8, cols, lev, emit, after_group, seam)
+    filter_columns(plain_lhs(vh, vl), w_refs, 8, cols, lev, emit, after_group, seam)
 
 
 def coarse_kernel(last_row, keep_ref, other_ref, odd_ref, odd_other_ref, fine_dog_ref, fine_hess_ref, late_ref,
                   fine_dog_hbm, fine_hess_hbm, dog_hbm, hess_hbm,
-                  dog_ref, hess_ref, vh, vl, lev, d1, d2, sems):
+                  dog_ref, hess_ref, ch, cl, ce, lev, d1, d2, sems):
     fine_copies = [
         pltpu.make_async_copy(fine_dog_ref, fine_dog_hbm, sems.at[0]),
         pltpu.make_async_copy(fine_hess_ref, fine_hess_hbm, sems.at[1]),
@@ -424,26 +432,22 @@
         copy.start()
     _, rows, cols = dog_ref.shape
     row, col = mesh_place()
-    tall = rows + 2 * PAD
+    tall = lev.shape[1]
     diffs = {1: d1, 2: d2}
     is_left = col == 0
     half = cols // 2
-    zero = jnp.zeros((tall, LANES), BF16)
-    for s in range(LEVELS):
-        for ref in (vh, vl):
-            ref[s, :, :LANES] = zero
-            ref[s, :, LANES + cols :] = zero
     zero = jnp.zeros((tall, LANES), F32)
     for d in (d1, d2):
         d[:, :LANES] = zero
         d[:, LANES + cols :] = zero
 
     strip_rows = keep_ref.shape[0]
-    height = LEVELS * tall
+    height = -(-LEVELS * tall // 16) * 16
     variant = 2 * (row % 2) + col
     start = pl.multiple_of(late_ref.shape[0] - 4 * height + variant * height, 16)
     lh = late_ref[pl.ds(start, height), : 3 * strip_rows + 4 * MESSAGE]
     lp = lh[:, 3 * strip_rows :]
+    values = []
     for at in range(0, cols, BLOCK):
         source = slice(at % half, at % half + BLOCK)
         second = slice(half + at % half, half + at % half + BLOCK)
@@ -463,17 +467,38 @@
         value = mm(lh, stack)
         if at_seam:
             value = value + join(mm(lp, jnp.concatenate([*extra, *extra], axis=0)))
-        to = slice(LANES + at, LANES + at + BLOCK)
+        values.append(value[: LEVELS * tall])
+
+    none = jnp.zeros((LEVELS * tall, LANES), F32)
+    lane = lax.broadcasted_iota(jnp.int32, none.shape, 1)
+    edges = []
+    for j in range(len(values)):
+        left = values[j - 1][:, BLOCK - LANES :] if j else none
+        right = values[j + 1][:, :LANES] if j + 1 < len(values) else none
+        value = jnp.where(lane < LANES // 2, right, left)
+        eh = value.astype(BF16).astype(F32)
+        el = value - eh
+        eh = jnp.where((lane >= 16) & (lane < 64), pltpu.roll(eh, 32, 1), eh)
+        edges.append(jnp.concatenate([eh, el], axis=1))
+    for p in range(len(values) // 2):
         for s in range(LEVELS):
-            vh[s, :, to], vl[s, :, to] = split(value[s * tall : (s + 1) * tall])
+            part = slice(s * tall, (s + 1) * tall)
+            ch[s, p], cl[s, p] = split(jnp.concatenate([values[2 * p][part], values[2 * p + 1][part]], axis=0))
+            ce[s, p] = jnp.concatenate([edges[2 * p][part], edges[2 * p + 1][part]], axis=0).astype(BF16)
+
+    def lhs(s, ats):
+        pairs = range((ats[0] - LANES) // (2 * BLOCK), (ats[-1] - LANES) // (2 * BLOCK) + 1)
+        return [jnp.concatenate([ref[s, p] for p in pairs], axis=0) for ref in (ch, cl, ce)]
 
     def emit(k, at, d):
-        dog_ref[k, :, at - LANES : at - LANES + BLOCK] = (80.0 * d[PAD : PAD + rows]).astype(BF16)
+        dog_ref[k, :, at - LANES : at - LANES + BLOCK] = (80.0 * d[:rows]).astype(BF16)
         if k in diffs:
             to = slice(at, at + BLOCK)
-            diffs[k][:PAD, to] = jnp.where((row == 0) & (col == 0), 0.0, d[:PAD])
-            diffs[k][PAD : PAD + rows, to] = d[PAD : PAD + rows]
-            diffs[k][PAD + rows :, to] = jnp.where((row == last_row) & (col == 1), 0.0, d[PAD + rows :])
+            diffs[k][:rows, to] = d[:rows]
+            index = lax.broadcasted_iota(jnp.int32, (tall - rows, BLOCK), 0)
+            below = index < (tall - rows) // 2
+            out = (below & (row == last_row) & (col == 1)) | (jnp.logical_not(below) & (row == 0) & (col == 0))
+            diffs[k][rows:, to] = jnp.where(out, 0.0, d[rows:])
 
     dog_copies = [pltpu.make_async_copy(dog_ref.at[k], dog_hbm.at[k], sems.at[4 + k]) for k in range(4)]
     hess_copies = [pltpu.make_async_copy(hess_ref.at[m], hess_hbm.at[m], sems.at[2 + m]) for m in range(2)]
@@ -482,17 +507,19 @@
         def put(t, value):
             hess_ref[m, :, t * LANES : (t + 1) * LANES] = value
 
-        hess_tiles(diffs[m + 1], 0, rows, first, count, 200000.0, put)
+        hess_tiles(diffs[m + 1], 0, rows, first, count, 200000.0, put, 0, tall)
 
     def after_level(s):
+        if s in (2, 3):
+            dog_copies[s - 1].start()
         if s == 0:
-            for copy in (dog_copies[1], dog_copies[2], hess_copies[0]):
-                copy.start()
+            dog_copies[0].start()
+            hess_copies[0].start()
+            hess_copies[1].start()
         if s == 4:
-            for copy in (hess_copies[1], dog_copies[0], dog_copies[3]):
-                copy.start()
-
-    filter_columns(vh, vl, band_refs(late_ref), 8, cols, lev, emit, after_group, after_level)
+            dog_copies[3].start()
+
+    filter_columns(lhs, band_refs(late_ref), 8, cols, lev, emit, after_group, after_level)
     for copy in fine_copies + dog_copies + hess_copies:
         copy.wait()
 
@@ -539,7 +566,7 @@
 
 def coarse_constants(strip, padded):
     inputs = np.arange(padded) - REACH - 1
-    centres = np.arange(-PAD, strip + PAD)
+    centres = np.concatenate([np.arange(strip + PAD // 2), np.arange(-PAD // 2, 0)])
     valid = ((centres >= -1) & (centres <= strip)).astype(np.float32)
     variants = []
     for parity in range(2):
@@ -552,6 +579,8 @@
                 high, low = two_parts(row_matrix(s, centres, inputs) * valid[:, None])
                 more_high, more_low = two_parts(row_matrix(s, centres, message) * valid[:, None])
                 variants.append(np.concatenate([high, high, low, more_high, more_low], axis=1))
+            rest = -LEVELS * len(centres) % 16
+            variants.append(np.zeros((rest, variants[-1].shape[1]), BF16))
     return np.concatenate(variants)
 
 
@@ -582,7 +611,7 @@
     row_count = lax.axis_size("row")
     strip = rows // 4
     wide = cols + LANES
-    small = strip + 2 * PAD
+    small = strip + PAD
     lh, lt, bm, strip_rows = fine_constants(rows)
     cw = coarse_constants(strip, strip_rows)
     bands = [column_weights(s, 1) for s in SIGMAS]
@@ -704,7 +733,8 @@
         scratch_shapes=[
             pltpu.VMEM((4, strip, cols), BF16),
             pltpu.VMEM((2, strip, cols), BF16),
-            *scratch(small, small, 0),
+            *[pltpu.VMEM((LEVELS, cols // (2 * BLOCK), 2 * small, BLOCK), BF16) for _ in range(3)],
+            *scratch(small, small, 0)[2:],
             pltpu.SemaphoreType.DMA((8,)),
         ],
         compiler_params=limit(12),

time: 17.5 us -> 16.9 us (0.966)
  Pallas kernels: 8.75 us -> 8.13 us
    pallas_call x1, Pallas kernels: 2.48 us -> 1.85 us  [local(): pl.pallas_call(functools.partial(coarse_kernel, row_count - 1), out_shape...]
  transfers between devices with their start and end apart: 5 -> 5, of which waited for: 2 -> 2; matrix products, arithmetic and copies ran while one was open for 0% -> 0% of each run, Pallas kernels for 27% -> 28%
where the time goes in v12:
time: 16.9 us; the launch traced here: 16.7 us
  Pallas kernels  8.13 us (48%)
  starting transfers between devices  6.51 us (39%)
  waiting for transfers between devices  1.31 us (8%)
  between operations  0.74 us (4%)
    ppermute x2, starting transfers between devices, swap(): return lax.ppermute(value, 'row', pairs + [(j, i) for i, j in pairs])  3.31 us
    pallas_call x1, Pallas kernels, local(): pl.pallas_call(inner_kernel, out_shape=(*fine_shapes, jax.ShapeDtypeStruc...  2.3 us
    pallas_call x2, Pallas kernels, finish(): pl.pallas_call(functools.partial(outer_kernel, row_count - 1, one_hop), o...  2.24 us
    pallas_call x1, Pallas kernels, local(): pl.pallas_call(functools.partial(coarse_kernel, row_count - 1), out_shape...  1.85 us
    ppermute x1, starting transfers between devices, local(): odd_other = lax.ppermute(odd, 'col', [(0, 1), (1, 0)])  1.49 us
    ppermute x2, waiting for transfers between devices, swap(): return lax.ppermute(value, 'row', pairs + [(j, i) for i, j in pairs])  1.19 us
    ppermute x1, starting transfers between devices, local(): other = lax.ppermute(send, 'col', [(0, 1), (1, 0)])  0.97 us
    pallas_call x1, Pallas kernels, local(): pl.pallas_call(border_kernel, out_shape=jax.ShapeDtypeStruct((rows, LANES...  0.85 us
  transfers between devices with their start and end apart: 5, of which 2 were waited for; matrix products, arithmetic and copies ran while one was open for 0% of the time, Pallas kernels for 28%

profile of v12, /device:TPU:11, one launch (start us, length us, event | category | flops | bytes accessed | tf_op | source)
XLA Modules:
  0.0 16.7 jit_solution(10619734034694375725)
XLA Ops:
  0.6 0.0 copy-start.2
  0.6 0.0 copy-start.1
  0.7 0.9 %border.1 = f32[64,128]{1,0:T(8,128)S(1)} custom-call(f32[64,2048]{1,0:T(8,128)} %x_hbm.1), custom_call_target="tpu_custom_call" | custom-call | flops 2000000000 | bytes 10000000 | tf_op jit(solution)/shard_map/border/pallas_call | solution.py:625
  1.5 0.0 copy-start
  1.5 0.7 %collective-permute-start = (f32[64,128]{1,0:T(8,128)S(1)}, f32[64,128]{1,0:T(8,128)S(1)}, u32[]{:S(2)}, u32[]{:S(2)}) collective-permute-start(f32[64,128]{1,0:T(8,128)S(1)} %border.1), channel_id=1, source_target_pairs={{0,1},{1,0},{2,3},{3,2},{4,5},{5,4},{6,7},{7,6},{8,9},{9,8},{10,11... | collective-permute-start | bytes 98312 | tf_op jit(solution)/shard_map/ppermute | solution.py:635
  2.3 0.0 copy-done.2
  2.3 0.0 copy-done.1
  2.3 0.7 %send.1 = (bf16[128,2176]{1,0:T(8,128)(2,1)S(1)}, bf16[24,2176]{1,0:T(8,128)(2,1)S(1)}, bf16[24,2176]{1,0:T(8,128)(2,1)S(1)}, f32[64,1152]{1,0:T(8,128)S(1)}) custom-call(f32[64,2048]{1,0:T(8,128)S(1)} %copy-done.1, bf16[832,256]{1,0:T(8,128)(2,1)S(1)} %copy-done.2), custom_call_target="tpu_custom_call" | custom-call | flops 1000000000 | bytes 1000000 | tf_op jit(solution)/shard_map/send/pallas_call | solution.py:636
  3.0 0.1 collective-permute-done.side_ref
  3.2 1.3 %collective-permute-start.1 = (bf16[24,2176]{1,0:T(8,128)(2,1)S(1)}, bf16[24,2176]{1,0:T(8,128)(2,1)S(1)}, u32[]{:S(2)}, u32[]{:S(2)}) collective-permute-start(bf16[24,2176]{1,0:T(8,128)(2,1)S(1)} %get-tuple-element.24), channel_id=1, source_target_pairs={{0,2},{4,6},{8,10},{12,14},{2,0},{6,4},{10,8},{14,12},{1,3},{5,7},... | collective-permute-start | bytes 313352 | tf_op jit(solution)/shard_map/ppermute | solution.py:661
  4.5 2.0 %collective-permute-start.3 = (bf16[24,2176]{1,0:T(8,128)(2,1)S(1)}, bf16[24,2176]{1,0:T(8,128)(2,1)S(1)}, u32[]{:S(2)}, u32[]{:S(2)}) collective-permute-start(bf16[24,2176]{1,0:T(8,128)(2,1)S(1)} %get-tuple-element.29), channel_id=1, source_target_pairs={{2,4},{6,8},{10,12},{4,2},{8,6},{12,10},{3,5},{7,9},{11,13},{5,3},... | collective-permute-start | bytes 313352 | tf_op jit(solution)/shard_map/ppermute | solution.py:661
  6.5 0.0 copy-done
  6.5 2.3 %inner.1 = (bf16[4,64,2048]{2,1,0:T(8,128)(2,1)S(1)}, bf16[2,64,2048]{2,1,0:T(8,128)(2,1)S(1)}, f32[4,48,2304]{2,1,0:T(8,128)S(1)}) custom-call(bf16[128,2176]{1,0:T(8,128)(2,1)S(1)} %get-tuple-element.25.own_ref, bf16[4992,256]{1,0:T(8,128)(2,1)S(1)} %copy-done), custom_call_target="tpu_custom_call" | custom-call | flops 2000000000 | bytes 10000000 | tf_op jit(solution)/shard_map/inner/pallas_call | solution.py:686
  8.8 0.0 collective-permute-done.1.even_ref.message_ref
  8.8 0.1 base.1
  8.9 1.0 %collective-permute-start.2 = (f32[48,1152]{1,0:T(8,128)S(1)}, f32[48,1152]{1,0:T(8,128)S(1)}, u32[]{:S(2)}, u32[]{:S(2)}) collective-permute-start(f32[48,1152]{1,0:T(8,128)S(1)} %get-tuple-element.28), channel_id=1, source_target_pairs={{0,1},{1,0},{2,3},{3,2},{4,5},{5,4},{6,7},{7,6},{8,9},{9,8},{10,11... | collective-permute-start | bytes 663560 | tf_op jit(solution)/shard_map/ppermute | solution.py:724
  9.9 1.2 %collective-permute-done.3.message_ref.odd_ref = bf16[24,2176]{1,0:T(8,128)(2,1)S(1)} collective-permute-done((bf16[24,2176]{1,0:T(8,128)(2,1)S(1)}, bf16[24,2176]{1,0:T(8,128)(2,1)S(1)}, u32[]{:S(2)}, u32[]{:S(2)}) %collective-permute-start.3) | collective-permute-done | bytes 104480 | tf_op jit(solution)/shard_map/ppermute | solution.py:661
  11.1 1.5 %collective-permute-start.4 = (bf16[24,2176]{1,0:T(8,128)(2,1)S(1)}, bf16[24,2176]{1,0:T(8,128)(2,1)S(1)}, u32[]{:S(2)}, u32[]{:S(2)}) collective-permute-start(bf16[24,2176]{1,0:T(8,128)(2,1)S(1)} %collective-permute-done.3.message_ref.odd_ref), channel_id=1, source_target_pairs={{0,1},{1,0},{2,3},{3,2},{4,5},{5,4},{6,7},{7,6},{8,9},{9,8},{10,11... | collective-permute-start | bytes 313352 | tf_op jit(solution)/shard_map/ppermute | solution.py:725
  12.6 1.1 %outer.2 = (bf16[4,64,2048]{2,1,0:T(8,128)(2,1)S(1)}, bf16[2,64,2048]{2,1,0:T(8,128)(2,1)S(1)}) custom-call(bf16[24,2176]{1,0:T(8,128)(2,1)S(1)} %collective-permute-done.1.even_ref.message_ref, bf16[128,2176]{1,0:T(8,128)(2,1)S(1)} %get-tuple-element.25.own_ref, bf16[4992,256]{1,0:T(8,128)(2,1)S(1)} %copy-done, ...), custom_call_target="tpu_custom_call", output_to_operand_aliasing={{0}: (4, {}), {1}: (5, {})} | custom-call | flops 1000000000 | bytes 1000000 | tf_op jit(solution)/shard_map/outer/pallas_call | solution.py:698
  13.7 1.1 %outer.3 = (bf16[4,64,2048]{2,1,0:T(8,128)(2,1)S(1)}, bf16[2,64,2048]{2,1,0:T(8,128)(2,1)S(1)}) custom-call(bf16[24,2176]{1,0:T(8,128)(2,1)S(1)} %collective-permute-done.3.message_ref.odd_ref, bf16[128,2176]{1,0:T(8,128)(2,1)S(1)} %get-tuple-element.25.own_ref, bf16[4992,256]{1,0:T(8,128)(2,1)S(1)} %copy-done, ...), custom_call_target="tpu_custom_call", output_to_operand_aliasing={{0}: (4, {}), {1}: (5, {})} | custom-call | flops 1000000000 | bytes 1000000 | tf_op jit(solution)/shard_map/outer/pallas_call | solution.py:698
  14.8 0.0 collective-permute-done.4.odd_other_ref
  14.8 0.0 collective-permute-done.2.other_ref
  14.9 1.9 %coarse.1 = (bf16[4,64,2048]{2,1,0:T(8,128)(2,1)}, bf16[2,64,2048]{2,1,0:T(8,128)(2,1)}, bf16[4,16,2048]{2,1,0:T(8,128)(2,1)}, bf16[2,16,2048]{2,1,0:T(8,128)(2,1)}) custom-call(f32[48,1152]{1,0:T(8,128)S(1)} %get-tuple-element.27.keep_ref, f32[48,1152]{1,0:T(8,128)S(1)} %collective-permute-done.2.other_ref, ...), custom_call_target="tpu_custom_call" | custom-call | tf_op jit(solution)/shard_map/coarse/pallas_call | solution.py:728
  (1 shorter events, 0.0 us)
Async XLA Ops:
  0.6 1.6 %copy-start.2 = (bf16[832,256]{1,0:T(8,128)(2,1)S(1)}, bf16[832,256]{1,0:T(8,128)(2,1)}, u32[]{:S(2)}) copy-start(bf16[832,256]{1,0:T(8,128)(2,1)} %constant.4.clone.early_ref) | copy-start | bytes 1277956
  0.6 1.6 %copy-start.1 = (f32[64,2048]{1,0:T(8,128)S(1)}, f32[64,2048]{1,0:T(8,128)}, u32[]{:S(2)}) copy-start(f32[64,2048]{1,0:T(8,128)} %x_hbm.1) | copy-start | bytes 1572868
  1.5 5.0 %copy-start = (bf16[4992,256]{1,0:T(8,128)(2,1)S(1)}, bf16[4992,256]{1,0:T(8,128)(2,1)}, u32[]{:S(2)}) copy-start(bf16[4992,256]{1,0:T(8,128)(2,1)} %constant.5.clone.late_ref) | copy-start | bytes 7667716
  1.5 1.6 %collective-permute-start = (f32[64,128]{1,0:T(8,128)S(1)}, f32[64,128]{1,0:T(8,128)S(1)}, u32[]{:S(2)}, u32[]{:S(2)}) collective-permute-start(f32[64,128]{1,0:T(8,128)S(1)} %border.1), channel_id=1, source_target_pairs={{0,1},{1,0},{2,3},{3,2},{4,5},{5,4},{6,7},{7,6},{8,9},{9,8},{10,11... | collective-permute-start | bytes 98312 | tf_op jit(solution)/shard_map/ppermute | solution.py:635
  3.2 5.6 %collective-permute-start.1 = (bf16[24,2176]{1,0:T(8,128)(2,1)S(1)}, bf16[24,2176]{1,0:T(8,128)(2,1)S(1)}, u32[]{:S(2)}, u32[]{:S(2)}) collective-permute-start(bf16[24,2176]{1,0:T(8,128)(2,1)S(1)} %get-tuple-element.24), channel_id=1, source_target_pairs={{0,2},{4,6},{8,10},{12,14},{2,0},{6,4},{10,8},{14,12},{1,3},{5,7},... | collective-permute-start | bytes 313352 | tf_op jit(solution)/shard_map/ppermute | solution.py:661
  4.5 6.6 %collective-permute-start.3 = (bf16[24,2176]{1,0:T(8,128)(2,1)S(1)}, bf16[24,2176]{1,0:T(8,128)(2,1)S(1)}, u32[]{:S(2)}, u32[]{:S(2)}) collective-permute-start(bf16[24,2176]{1,0:T(8,128)(2,1)S(1)} %get-tuple-element.29), channel_id=1, source_target_pairs={{2,4},{6,8},{10,12},{4,2},{8,6},{12,10},{3,5},{7,9},{11,13},{5,3},... | collective-permute-start | bytes 313352 | tf_op jit(solution)/shard_map/ppermute | solution.py:661
  8.9 5.9 %collective-permute-start.2 = (f32[48,1152]{1,0:T(8,128)S(1)}, f32[48,1152]{1,0:T(8,128)S(1)}, u32[]{:S(2)}, u32[]{:S(2)}) collective-permute-start(f32[48,1152]{1,0:T(8,128)S(1)} %get-tuple-element.28), channel_id=1, source_target_pairs={{0,1},{1,0},{2,3},{3,2},{4,5},{5,4},{6,7},{7,6},{8,9},{9,8},{10,11... | collective-permute-start | bytes 663560 | tf_op jit(solution)/shard_map/ppermute | solution.py:724
  11.1 3.7 %collective-permute-start.4 = (bf16[24,2176]{1,0:T(8,128)(2,1)S(1)}, bf16[24,2176]{1,0:T(8,128)(2,1)S(1)}, u32[]{:S(2)}, u32[]{:S(2)}) collective-permute-start(bf16[24,2176]{1,0:T(8,128)(2,1)S(1)} %collective-permute-done.3.message_ref.odd_ref), channel_id=1, source_target_pairs={{0,1},{1,0},{2,3},{3,2},{4,5},{5,4},{6,7},{7,6},{8,9},{9,8},{10,11... | collective-permute-start | bytes 313352 | tf_op jit(solution)/shard_map/ppermute | solution.py:725
